TPU v7x, 32 devices: a whole 2x2x4 slice. The times are simulated.
32 devices in a mesh: beads: 2 (over y), atoms: 4 (over z), kvec: 4 (over x, core).
Axes of the slice: x: 2, y: 2, z: 4, core: 2. Of those that a mesh axis runs over, the one named last changes fastest.
Arguments:
- lattice: int32 [3, 1024], P(None, ('atoms', 'kvec')), may hold values from -20 to 20, as said below
- positions: float32 [3, 8192], P(None, ('beads', 'atoms', 'kvec')), parts along dimension 1, may hold values from 0 to 1
- cotangent: bfloat16 [8192, 128], P(('beads', 'atoms', 'kvec')), parts along dimension 0, may hold values from -6 to 6
- filters: float32 [1024, 128], P(('atoms', 'kvec')), may hold values from 0.1 to 2
- saved_factor: float32 [2, 2048, 128], P(None, ('beads', 'atoms', 'kvec')), parts along dimension 1, may hold values from -6 to 6
Outputs:
- node_grad: bfloat16 [8192, 128], P(('beads', 'atoms', 'kvec')), parts along dimension 0
- filter_grad: float32 [2048, 128], P(('beads', 'atoms', 'kvec')), parts along dimension 0
There are 2 independent parts, one for each index of `beads`. A program takes and returns all parts, laid end to end along the dimension named above; an argument that names none is the same for every part. Nothing has to cross between parts.
Inputs may be any that keep to these rules, and one draw needn't show every extreme that they name: `lattice`: the columns are 1024 distinct integer vectors of length at most 20, all in one half-space (no vector appears together with its negative), in random order.
All inputs are finite; a program needn't handle non-finite values.
Results may differ from a plain program's by a relative error of at most 0.0056.
Values may be sent and summed in bfloat16 or wider, within the bound.
No kernel may reach another device: no remote copies, remote signals or barrier semaphores. Data moves between devices by JAX's collectives and lax.ppermute only.
A program may use at most 64 MiB of HBM per device.

v0:
```python
import math

import jax
import jax.numpy as jnp
from jax import lax
from jax.experimental import pallas as pl
from jax.experimental.pallas import tpu as pltpu
from jax.sharding import PartitionSpec as P


f32 = jnp.float32
bf16 = jnp.bfloat16


SIN_COEF = None
COS_COEF = None


def _fit():
    import numpy as np

    n = 4001
    t = np.cos(np.pi * (np.arange(n) + 0.5) / n)
    u = (t + 1.0) * 0.125
    r = np.sqrt(u)
    root = math.sqrt(2.0)
    sin_ratio = np.where(r > 1e-9, root * np.sin(np.pi * r) / np.maximum(r, 1e-9), root * np.pi)
    cheb = np.polynomial.chebyshev.Chebyshev
    s = cheb.fit(u, sin_ratio, 4, domain=[0.0, 0.25]).convert(kind=np.polynomial.Polynomial)
    c = cheb.fit(u, root * np.cos(np.pi * r), 4, domain=[0.0, 0.25]).convert(kind=np.polynomial.Polynomial)
    return tuple(float(v) for v in s.coef), tuple(float(v) for v in c.coef)


SIN_COEF, COS_COEF = _fit()


def _horner(coef, u):
    acc = jnp.full_like(u, coef[-1])
    for value in coef[-2::-1]:
        acc = acc * u + value
    return acc


def cos_sin(phase):
    r = phase - jnp.round(phase)
    u = r * r
    s = r * _horner(SIN_COEF, u)
    c = _horner(COS_COEF, u)
    return 1.0 - s * s, s * c


def full_spec(count):
    return [pl.BlockSpec(memory_space=pltpu.VMEM)] * count


VMEM_BUDGET = 4 * 1024 * 1024


def call(body, outs, *args, keep_args=True, keep_outs=True):
    if keep_args:
        args = [pltpu.with_memory_space_constraint(arg, pltpu.VMEM) for arg in args]
    if keep_outs:
        outs = [pltpu.VMEM(v.shape, v.dtype) for v in outs]
    return pl.pallas_call(
        body,
        out_shape=outs,
        in_specs=full_spec(len(args)),
        out_specs=full_spec(len(outs)),
    )(*args)


def pack_body(lat_ref, pos_ref, cot_ref, out_ref, wide_ref):
    natom, width = cot_ref.shape
    nk = lat_ref.shape[1]
    out_ref[0:natom, :] = cot_ref[...]
    x = pos_ref[...]
    hi = x.astype(bf16).astype(f32)
    rest = x - hi
    mid = rest.astype(bf16).astype(f32)
    low = rest - mid
    zero = jnp.zeros_like(x)
    parts = jnp.concatenate([hi, mid, low, zero, zero, zero[:1]], 0).astype(bf16)
    for j in range(natom // width):
        out_ref[natom + 16 * j : natom + 16 * (j + 1), :] = parts[:, j * width : (j + 1) * width]
    row = lax.broadcasted_iota(jnp.int32, (nk, width), 0)
    col = lax.broadcasted_iota(jnp.int32, (nk, width), 1)
    spread = (row == col % nk).astype(bf16)
    lat = lat_ref[...].astype(f32).astype(bf16)
    wide = jnp.dot(lat, spread, preferred_element_type=f32)
    wide_ref[...] = jnp.concatenate([wide, wide, wide[:2]], 0)


def join_body(own_ref, got_ref, out_ref):
    out_ref[0:8, :] = own_ref[...]
    out_ref[8:16, :] = got_ref[...]


def table_body(nk, lat_ref, out_ref):
    width = lat_ref.shape[1]
    zero = jnp.zeros((3, width), f32)
    for h in range(2):
        lat = lat_ref[8 * h : 8 * h + 3, :]
        cols = jnp.concatenate([lat, lat, lat, zero, zero, zero[:1]], 0).T
        out_ref[h * nk : (h + 1) * nk, :] = cols[0:nk].astype(bf16)


def factor_body(natom, nk, blocks, first, last, *refs):
    zb = refs[0]
    refs = refs[1:]
    count = len(blocks)
    tables, refs = refs[:count], refs[count:]
    before, refs = ((), refs) if first else (refs[:count], refs[count:])
    tiles, outs = refs[:count], refs[count:]
    width = zb.shape[1]
    parts = jnp.concatenate([zb[natom + 16 * j : natom + 16 * (j + 1), :] for j in range(natom // width)], 1)
    phases = [
        jnp.dot(table[h * nk : (h + 1) * nk, :], parts, preferred_element_type=f32)
        for table, h in zip(tables, (t % 2 for t in blocks))
    ]
    cot = zb[0:natom, :]
    step = 32
    for b in range(count):
        for i in range(0, nk, step):
            for k, value in enumerate(cos_sin(phases[b][i : i + step])):
                rows = pl.ds(k * nk + i, step)
                value = value.astype(bf16)
                tiles[b][rows, :] = value
                total = jnp.dot(value, cot, preferred_element_type=f32)
                if not first:
                    total = total + before[b][rows, :]
                if last:
                    rows = pl.ds(2 * nk * b + k * nk + i, step)
                    outs[0][rows, :] = total.astype(outs[0].dtype)
                else:
                    outs[b][rows, :] = total


def shuffled(ref, flip, half, nk):
    rows = [ref[2 * nk * (t ^ flip) : 2 * nk * ((t ^ flip) + 1), :] for t in range(half)]
    return jnp.concatenate(rows, 0).astype(f32)


def pair_body(own_ref, got_ref, f_ref, fb_ref):
    total = own_ref[...] + got_ref[...].astype(f32)
    f_ref[...] = total
    fb_ref[...] = total.astype(bf16)


def weight_body(half, nk, flips, scale, *refs):
    total = refs[0][...]
    for ref, flip in zip(refs[1:], flips):
        total = total + shuffled(ref, flip // 2, half, nk)
    total = total * scale
    fb = refs[1 + len(flips) : 1 + len(flips) + half]
    weight_ref, head_ref = refs[1 + len(flips) + half :]
    for t in range(half):
        fil = fb[t][...]
        rows = total[2 * nk * t : 2 * nk * (t + 1)] * jnp.concatenate([fil, fil], 0)
        weight_ref[:, 2 * nk * t : 2 * nk * (t + 1)] = rows.T.astype(bf16)
    head_ref[...] = total[0 : 2 * nk]


def part_of(weight_ref, tiles):
    tile = jnp.concatenate([ref[...] for ref in tiles], 0)
    return jnp.dot(weight_ref[...], tile, preferred_element_type=f32)


def mine_body(nz, half, weight_ref, *refs):
    for z in range(nz):
        refs[nz * half + z][...] = part_of(weight_ref, refs[z * half : (z + 1) * half])


def node_body(half, part_ref, weight_ref, *refs):
    total = part_ref[...] + part_of(weight_ref, refs[:half])
    refs[half][...] = total.T.astype(refs[half].dtype)


def own_body(half, head_ref, saved_ref, part_ref, weight_ref, *refs):
    node_body(half, part_ref, weight_ref, *refs)
    grad_ref = refs[half + 1]
    nk = grad_ref.shape[0]
    grad_ref[...] = head_ref[0:nk] * saved_ref[0] + head_ref[nk : 2 * nk] * saved_ref[1]


def final_body(scale, *refs):
    total = refs[0][...]
    for ref in refs[1:-1]:
        total = total + ref[...].astype(f32)
    refs[-1][...] = (total * scale).astype(bf16)


def shape(dims, kind):
    return jax.ShapeDtypeStruct(dims, kind)


def local(lattice, positions, cotangent, filters, saved_factor):
    nz = lax.axis_size("atoms")
    nq = lax.axis_size("kvec")
    natom, width = cotangent.shape
    nk = lattice.shape[1]
    half = nq // 2
    count = half * nk
    scale_n = 1.0 / math.sqrt(natom * nz * nq)
    scale_k = 1.0 / math.sqrt(nk * nz * nq)
    keep = nz * natom * 4 * count * 2 <= VMEM_BUDGET

    def swap(value, axis, size, flip):
        return lax.ppermute(value, axis, [(i, i ^ flip) for i in range(size)])

    def run(body, outs, *args, keep_args=keep, keep_outs=keep):
        return call(body, outs, *args, keep_args=keep_args, keep_outs=keep_outs)

    zbuf, wide = run(
        pack_body,
        [shape((natom + 16 * (natom // width), width), bf16), shape((8, width), f32)],
        lattice,
        positions,
        cotangent,
        keep_args=False,
    )
    far = list(range(nz - 1, 0, -1))
    flips = list(range(2, nq, 2))
    zb = {0: zbuf}
    for s in far:
        zb[s] = swap(zbuf, "atoms", nz, s)
    (cores,) = run(join_body, [shape((16, width), f32)], wide, swap(wide, "kvec", nq, 1))
    lats = [cores] + [swap(cores, "kvec", nq, s) for s in flips]
    fils = [filters] + [swap(filters, "kvec", nq, s) for s in flips]
    table = {}
    for s, lat in zip([0] + flips, lats):
        (both,) = run(lambda *refs: table_body(nk, *refs), [shape((2 * nk, 16), bf16)], lat)
        table[s] = table[s + 1] = both
    mine = list(range(0, nq, 2))
    theirs = list(range(1, nq, 2))
    tiles = {}
    total = {}

    def factor(s, blocks, first=False, last=None):
        outs = [shape((2 * nk, natom), bf16)] * len(blocks)
        sums = [shape((2 * nk, width), f32)] * len(blocks)
        if last is not None:
            sums = [shape((2 * nk * len(blocks), width), last)]
        args = [zb[s]] + [table[t] for t in blocks] + ([] if first else [total[t] for t in blocks])
        body = lambda *refs: factor_body(natom, nk, blocks, first, last is not None, *refs)
        got = run(body, outs + sums, *args)
        for t, tile in zip(blocks, got):
            tiles[s, t] = tile
        if last is not None:
            return got[-1]
        for t, value in zip(blocks, got[len(blocks) :]):
            total[t] = value
        return None

    order = [0] + far
    for s in order[:-1]:
        for t in range(0, nq, 2):
            factor(s, [t, t + 1], first=s == order[0])
    sent = factor(order[-1], theirs, last=bf16)
    kept = factor(order[-1], mine, last=f32)
    pair, pair16 = run(
        pair_body,
        [shape((2 * count, width), f32), shape((2 * count, width), bf16)],
        kept,
        swap(sent, "kvec", nq, 1),
    )
    got = [swap(pair16, "kvec", nq, s) for s in flips]
    weight, head = run(
        lambda *refs: weight_body(half, nk, flips, scale_n, *refs),
        [shape((width, 2 * count), bf16), shape((2 * nk, width), f32)],
        pair,
        *got,
        *fils,
    )
    other = swap(weight, "kvec", nq, 1)
    parts = run(
        lambda *refs: mine_body(nz, half, *refs),
        [shape((width, natom), f32)] * nz,
        weight,
        *[tiles[s, t] for s in order for t in mine],
    )
    landed = []
    for s, part in zip(order[1:], parts[1:]):
        (node,) = run(
            lambda *refs: node_body(half, *refs),
            [shape((natom, width), bf16)],
            part,
            other,
            *[tiles[s, t] for t in theirs],
        )
        landed.append(swap(node, "atoms", nz, s))
    own, filter_grad = run(
        lambda *refs: own_body(half, *refs),
        [shape((natom, width), f32), shape((nk, width), f32)],
        head,
        saved_factor,
        parts[0],
        other,
        *[tiles[0, t] for t in theirs],
    )
    (node_grad,) = run(
        lambda *refs: final_body(scale_k, *refs),
        [shape((natom, width), bf16)],
        own,
        *landed,
        keep_outs=False,
    )
    return (node_grad, filter_grad)


def solution(mesh):
    in_specs = (
        P(None, ("atoms", "kvec")),
        P(None, ("beads", "atoms", "kvec")),
        P(("beads", "atoms", "kvec"), None),
        P(("atoms", "kvec"), None),
        P(None, ("beads", "atoms", "kvec"), None),
    )
    out_specs = (P(("beads", "atoms", "kvec"), None), P(("beads", "atoms", "kvec"), None))
    return jax.shard_map(local, mesh=mesh, in_specs=in_specs, out_specs=out_specs, check_vma=False)
```

profile of v0, /device:TPU:0, one launch (start us, length us, event | category | flops | bytes accessed | tf_op | source)
XLA Modules:
  0.0 33.7 jit_solution(15352865421336134602)
XLA Ops:
  0.6 1.0 %shard_map.68 = (bf16[288,128]{1,0:T(8,128)(2,1)S(1)}, f32[8,128]{1,0:T(8,128)S(1)}) custom-call(s32[3,64]{1,0:T(4,128)} %lat_ref.1, f32[3,256]{1,0:T(4,128)} %pos_ref.1, bf16[256,128]{1,0:T(8,128)(2,1)} %cot_ref.1), custom_call_target="tpu_custom_call" | custom-call | tf_op jit(solution)/shard_map/pallas_call | solution.py:64
  1.6 5.1 %collective-permute-start.4 = (bf16[288,128]{1,0:T(8,128)(2,1)S(1)}, bf16[288,128]{1,0:T(8,128)(2,1)S(1)}, u32[]{:S(2)}, u32[]{:S(2)}) collective-permute-start(bf16[288,128]{1,0:T(8,128)(2,1)S(1)} %get-tuple-element.44.refs_0_), channel_id=1, source_target_pairs={{0,12},{4,8},{8,4},{12,0},{1,13},{5,9},{9,5},{13,1},{2,14},{6,10},... | collective-permute-start | bytes 221192 | tf_op jit(solution)/shard_map/ppermute | solution.py:208
  6.7 0.6 %collective-permute-start = (bf16[288,128]{1,0:T(8,128)(2,1)S(1)}, bf16[288,128]{1,0:T(8,128)(2,1)S(1)}, u32[]{:S(2)}, u32[]{:S(2)}) collective-permute-start(bf16[288,128]{1,0:T(8,128)(2,1)S(1)} %get-tuple-element.44.refs_0_), channel_id=1, source_target_pairs={{0,4},{4,0},{8,12},{12,8},{1,5},{5,1},{9,13},{13,9},{2,6},{6,2},{1... | collective-permute-start | bytes 221192 | tf_op jit(solution)/shard_map/ppermute | solution.py:208
  7.3 1.2 %collective-permute-done.1.got_ref = f32[8,128]{1,0:T(8,128)S(1)} collective-permute-done((f32[8,128]{1,0:T(8,128)S(1)}, f32[8,128]{1,0:T(8,128)S(1)}, u32[]{:S(2)}, u32[]{:S(2)}) %collective-permute-start.1) | collective-permute-done | bytes 4128 | tf_op jit(solution)/shard_map/ppermute | solution.py:208
  8.5 1.7 %collective-permute-start.2 = (f32[16,128]{1,0:T(8,128)S(1)}, f32[16,128]{1,0:T(8,128)S(1)}, u32[]{:S(2)}, u32[]{:S(2)}) collective-permute-start(f32[16,128]{1,0:T(8,128)S(1)} %shard_map.69.refs_0_), channel_id=1, source_target_pairs={{0,2},{1,3},{2,0},{3,1},{4,6},{5,7},{6,4},{7,5},{8,10},{9,11},{10,... | collective-permute-start | bytes 24584 | tf_op jit(solution)/shard_map/ppermute | solution.py:208
  10.2 0.4 %shard_map.72 = (bf16[128,256]{1,0:T(8,128)(2,1)S(1)}, bf16[128,256]{1,0:T(8,128)(2,1)S(1)}, f32[128,128]{1,0:T(8,128)S(1)}, f32[128,128]{1,0:T(8,128)S(1)}) custom-call(bf16[288,128]{1,0:T(8,128)(2,1)S(1)} %get-tuple-element.44.refs_0_, bf16[128,16]{1,0:T(8,128)(2,1)S(1)} %shard_map.70.refs_1_.refs_2_, bf16[128,16]{1,0:T(8,128)(2,1)S(1)} %shard_map.70.refs_1_.refs_2_), custom_call_target="tpu_custom_call" | custom-call | tf_op jit(solution)/shard_map/pallas_call | solution.py:64
  10.6 1.5 %collective-permute-done.2.refs_0_ = f32[16,128]{1,0:T(8,128)S(1)} collective-permute-done((f32[16,128]{1,0:T(8,128)S(1)}, f32[16,128]{1,0:T(8,128)S(1)}, u32[]{:S(2)}, u32[]{:S(2)}) %collective-permute-start.2) | collective-permute-done | bytes 8224 | tf_op jit(solution)/shard_map/ppermute | solution.py:208
  12.2 0.4 %shard_map.75 = (bf16[128,256]{1,0:T(8,128)(2,1)S(1)}, bf16[128,256]{1,0:T(8,128)(2,1)S(1)}, f32[128,128]{1,0:T(8,128)S(1)}, f32[128,128]{1,0:T(8,128)S(1)}) custom-call(bf16[288,128]{1,0:T(8,128)(2,1)S(1)} %get-tuple-element.44.refs_0_, bf16[128,16]{1,0:T(8,128)(2,1)S(1)} %shard_map.71.refs_1_.refs_2_, bf16[128,16]{1,0:T(8,128)(2,1)S(1)} %shard_map.71.refs_1_.refs_2_), custom_call_target="tpu_custom_call" | custom-call | tf_op jit(solution)/shard_map/pallas_call | solution.py:64
  12.6 0.4 %shard_map.73 = (bf16[128,256]{1,0:T(8,128)(2,1)S(1)}, bf16[128,256]{1,0:T(8,128)(2,1)S(1)}, f32[128,128]{1,0:T(8,128)S(1)}, f32[128,128]{1,0:T(8,128)S(1)}) custom-call(bf16[288,128]{1,0:T(8,128)(2,1)S(1)} %collective-permute-done.4.refs_0_, bf16[128,16]{1,0:T(8,128)(2,1)S(1)} %shard_map.70.refs_1_.refs_2_, bf16[128,16]{1,0:T(8,128)(2,1)S(1)} %shard_map.70.refs_1_.refs_2_, ...), custom_call_target="tpu_custom_call" | custom-call | tf_op jit(solution)/shard_map/pallas_call | solution.py:64
  13.0 0.4 %shard_map.76 = (bf16[128,256]{1,0:T(8,128)(2,1)S(1)}, bf16[128,256]{1,0:T(8,128)(2,1)S(1)}, f32[128,128]{1,0:T(8,128)S(1)}, f32[128,128]{1,0:T(8,128)S(1)}) custom-call(bf16[288,128]{1,0:T(8,128)(2,1)S(1)} %collective-permute-done.4.refs_0_, bf16[128,16]{1,0:T(8,128)(2,1)S(1)} %shard_map.71.refs_1_.refs_2_, bf16[128,16]{1,0:T(8,128)(2,1)S(1)} %shard_map.71.refs_1_.refs_2_, ...), custom_call_target="tpu_custom_call" | custom-call | tf_op jit(solution)/shard_map/pallas_call | solution.py:64
  13.3 0.4 %shard_map.74 = (bf16[128,256]{1,0:T(8,128)(2,1)S(1)}, bf16[128,256]{1,0:T(8,128)(2,1)S(1)}, f32[128,128]{1,0:T(8,128)S(1)}, f32[128,128]{1,0:T(8,128)S(1)}) custom-call(bf16[288,128]{1,0:T(8,128)(2,1)S(1)} %collective-permute-done.3.refs_0_, bf16[128,16]{1,0:T(8,128)(2,1)S(1)} %shard_map.70.refs_1_.refs_2_, bf16[128,16]{1,0:T(8,128)(2,1)S(1)} %shard_map.70.refs_1_.refs_2_, ...), custom_call_target="tpu_custom_call" | custom-call | tf_op jit(solution)/shard_map/pallas_call | solution.py:64
  13.7 0.4 %shard_map.77 = (bf16[128,256]{1,0:T(8,128)(2,1)S(1)}, bf16[128,256]{1,0:T(8,128)(2,1)S(1)}, f32[128,128]{1,0:T(8,128)S(1)}, f32[128,128]{1,0:T(8,128)S(1)}) custom-call(bf16[288,128]{1,0:T(8,128)(2,1)S(1)} %collective-permute-done.3.refs_0_, bf16[128,16]{1,0:T(8,128)(2,1)S(1)} %shard_map.71.refs_1_.refs_2_, bf16[128,16]{1,0:T(8,128)(2,1)S(1)} %shard_map.71.refs_1_.refs_2_, ...), custom_call_target="tpu_custom_call" | custom-call | tf_op jit(solution)/shard_map/pallas_call | solution.py:64
  14.1 0.4 %shard_map.79 = (bf16[128,256]{1,0:T(8,128)(2,1)S(1)}, bf16[128,256]{1,0:T(8,128)(2,1)S(1)}, bf16[256,128]{1,0:T(8,128)(2,1)S(1)}) custom-call(bf16[288,128]{1,0:T(8,128)(2,1)S(1)} %collective-permute-done.refs_0_, bf16[128,16]{1,0:T(8,128)(2,1)S(1)} %shard_map.70.refs_1_.refs_2_, bf16[128,16]{1,0:T(8,128)(2,1)S(1)} %shard_map.71.refs_1_.refs_2_, ...), custom_call_target="tpu_custom_call" | custom-call | tf_op jit(solution)/shard_map/pallas_call | solution.py:64
  14.5 0.4 %shard_map.78 = (bf16[128,256]{1,0:T(8,128)(2,1)S(1)}, bf16[128,256]{1,0:T(8,128)(2,1)S(1)}, f32[256,128]{1,0:T(8,128)S(1)}) custom-call(bf16[288,128]{1,0:T(8,128)(2,1)S(1)} %collective-permute-done.refs_0_, bf16[128,16]{1,0:T(8,128)(2,1)S(1)} %shard_map.70.refs_1_.refs_2_, bf16[128,16]{1,0:T(8,128)(2,1)S(1)} %shard_map.71.refs_1_.refs_2_, ...), custom_call_target="tpu_custom_call" | custom-call | tf_op jit(solution)/shard_map/pallas_call | solution.py:64
  14.9 0.9 %collective-permute-done.5.got_ref = bf16[256,128]{1,0:T(8,128)(2,1)S(1)} collective-permute-done((bf16[256,128]{1,0:T(8,128)(2,1)S(1)}, bf16[256,128]{1,0:T(8,128)(2,1)S(1)}, u32[]{:S(2)}, u32[]{:S(2)}) %collective-permute-start.5) | collective-permute-done | bytes 65568 | tf_op jit(solution)/shard_map/ppermute | solution.py:208
  15.8 1.7 %collective-permute-start.6 = (bf16[256,128]{1,0:T(8,128)(2,1)S(1)}, bf16[256,128]{1,0:T(8,128)(2,1)S(1)}, u32[]{:S(2)}, u32[]{:S(2)}) collective-permute-start(bf16[256,128]{1,0:T(8,128)(2,1)S(1)} %get-tuple-element.61), channel_id=1, source_target_pairs={{0,2},{1,3},{2,0},{3,1},{4,6},{5,7},{6,4},{7,5},{8,10},{9,11},{10,... | collective-permute-start | bytes 196616 | tf_op jit(solution)/shard_map/ppermute | solution.py:208
  17.5 0.7 %collective-permute-start.7 = (f32[64,128]{1,0:T(8,128)S(1)}, f32[64,128]{1,0:T(8,128)S(1)}, u32[]{:S(2)}, u32[]{:S(2)}) collective-permute-start(f32[64,128]{1,0:T(8,128)S(1)} %copy-done.1), channel_id=1, source_target_pairs={{0,2},{1,3},{2,0},{3,1},{4,6},{5,7},{6,4},{7,5},{8,10},{9,11},{10,... | collective-permute-start | bytes 98312 | tf_op jit(solution)/shard_map/ppermute | solution.py:208
  18.2 3.2 %collective-permute-done.7.refs_3_ = f32[64,128]{1,0:T(8,128)S(1)} collective-permute-done((f32[64,128]{1,0:T(8,128)S(1)}, f32[64,128]{1,0:T(8,128)S(1)}, u32[]{:S(2)}, u32[]{:S(2)}) %collective-permute-start.7) | collective-permute-done | bytes 32800 | tf_op jit(solution)/shard_map/ppermute | solution.py:208
  21.4 0.1 shard_map.81
  21.6 0.2 shard_map.82
  21.9 1.0 %collective-permute-done.8.refs_3_.refs_1_ = bf16[128,256]{1,0:T(8,128)(2,1)S(1)} collective-permute-done((bf16[128,256]{1,0:T(8,128)(2,1)S(1)}, bf16[128,256]{1,0:T(8,128)(2,1)S(1)}, u32[]{:S(2)}, u32[]{:S(2)}) %collective-permute-start.8) | collective-permute-done | bytes 65568 | tf_op jit(solution)/shard_map/ppermute | solution.py:208
  22.9 0.2 shard_map.84
  23.1 3.7 %collective-permute-start.9 = (bf16[256,128]{1,0:T(8,128)(2,1)S(1)}, bf16[256,128]{1,0:T(8,128)(2,1)S(1)}, u32[]{:S(2)}, u32[]{:S(2)}) collective-permute-start(bf16[256,128]{1,0:T(8,128)(2,1)S(1)} %shard_map.84), channel_id=1, source_target_pairs={{0,12},{4,8},{8,4},{12,0},{1,13},{5,9},{9,5},{13,1},{2,14},{6,10},... | collective-permute-start | bytes 196616 | tf_op jit(solution)/shard_map/ppermute | solution.py:208
  26.8 0.2 shard_map.85
  27.1 0.2 shard_map.86
  27.4 0.8 %collective-permute-start.11 = (bf16[256,128]{1,0:T(8,128)(2,1)S(1)}, bf16[256,128]{1,0:T(8,128)(2,1)S(1)}, u32[]{:S(2)}, u32[]{:S(2)}) collective-permute-start(bf16[256,128]{1,0:T(8,128)(2,1)S(1)} %shard_map.86), channel_id=1, source_target_pairs={{0,4},{4,0},{8,12},{12,8},{1,5},{5,1},{9,13},{13,9},{2,6},{6,2},{1... | collective-permute-start | bytes 196616 | tf_op jit(solution)/shard_map/ppermute | solution.py:208
  28.2 0.2 shard_map.83
  28.5 0.6 %copy.7 = f32[64,128]{1,0:T(8,128)} copy(f32[64,128]{1,0:T(8,128)S(1)} %get-tuple-element.87) | data formatting | bytes 65536
  29.1 0.4 %collective-permute-done.9.refs_1_ = bf16[256,128]{1,0:T(8,128)(2,1)S(1)} collective-permute-done((bf16[256,128]{1,0:T(8,128)(2,1)S(1)}, bf16[256,128]{1,0:T(8,128)(2,1)S(1)}, u32[]{:S(2)}, u32[]{:S(2)}) %collective-permute-start.9) | collective-permute-done | bytes 65568 | tf_op jit(solution)/shard_map/ppermute | solution.py:208
  29.6 2.9 %collective-permute-done.10.refs_2_ = bf16[256,128]{1,0:T(8,128)(2,1)S(1)} collective-permute-done((bf16[256,128]{1,0:T(8,128)(2,1)S(1)}, bf16[256,128]{1,0:T(8,128)(2,1)S(1)}, u32[]{:S(2)}, u32[]{:S(2)}) %collective-permute-start.10) | collective-permute-done | bytes 65568 | tf_op jit(solution)/shard_map/ppermute | solution.py:208
  32.5 0.6 %collective-permute-done.11.refs_3_ = bf16[256,128]{1,0:T(8,128)(2,1)S(1)} collective-permute-done((bf16[256,128]{1,0:T(8,128)(2,1)S(1)}, bf16[256,128]{1,0:T(8,128)(2,1)S(1)}, u32[]{:S(2)}, u32[]{:S(2)}) %collective-permute-start.11) | collective-permute-done | bytes 65568 | tf_op jit(solution)/shard_map/ppermute | solution.py:208
  33.0 0.7 %shard_map.87 = bf16[256,128]{1,0:T(8,128)(2,1)} custom-call(f32[256,128]{1,0:T(8,128)S(1)} %get-tuple-element.75.refs_0_, bf16[256,128]{1,0:T(8,128)(2,1)S(1)} %collective-permute-done.9.refs_1_, bf16[256,128]{1,0:T(8,128)(2,1)S(1)} %collective-permute-done.10.refs_2_, bf16[256,128]{1,0:T(8,128)(2,1)S(1)} %collective-permute-done.11.refs_3_), custom_call_target="tpu_custom_call" | custom-call | tf_op jit(solution)/shard_map/pallas_call | solution.py:64
  (17 shorter events, 0.4 us)
Async XLA Ops:
  1.6 11.0 %collective-permute-start.4 = (bf16[288,128]{1,0:T(8,128)(2,1)S(1)}, bf16[288,128]{1,0:T(8,128)(2,1)S(1)}, u32[]{:S(2)}, u32[]{:S(2)}) collective-permute-start(bf16[288,128]{1,0:T(8,128)(2,1)S(1)} %get-tuple-element.44.refs_0_), channel_id=1, source_target_pairs={{0,12},{4,8},{8,4},{12,0},{1,13},{5,9},{9,5},{13,1},{2,14},{6,10},... | collective-permute-start | bytes 221192 | tf_op jit(solution)/shard_map/ppermute | solution.py:208
  6.7 6.6 %collective-permute-start.3 = (bf16[288,128]{1,0:T(8,128)(2,1)S(1)}, bf16[288,128]{1,0:T(8,128)(2,1)S(1)}, u32[]{:S(2)}, u32[]{:S(2)}) collective-permute-start(bf16[288,128]{1,0:T(8,128)(2,1)S(1)} %get-tuple-element.44.refs_0_), channel_id=1, source_target_pairs={{0,8},{4,12},{8,0},{12,4},{1,9},{5,13},{9,1},{13,5},{2,10},{6,14},... | collective-permute-start | bytes 221192 | tf_op jit(solution)/shard_map/ppermute | solution.py:208
  6.7 7.4 %collective-permute-start = (bf16[288,128]{1,0:T(8,128)(2,1)S(1)}, bf16[288,128]{1,0:T(8,128)(2,1)S(1)}, u32[]{:S(2)}, u32[]{:S(2)}) collective-permute-start(bf16[288,128]{1,0:T(8,128)(2,1)S(1)} %get-tuple-element.44.refs_0_), channel_id=1, source_target_pairs={{0,4},{4,0},{8,12},{12,8},{1,5},{5,1},{9,13},{13,9},{2,6},{6,2},{1... | collective-permute-start | bytes 221192 | tf_op jit(solution)/shard_map/ppermute | solution.py:208
  7.3 1.2 %collective-permute-start.1 = (f32[8,128]{1,0:T(8,128)S(1)}, f32[8,128]{1,0:T(8,128)S(1)}, u32[]{:S(2)}, u32[]{:S(2)}) collective-permute-start(f32[8,128]{1,0:T(8,128)S(1)} %get-tuple-element.45.own_ref), channel_id=1, source_target_pairs={{0,1},{1,0},{2,3},{3,2},{4,5},{5,4},{6,7},{7,6},{8,9},{9,8},{10,11... | collective-permute-start | bytes 12296 | tf_op jit(solution)/shard_map/ppermute | solution.py:208
  8.5 3.7 %collective-permute-start.2 = (f32[16,128]{1,0:T(8,128)S(1)}, f32[16,128]{1,0:T(8,128)S(1)}, u32[]{:S(2)}, u32[]{:S(2)}) collective-permute-start(f32[16,128]{1,0:T(8,128)S(1)} %shard_map.69.refs_0_), channel_id=1, source_target_pairs={{0,2},{1,3},{2,0},{3,1},{4,6},{5,7},{6,4},{7,5},{8,10},{9,11},{10,... | collective-permute-start | bytes 24584 | tf_op jit(solution)/shard_map/ppermute | solution.py:208
  14.4 1.3 %collective-permute-start.5 = (bf16[256,128]{1,0:T(8,128)(2,1)S(1)}, bf16[256,128]{1,0:T(8,128)(2,1)S(1)}, u32[]{:S(2)}, u32[]{:S(2)}) collective-permute-start(bf16[256,128]{1,0:T(8,128)(2,1)S(1)} %get-tuple-element.59), channel_id=1, source_target_pairs={{0,1},{1,0},{2,3},{3,2},{4,5},{5,4},{6,7},{7,6},{8,9},{9,8},{10,11... | collective-permute-start | bytes 196616 | tf_op jit(solution)/shard_map/ppermute | solution.py:208
  15.8 1.8 %copy-start.1 = (f32[64,128]{1,0:T(8,128)S(1)}, f32[64,128]{1,0:T(8,128)}, u32[]{:S(2)}) copy-start(f32[64,128]{1,0:T(8,128)} %refs_2_.1) | copy-start | bytes 98308
  15.8 5.7 %collective-permute-start.6 = (bf16[256,128]{1,0:T(8,128)(2,1)S(1)}, bf16[256,128]{1,0:T(8,128)(2,1)S(1)}, u32[]{:S(2)}, u32[]{:S(2)}) collective-permute-start(bf16[256,128]{1,0:T(8,128)(2,1)S(1)} %get-tuple-element.61), channel_id=1, source_target_pairs={{0,2},{1,3},{2,0},{3,1},{4,6},{5,7},{6,4},{7,5},{8,10},{9,11},{10,... | collective-permute-start | bytes 196616 | tf_op jit(solution)/shard_map/ppermute | solution.py:208
  17.5 3.9 %collective-permute-start.7 = (f32[64,128]{1,0:T(8,128)S(1)}, f32[64,128]{1,0:T(8,128)S(1)}, u32[]{:S(2)}, u32[]{:S(2)}) collective-permute-start(f32[64,128]{1,0:T(8,128)S(1)} %copy-done.1), channel_id=1, source_target_pairs={{0,2},{1,3},{2,0},{3,1},{4,6},{5,7},{6,4},{7,5},{8,10},{9,11},{10,... | collective-permute-start | bytes 98312 | tf_op jit(solution)/shard_map/ppermute | solution.py:208
  21.6 1.3 %collective-permute-start.8 = (bf16[128,256]{1,0:T(8,128)(2,1)S(1)}, bf16[128,256]{1,0:T(8,128)(2,1)S(1)}, u32[]{:S(2)}, u32[]{:S(2)}) collective-permute-start(bf16[128,256]{1,0:T(8,128)(2,1)S(1)} %get-tuple-element.63.refs_0_), channel_id=1, source_target_pairs={{0,1},{1,0},{2,3},{3,2},{4,5},{5,4},{6,7},{7,6},{8,9},{9,8},{10,11... | collective-permute-start | bytes 196616 | tf_op jit(solution)/shard_map/ppermute | solution.py:208
  23.1 6.4 %collective-permute-start.9 = (bf16[256,128]{1,0:T(8,128)(2,1)S(1)}, bf16[256,128]{1,0:T(8,128)(2,1)S(1)}, u32[]{:S(2)}, u32[]{:S(2)}) collective-permute-start(bf16[256,128]{1,0:T(8,128)(2,1)S(1)} %shard_map.84), channel_id=1, source_target_pairs={{0,12},{4,8},{8,4},{12,0},{1,13},{5,9},{9,5},{13,1},{2,14},{6,10},... | collective-permute-start | bytes 196616 | tf_op jit(solution)/shard_map/ppermute | solution.py:208
  27.0 5.4 %collective-permute-start.10 = (bf16[256,128]{1,0:T(8,128)(2,1)S(1)}, bf16[256,128]{1,0:T(8,128)(2,1)S(1)}, u32[]{:S(2)}, u32[]{:S(2)}) collective-permute-start(bf16[256,128]{1,0:T(8,128)(2,1)S(1)} %shard_map.85), channel_id=1, source_target_pairs={{0,8},{4,12},{8,0},{12,4},{1,9},{5,13},{9,1},{13,5},{2,10},{6,14},... | collective-permute-start | bytes 196616 | tf_op jit(solution)/shard_map/ppermute | solution.py:208
  27.1 1.1 %copy-start = (f32[2,64,128]{2,1,0:T(8,128)S(1)}, f32[2,64,128]{2,1,0:T(8,128)}, u32[]{:S(2)}) copy-start(f32[2,64,128]{2,1,0:T(8,128)} %refs_1_.1) | copy-start | bytes 196612
  27.4 5.6 %collective-permute-start.11 = (bf16[256,128]{1,0:T(8,128)(2,1)S(1)}, bf16[256,128]{1,0:T(8,128)(2,1)S(1)}, u32[]{:S(2)}, u32[]{:S(2)}) collective-permute-start(bf16[256,128]{1,0:T(8,128)(2,1)S(1)} %shard_map.86), channel_id=1, source_target_pairs={{0,4},{4,0},{8,12},{12,8},{1,5},{5,1},{9,13},{13,9},{2,6},{6,2},{1... | collective-permute-start | bytes 196616 | tf_op jit(solution)/shard_map/ppermute | solution.py:208
where the time goes:
time: 33.9 us; the launch traced here: 33.7 us
  starting transfers between devices  14.5 us (43%)
  waiting for transfers between devices  11.7 us (35%)
  Pallas kernels  6.04 us (18%)
  between operations  0.81 us (2%)
  local copies, waits for them, and re-layouts  0.63 us (2%)
    ppermute x12, starting transfers between devices, swap(): return lax.ppermute(value, axis, [(i, i ^ flip) for i in range(size)])  14.5 us
    ppermute x12, waiting for transfers between devices, swap(): return lax.ppermute(value, axis, [(i, i ^ flip) for i in range(size)])  11.7 us
    pallas_call x20, Pallas kernels, call(): pl.pallas_call(body, out_shape=outs, in_specs=full_spec(len(args)), out_s...  6.04 us
  transfers between devices with their start and end apart: 12, of which 8 were waited for; matrix products, arithmetic and copies ran while one was open for 2% of the time, Pallas kernels for 11%

commit v1 on v0

--- a/solution.py
+++ b/solution.py
@@ -104,35 +104,40 @@
         out_ref[h * nk : (h + 1) * nk, :] = cols[0:nk].astype(bf16)
 
 
-def factor_body(natom, nk, blocks, first, last, *refs):
-    zb = refs[0]
-    refs = refs[1:]
-    count = len(blocks)
-    tables, refs = refs[:count], refs[count:]
-    before, refs = ((), refs) if first else (refs[:count], refs[count:])
-    tiles, outs = refs[:count], refs[count:]
-    width = zb.shape[1]
-    parts = jnp.concatenate([zb[natom + 16 * j : natom + 16 * (j + 1), :] for j in range(natom // width)], 1)
-    phases = [
-        jnp.dot(table[h * nk : (h + 1) * nk, :], parts, preferred_element_type=f32)
-        for table, h in zip(tables, (t % 2 for t in blocks))
-    ]
-    cot = zb[0:natom, :]
+def factor_body(natom, nk, pairs, blocks, started, last, *refs):
+    atoms = sorted({z for z, t in pairs})
+    zb, refs = dict(zip(atoms, refs)), refs[len(atoms) :]
+    tables, refs = dict(zip(blocks, refs)), refs[len(blocks) :]
+    before, refs = (dict(zip(blocks, refs)), refs[len(blocks) :]) if started else ({}, refs)
+    tiles, outs = dict(zip(pairs, refs)), refs[len(pairs) :]
+    width = zb[atoms[0]].shape[1]
+    parts = {
+        z: jnp.concatenate([ref[natom + 16 * j : natom + 16 * (j + 1), :] for j in range(natom // width)], 1)
+        for z, ref in zb.items()
+    }
+    phases = {}
+    for z, t in pairs:
+        table = tables[t][(t % 2) * nk : (t % 2 + 1) * nk, :]
+        phases[z, t] = jnp.dot(table, parts[z], preferred_element_type=f32)
+    cot = {z: ref[0:natom, :] for z, ref in zb.items()}
     step = 32
-    for b in range(count):
+    for b, t in enumerate(blocks):
         for i in range(0, nk, step):
-            for k, value in enumerate(cos_sin(phases[b][i : i + step])):
-                rows = pl.ds(k * nk + i, step)
-                value = value.astype(bf16)
-                tiles[b][rows, :] = value
-                total = jnp.dot(value, cot, preferred_element_type=f32)
-                if not first:
-                    total = total + before[b][rows, :]
+            sums = [None, None]
+            for z in atoms:
+                for k, value in enumerate(cos_sin(phases[z, t][i : i + step])):
+                    value = value.astype(bf16)
+                    tiles[z, t][k * nk + i : k * nk + i + step, :] = value
+                    part = jnp.dot(value, cot[z], preferred_element_type=f32)
+                    sums[k] = part if sums[k] is None else sums[k] + part
+            for k, total in enumerate(sums):
+                row = k * nk + i
+                if started:
+                    total = total + before[t][row : row + step, :]
                 if last:
-                    rows = pl.ds(2 * nk * b + k * nk + i, step)
-                    outs[0][rows, :] = total.astype(outs[0].dtype)
+                    outs[0][2 * nk * b + row : 2 * nk * b + row + step, :] = total.astype(outs[0].dtype)
                 else:
-                    outs[b][rows, :] = total
+                    outs[b][row : row + step, :] = total
 
 
 def shuffled(ref, flip, half, nk):
@@ -235,33 +240,34 @@
     tiles = {}
     total = {}
 
-    def factor(s, blocks, first=False, last=None):
-        outs = [shape((2 * nk, natom), bf16)] * len(blocks)
-        sums = [shape((2 * nk, width), f32)] * len(blocks)
-        if last is not None:
-            sums = [shape((2 * nk * len(blocks), width), last)]
-        args = [zb[s]] + [table[t] for t in blocks] + ([] if first else [total[t] for t in blocks])
-        body = lambda *refs: factor_body(natom, nk, blocks, first, last is not None, *refs)
-        got = run(body, outs + sums, *args)
-        for t, tile in zip(blocks, got):
-            tiles[s, t] = tile
-        if last is not None:
-            return got[-1]
-        for t, value in zip(blocks, got[len(blocks) :]):
-            total[t] = value
-        return None
+    def factor(atoms, blocks, last=None):
+        pairs = [(z, t) for z in sorted(atoms) for t in blocks]
+        outs = [shape((2 * nk, natom), bf16)] * len(pairs)
+        if last is None:
+            outs += [shape((2 * nk, width), f32)] * len(blocks)
+        else:
+            outs.append(shape((2 * nk * len(blocks), width), last))
+        started = blocks[0] in total
+        args = [zb[z] for z in sorted(atoms)] + [table[t] for t in blocks] + [total[t] for t in blocks if started]
+        body = lambda *refs: factor_body(natom, nk, pairs, blocks, started, last is not None, *refs)
+        got = run(body, outs, *args)
+        tiles.update(zip(pairs, got))
+        if last is None:
+            total.update(zip(blocks, got[len(pairs) :]))
+        return got[-1]
 
     order = [0] + far
-    for s in order[:-1]:
-        for t in range(0, nq, 2):
-            factor(s, [t, t + 1], first=s == order[0])
-    sent = factor(order[-1], theirs, last=bf16)
-    kept = factor(order[-1], mine, last=f32)
+    early = order[: min(2, len(order) - 1)]
+    for z in early:
+        factor([z], [0, 1])
+    for t in flips:
+        factor(early, [t, t + 1])
+    for z in order[len(early) : -1]:
+        factor([z], list(range(nq)))
+    sent = factor(order[-1:], theirs, bf16)
+    kept = factor(order[-1:], mine, f32)
     pair, pair16 = run(
-        pair_body,
-        [shape((2 * count, width), f32), shape((2 * count, width), bf16)],
-        kept,
-        swap(sent, "kvec", nq, 1),
+        pair_body, [shape((2 * count, width), f32), shape((2 * count, width), bf16)], kept, swap(sent, "kvec", nq, 1)
     )
     got = [swap(pair16, "kvec", nq, s) for s in flips]
     weight, head = run(
@@ -298,11 +304,7 @@
         *[tiles[0, t] for t in theirs],
     )
     (node_grad,) = run(
-        lambda *refs: final_body(scale_k, *refs),
-        [shape((natom, width), bf16)],
-        own,
-        *landed,
-        keep_outs=False,
+        lambda *refs: final_body(scale_k, *refs), [shape((natom, width), bf16)], own, *landed, keep_outs=False
     )
     return (node_grad, filter_grad)
 

time: 33.9 us -> 33.5 us (0.988)
  Pallas kernels: 6.04 us -> 5.57 us
    pallas_call x20 -> x18, Pallas kernels: 6.04 us -> 5.57 us  [call(): pl.pallas_call(body, out_shape=outs, in_specs=full_spec(len(args)), out_s...]
  transfers between devices with their start and end apart: 12 -> 12, of which waited for: 8 -> 8; matrix products, arithmetic and copies ran while one was open for 2% -> 2% of each run, Pallas kernels for 11% -> 10%
where the time goes in v1:
time: 33.5 us; the launch traced here: 33.2 us
  starting transfers between devices  14.5 us (43%)
  waiting for transfers between devices  11.8 us (35%)
  Pallas kernels  5.57 us (17%)
  between operations  0.79 us (2%)
  local copies, waits for them, and re-layouts  0.63 us (2%)
    ppermute x12, starting transfers between devices, swap(): return lax.ppermute(value, axis, [(i, i ^ flip) for i in range(size)])  14.5 us
    ppermute x12, waiting for transfers between devices, swap(): return lax.ppermute(value, axis, [(i, i ^ flip) for i in range(size)])  11.8 us
    pallas_call x18, Pallas kernels, call(): pl.pallas_call(body, out_shape=outs, in_specs=full_spec(len(args)), out_s...  5.57 us
  transfers between devices with their start and end apart: 12, of which 8 were waited for; matrix products, arithmetic and copies ran while one was open for 2% of the time, Pallas kernels for 10%

profile of v1, /device:TPU:0, one launch (start us, length us, event | category | flops | bytes accessed | tf_op | source)
XLA Modules:
  0.0 33.2 jit_solution(17604921911213380596)
XLA Ops:
  0.6 1.0 %shard_map.68 = (bf16[288,128]{1,0:T(8,128)(2,1)S(1)}, f32[8,128]{1,0:T(8,128)S(1)}) custom-call(s32[3,64]{1,0:T(4,128)} %lat_ref.1, f32[3,256]{1,0:T(4,128)} %pos_ref.1, bf16[256,128]{1,0:T(8,128)(2,1)} %cot_ref.1), custom_call_target="tpu_custom_call" | custom-call | tf_op jit(solution)/shard_map/pallas_call | solution.py:64
  1.6 5.1 %collective-permute-start.4 = (bf16[288,128]{1,0:T(8,128)(2,1)S(1)}, bf16[288,128]{1,0:T(8,128)(2,1)S(1)}, u32[]{:S(2)}, u32[]{:S(2)}) collective-permute-start(bf16[288,128]{1,0:T(8,128)(2,1)S(1)} %get-tuple-element.42.refs_0_), channel_id=1, source_target_pairs={{0,12},{4,8},{8,4},{12,0},{1,13},{5,9},{9,5},{13,1},{2,14},{6,10},... | collective-permute-start | bytes 221192 | tf_op jit(solution)/shard_map/ppermute | solution.py:213
  6.7 0.6 %collective-permute-start = (bf16[288,128]{1,0:T(8,128)(2,1)S(1)}, bf16[288,128]{1,0:T(8,128)(2,1)S(1)}, u32[]{:S(2)}, u32[]{:S(2)}) collective-permute-start(bf16[288,128]{1,0:T(8,128)(2,1)S(1)} %get-tuple-element.42.refs_0_), channel_id=1, source_target_pairs={{0,4},{4,0},{8,12},{12,8},{1,5},{5,1},{9,13},{13,9},{2,6},{6,2},{1... | collective-permute-start | bytes 221192 | tf_op jit(solution)/shard_map/ppermute | solution.py:213
  7.3 1.2 %collective-permute-done.1.got_ref = f32[8,128]{1,0:T(8,128)S(1)} collective-permute-done((f32[8,128]{1,0:T(8,128)S(1)}, f32[8,128]{1,0:T(8,128)S(1)}, u32[]{:S(2)}, u32[]{:S(2)}) %collective-permute-start.1) | collective-permute-done | bytes 4128 | tf_op jit(solution)/shard_map/ppermute | solution.py:213
  8.5 1.7 %collective-permute-start.2 = (f32[16,128]{1,0:T(8,128)S(1)}, f32[16,128]{1,0:T(8,128)S(1)}, u32[]{:S(2)}, u32[]{:S(2)}) collective-permute-start(f32[16,128]{1,0:T(8,128)S(1)} %shard_map.69.refs_0_), channel_id=1, source_target_pairs={{0,2},{1,3},{2,0},{3,1},{4,6},{5,7},{6,4},{7,5},{8,10},{9,11},{10,... | collective-permute-start | bytes 24584 | tf_op jit(solution)/shard_map/ppermute | solution.py:213
  10.2 0.1 shard_map.70.refs_1_.refs_2_
  10.2 0.4 %shard_map.72 = (bf16[128,256]{1,0:T(8,128)(2,1)S(1)}, bf16[128,256]{1,0:T(8,128)(2,1)S(1)}, f32[128,128]{1,0:T(8,128)S(1)}, f32[128,128]{1,0:T(8,128)S(1)}) custom-call(bf16[288,128]{1,0:T(8,128)(2,1)S(1)} %get-tuple-element.42.refs_0_, bf16[128,16]{1,0:T(8,128)(2,1)S(1)} %shard_map.70.refs_1_.refs_2_, bf16[128,16]{1,0:T(8,128)(2,1)S(1)} %shard_map.70.refs_1_.refs_2_), custom_call_target="tpu_custom_call" | custom-call | tf_op jit(solution)/shard_map/pallas_call | solution.py:64
  10.6 1.5 %collective-permute-done.2.refs_0_ = f32[16,128]{1,0:T(8,128)S(1)} collective-permute-done((f32[16,128]{1,0:T(8,128)S(1)}, f32[16,128]{1,0:T(8,128)S(1)}, u32[]{:S(2)}, u32[]{:S(2)}) %collective-permute-start.2) | collective-permute-done | bytes 8224 | tf_op jit(solution)/shard_map/ppermute | solution.py:213
  12.1 0.1 shard_map.71.refs_2_.refs_3_.refs_4_
  12.2 0.5 %shard_map.74 = (bf16[128,256]{1,0:T(8,128)(2,1)S(1)}, bf16[128,256]{1,0:T(8,128)(2,1)S(1)}, bf16[128,256]{1,0:T(8,128)(2,1)S(1)}, bf16[128,256]{1,0:T(8,128)(2,...) custom-call(bf16[288,128]{1,0:T(8,128)(2,1)S(1)} %get-tuple-element.42.refs_0_, ...), custom_call_target="tpu_custom_call" | custom-call | tf_op jit(solution)/shard_map/pallas_call | solution.py:64
  12.7 0.4 %shard_map.73 = (bf16[128,256]{1,0:T(8,128)(2,1)S(1)}, bf16[128,256]{1,0:T(8,128)(2,1)S(1)}, f32[128,128]{1,0:T(8,128)S(1)}, f32[128,128]{1,0:T(8,128)S(1)}) custom-call(bf16[288,128]{1,0:T(8,128)(2,1)S(1)} %collective-permute-done.4.refs_0_.refs_1_, bf16[128,16]{1,0:T(8,128)(2,1)S(1)} %shard_map.70.refs_1_.refs_2_, ...), custom_call_target="tpu_custom_call" | custom-call | tf_op jit(solution)/shard_map/pallas_call | solution.py:64
  13.1 0.5 %shard_map.75 = (bf16[128,256]{1,0:T(8,128)(2,1)S(1)}, bf16[128,256]{1,0:T(8,128)(2,1)S(1)}, bf16[128,256]{1,0:T(8,128)(2,1)S(1)}, bf16[128,256]{1,0:T(8,128)(2,...) custom-call(bf16[288,128]{1,0:T(8,128)(2,1)S(1)} %collective-permute-, ...), custom_call_target="tpu_custom_call" | custom-call | tf_op jit(solution)/shard_map/pallas_call | solution.py:64
  13.6 0.4 %shard_map.77 = (bf16[128,256]{1,0:T(8,128)(2,1)S(1)}, bf16[128,256]{1,0:T(8,128)(2,1)S(1)}, bf16[256,128]{1,0:T(8,128)(2,1)S(1)}) custom-call(bf16[288,128]{1,0:T(8,128)(2,1)S(1)} %collective-permute-done.refs_0_, bf16[128,16]{1,0:T(8,128)(2,1)S(1)} %shard_map.70.refs_1_.refs_2_, bf16[128,16]{1,0:T(8,128)(2,1)S(1)} %shard_map.71.refs_2_.refs_3_.refs_4_, ...), custom_call_target="tpu_custom_call" | custom-call | tf_op jit(solution)/shard_map/pallas_call | solution.py:64
  14.0 0.4 %shard_map.76 = (bf16[128,256]{1,0:T(8,128)(2,1)S(1)}, bf16[128,256]{1,0:T(8,128)(2,1)S(1)}, f32[256,128]{1,0:T(8,128)S(1)}) custom-call(bf16[288,128]{1,0:T(8,128)(2,1)S(1)} %collective-permute-done.refs_0_, bf16[128,16]{1,0:T(8,128)(2,1)S(1)} %shard_map.70.refs_1_.refs_2_, bf16[128,16]{1,0:T(8,128)(2,1)S(1)} %shard_map.71.refs_2_.refs_3_.refs_4_, ...), custom_call_target="tpu_custom_call" | custom-call | tf_op jit(solution)/shard_map/pallas_call | solution.py:64
  14.4 0.9 %collective-permute-done.5.got_ref = bf16[256,128]{1,0:T(8,128)(2,1)S(1)} collective-permute-done((bf16[256,128]{1,0:T(8,128)(2,1)S(1)}, bf16[256,128]{1,0:T(8,128)(2,1)S(1)}, u32[]{:S(2)}, u32[]{:S(2)}) %collective-permute-start.5) | collective-permute-done | bytes 65568 | tf_op jit(solution)/shard_map/ppermute | solution.py:213
  15.3 1.7 %collective-permute-start.6 = (bf16[256,128]{1,0:T(8,128)(2,1)S(1)}, bf16[256,128]{1,0:T(8,128)(2,1)S(1)}, u32[]{:S(2)}, u32[]{:S(2)}) collective-permute-start(bf16[256,128]{1,0:T(8,128)(2,1)S(1)} %get-tuple-element.57), channel_id=1, source_target_pairs={{0,2},{1,3},{2,0},{3,1},{4,6},{5,7},{6,4},{7,5},{8,10},{9,11},{10,... | collective-permute-start | bytes 196616 | tf_op jit(solution)/shard_map/ppermute | solution.py:213
  17.1 0.7 %collective-permute-start.7 = (f32[64,128]{1,0:T(8,128)S(1)}, f32[64,128]{1,0:T(8,128)S(1)}, u32[]{:S(2)}, u32[]{:S(2)}) collective-permute-start(f32[64,128]{1,0:T(8,128)S(1)} %copy-done.1), channel_id=1, source_target_pairs={{0,2},{1,3},{2,0},{3,1},{4,6},{5,7},{6,4},{7,5},{8,10},{9,11},{10,... | collective-permute-start | bytes 98312 | tf_op jit(solution)/shard_map/ppermute | solution.py:213
  17.7 3.2 %collective-permute-done.7.refs_3_ = f32[64,128]{1,0:T(8,128)S(1)} collective-permute-done((f32[64,128]{1,0:T(8,128)S(1)}, f32[64,128]{1,0:T(8,128)S(1)}, u32[]{:S(2)}, u32[]{:S(2)}) %collective-permute-start.7) | collective-permute-done | bytes 32800 | tf_op jit(solution)/shard_map/ppermute | solution.py:213
  21.0 0.1 shard_map.79
  21.2 0.2 shard_map.80
  21.4 1.0 %collective-permute-done.8.refs_3_.refs_1_ = bf16[128,256]{1,0:T(8,128)(2,1)S(1)} collective-permute-done((bf16[128,256]{1,0:T(8,128)(2,1)S(1)}, bf16[128,256]{1,0:T(8,128)(2,1)S(1)}, u32[]{:S(2)}, u32[]{:S(2)}) %collective-permute-start.8) | collective-permute-done | bytes 65568 | tf_op jit(solution)/shard_map/ppermute | solution.py:213
  22.4 0.2 shard_map.82
  22.7 3.7 %collective-permute-start.9 = (bf16[256,128]{1,0:T(8,128)(2,1)S(1)}, bf16[256,128]{1,0:T(8,128)(2,1)S(1)}, u32[]{:S(2)}, u32[]{:S(2)}) collective-permute-start(bf16[256,128]{1,0:T(8,128)(2,1)S(1)} %shard_map.82), channel_id=1, source_target_pairs={{0,12},{4,8},{8,4},{12,0},{1,13},{5,9},{9,5},{13,1},{2,14},{6,10},... | collective-permute-start | bytes 196616 | tf_op jit(solution)/shard_map/ppermute | solution.py:213
  26.3 0.2 shard_map.83
  26.7 0.2 shard_map.84
  26.9 0.8 %collective-permute-start.11 = (bf16[256,128]{1,0:T(8,128)(2,1)S(1)}, bf16[256,128]{1,0:T(8,128)(2,1)S(1)}, u32[]{:S(2)}, u32[]{:S(2)}) collective-permute-start(bf16[256,128]{1,0:T(8,128)(2,1)S(1)} %shard_map.84), channel_id=1, source_target_pairs={{0,4},{4,0},{8,12},{12,8},{1,5},{5,1},{9,13},{13,9},{2,6},{6,2},{1... | collective-permute-start | bytes 196616 | tf_op jit(solution)/shard_map/ppermute | solution.py:213
  27.8 0.2 shard_map.81
  28.0 0.6 %copy.7 = f32[64,128]{1,0:T(8,128)} copy(f32[64,128]{1,0:T(8,128)S(1)} %get-tuple-element.83) | data formatting | bytes 65536
  28.6 0.5 %collective-permute-done.9.refs_1_ = bf16[256,128]{1,0:T(8,128)(2,1)S(1)} collective-permute-done((bf16[256,128]{1,0:T(8,128)(2,1)S(1)}, bf16[256,128]{1,0:T(8,128)(2,1)S(1)}, u32[]{:S(2)}, u32[]{:S(2)}) %collective-permute-start.9) | collective-permute-done | bytes 65568 | tf_op jit(solution)/shard_map/ppermute | solution.py:213
  29.1 2.9 %collective-permute-done.10.refs_2_ = bf16[256,128]{1,0:T(8,128)(2,1)S(1)} collective-permute-done((bf16[256,128]{1,0:T(8,128)(2,1)S(1)}, bf16[256,128]{1,0:T(8,128)(2,1)S(1)}, u32[]{:S(2)}, u32[]{:S(2)}) %collective-permute-start.10) | collective-permute-done | bytes 65568 | tf_op jit(solution)/shard_map/ppermute | solution.py:213
  32.0 0.6 %collective-permute-done.11.refs_3_ = bf16[256,128]{1,0:T(8,128)(2,1)S(1)} collective-permute-done((bf16[256,128]{1,0:T(8,128)(2,1)S(1)}, bf16[256,128]{1,0:T(8,128)(2,1)S(1)}, u32[]{:S(2)}, u32[]{:S(2)}) %collective-permute-start.11) | collective-permute-done | bytes 65568 | tf_op jit(solution)/shard_map/ppermute | solution.py:213
  32.6 0.7 %shard_map.85 = bf16[256,128]{1,0:T(8,128)(2,1)} custom-call(f32[256,128]{1,0:T(8,128)S(1)} %get-tuple-element.71.refs_0_, bf16[256,128]{1,0:T(8,128)(2,1)S(1)} %collective-permute-done.9.refs_1_, bf16[256,128]{1,0:T(8,128)(2,1)S(1)} %collective-permute-done.10.refs_2_, bf16[256,128]{1,0:T(8,128)(2,1)S(1)} %collective-permute-done.11.refs_3_), custom_call_target="tpu_custom_call" | custom-call | tf_op jit(solution)/shard_map/pallas_call | solution.py:64
  (15 shorter events, 0.3 us)
Async XLA Ops:
  1.6 10.6 %collective-permute-start.4 = (bf16[288,128]{1,0:T(8,128)(2,1)S(1)}, bf16[288,128]{1,0:T(8,128)(2,1)S(1)}, u32[]{:S(2)}, u32[]{:S(2)}) collective-permute-start(bf16[288,128]{1,0:T(8,128)(2,1)S(1)} %get-tuple-element.42.refs_0_), channel_id=1, source_target_pairs={{0,12},{4,8},{8,4},{12,0},{1,13},{5,9},{9,5},{13,1},{2,14},{6,10},... | collective-permute-start | bytes 221192 | tf_op jit(solution)/shard_map/ppermute | solution.py:213
  6.7 6.4 %collective-permute-start.3 = (bf16[288,128]{1,0:T(8,128)(2,1)S(1)}, bf16[288,128]{1,0:T(8,128)(2,1)S(1)}, u32[]{:S(2)}, u32[]{:S(2)}) collective-permute-start(bf16[288,128]{1,0:T(8,128)(2,1)S(1)} %get-tuple-element.42.refs_0_), channel_id=1, source_target_pairs={{0,8},{4,12},{8,0},{12,4},{1,9},{5,13},{9,1},{13,5},{2,10},{6,14},... | collective-permute-start | bytes 221192 | tf_op jit(solution)/shard_map/ppermute | solution.py:213
  6.7 6.9 %collective-permute-start = (bf16[288,128]{1,0:T(8,128)(2,1)S(1)}, bf16[288,128]{1,0:T(8,128)(2,1)S(1)}, u32[]{:S(2)}, u32[]{:S(2)}) collective-permute-start(bf16[288,128]{1,0:T(8,128)(2,1)S(1)} %get-tuple-element.42.refs_0_), channel_id=1, source_target_pairs={{0,4},{4,0},{8,12},{12,8},{1,5},{5,1},{9,13},{13,9},{2,6},{6,2},{1... | collective-permute-start | bytes 221192 | tf_op jit(solution)/shard_map/ppermute | solution.py:213
  7.3 1.2 %collective-permute-start.1 = (f32[8,128]{1,0:T(8,128)S(1)}, f32[8,128]{1,0:T(8,128)S(1)}, u32[]{:S(2)}, u32[]{:S(2)}) collective-permute-start(f32[8,128]{1,0:T(8,128)S(1)} %get-tuple-element.43.own_ref), channel_id=1, source_target_pairs={{0,1},{1,0},{2,3},{3,2},{4,5},{5,4},{6,7},{7,6},{8,9},{9,8},{10,11... | collective-permute-start | bytes 12296 | tf_op jit(solution)/shard_map/ppermute | solution.py:213
  8.5 3.7 %collective-permute-start.2 = (f32[16,128]{1,0:T(8,128)S(1)}, f32[16,128]{1,0:T(8,128)S(1)}, u32[]{:S(2)}, u32[]{:S(2)}) collective-permute-start(f32[16,128]{1,0:T(8,128)S(1)} %shard_map.69.refs_0_), channel_id=1, source_target_pairs={{0,2},{1,3},{2,0},{3,1},{4,6},{5,7},{6,4},{7,5},{8,10},{9,11},{10,... | collective-permute-start | bytes 24584 | tf_op jit(solution)/shard_map/ppermute | solution.py:213
  14.0 1.3 %collective-permute-start.5 = (bf16[256,128]{1,0:T(8,128)(2,1)S(1)}, bf16[256,128]{1,0:T(8,128)(2,1)S(1)}, u32[]{:S(2)}, u32[]{:S(2)}) collective-permute-start(bf16[256,128]{1,0:T(8,128)(2,1)S(1)} %get-tuple-element.55), channel_id=1, source_target_pairs={{0,1},{1,0},{2,3},{3,2},{4,5},{5,4},{6,7},{7,6},{8,9},{9,8},{10,11... | collective-permute-start | bytes 196616 | tf_op jit(solution)/shard_map/ppermute | solution.py:213
  15.3 1.8 %copy-start.1 = (f32[64,128]{1,0:T(8,128)S(1)}, f32[64,128]{1,0:T(8,128)}, u32[]{:S(2)}) copy-start(f32[64,128]{1,0:T(8,128)} %refs_2_.1) | copy-start | bytes 98308
  15.3 5.7 %collective-permute-start.6 = (bf16[256,128]{1,0:T(8,128)(2,1)S(1)}, bf16[256,128]{1,0:T(8,128)(2,1)S(1)}, u32[]{:S(2)}, u32[]{:S(2)}) collective-permute-start(bf16[256,128]{1,0:T(8,128)(2,1)S(1)} %get-tuple-element.57), channel_id=1, source_target_pairs={{0,2},{1,3},{2,0},{3,1},{4,6},{5,7},{6,4},{7,5},{8,10},{9,11},{10,... | collective-permute-start | bytes 196616 | tf_op jit(solution)/shard_map/ppermute | solution.py:213
  17.1 3.9 %collective-permute-start.7 = (f32[64,128]{1,0:T(8,128)S(1)}, f32[64,128]{1,0:T(8,128)S(1)}, u32[]{:S(2)}, u32[]{:S(2)}) collective-permute-start(f32[64,128]{1,0:T(8,128)S(1)} %copy-done.1), channel_id=1, source_target_pairs={{0,2},{1,3},{2,0},{3,1},{4,6},{5,7},{6,4},{7,5},{8,10},{9,11},{10,... | collective-permute-start | bytes 98312 | tf_op jit(solution)/shard_map/ppermute | solution.py:213
  21.1 1.3 %collective-permute-start.8 = (bf16[128,256]{1,0:T(8,128)(2,1)S(1)}, bf16[128,256]{1,0:T(8,128)(2,1)S(1)}, u32[]{:S(2)}, u32[]{:S(2)}) collective-permute-start(bf16[128,256]{1,0:T(8,128)(2,1)S(1)} %get-tuple-element.59.refs_0_), channel_id=1, source_target_pairs={{0,1},{1,0},{2,3},{3,2},{4,5},{5,4},{6,7},{7,6},{8,9},{9,8},{10,11... | collective-permute-start | bytes 196616 | tf_op jit(solution)/shard_map/ppermute | solution.py:213
  22.7 6.4 %collective-permute-start.9 = (bf16[256,128]{1,0:T(8,128)(2,1)S(1)}, bf16[256,128]{1,0:T(8,128)(2,1)S(1)}, u32[]{:S(2)}, u32[]{:S(2)}) collective-permute-start(bf16[256,128]{1,0:T(8,128)(2,1)S(1)} %shard_map.82), channel_id=1, source_target_pairs={{0,12},{4,8},{8,4},{12,0},{1,13},{5,9},{9,5},{13,1},{2,14},{6,10},... | collective-permute-start | bytes 196616 | tf_op jit(solution)/shard_map/ppermute | solution.py:213
  26.6 5.4 %collective-permute-start.10 = (bf16[256,128]{1,0:T(8,128)(2,1)S(1)}, bf16[256,128]{1,0:T(8,128)(2,1)S(1)}, u32[]{:S(2)}, u32[]{:S(2)}) collective-permute-start(bf16[256,128]{1,0:T(8,128)(2,1)S(1)} %shard_map.83), channel_id=1, source_target_pairs={{0,8},{4,12},{8,0},{12,4},{1,9},{5,13},{9,1},{13,5},{2,10},{6,14},... | collective-permute-start | bytes 196616 | tf_op jit(solution)/shard_map/ppermute | solution.py:213
  26.7 1.1 %copy-start = (f32[2,64,128]{2,1,0:T(8,128)S(1)}, f32[2,64,128]{2,1,0:T(8,128)}, u32[]{:S(2)}) copy-start(f32[2,64,128]{2,1,0:T(8,128)} %refs_1_.1) | copy-start | bytes 196612
  26.9 5.6 %collective-permute-start.11 = (bf16[256,128]{1,0:T(8,128)(2,1)S(1)}, bf16[256,128]{1,0:T(8,128)(2,1)S(1)}, u32[]{:S(2)}, u32[]{:S(2)}) collective-permute-start(bf16[256,128]{1,0:T(8,128)(2,1)S(1)} %shard_map.84), channel_id=1, source_target_pairs={{0,4},{4,0},{8,12},{12,8},{1,5},{5,1},{9,13},{13,9},{2,6},{6,2},{1... | collective-permute-start | bytes 196616 | tf_op jit(solution)/shard_map/ppermute | solution.py:213

commit v2 on v1

--- a/solution.py
+++ b/solution.py
@@ -209,8 +209,11 @@
     scale_k = 1.0 / math.sqrt(nk * nz * nq)
     keep = nz * natom * 4 * count * 2 <= VMEM_BUDGET
 
-    def swap(value, axis, size, flip):
-        return lax.ppermute(value, axis, [(i, i ^ flip) for i in range(size)])
+    def swap(value, flip):
+        return lax.ppermute(value, "kvec", [(i, i ^ flip) for i in range(nq)])
+
+    def shift(value, by):
+        return lax.ppermute(value, "atoms", [(i, (i + by) % nz) for i in range(nz)])
 
     def run(body, outs, *args, keep_args=keep, keep_outs=keep):
         return call(body, outs, *args, keep_args=keep_args, keep_outs=keep_outs)
@@ -223,14 +226,14 @@
         cotangent,
         keep_args=False,
     )
-    far = list(range(nz - 1, 0, -1))
+    ring = gather_order(nz)
     flips = list(range(2, nq, 2))
     zb = {0: zbuf}
-    for s in far:
-        zb[s] = swap(zbuf, "atoms", nz, s)
-    (cores,) = run(join_body, [shape((16, width), f32)], wide, swap(wide, "kvec", nq, 1))
-    lats = [cores] + [swap(cores, "kvec", nq, s) for s in flips]
-    fils = [filters] + [swap(filters, "kvec", nq, s) for s in flips]
+    for d in ring:
+        zb[d] = shift(zbuf, -d)
+    (cores,) = run(join_body, [shape((16, width), f32)], wide, swap(wide, 1))
+    lats = [cores] + [swap(cores, s) for s in flips]
+    fils = [filters] + [swap(filters, s) for s in flips]
     table = {}
     for s, lat in zip([0] + flips, lats):
         (both,) = run(lambda *refs: table_body(nk, *refs), [shape((2 * nk, 16), bf16)], lat)
@@ -256,7 +259,7 @@
             total.update(zip(blocks, got[len(pairs) :]))
         return got[-1]
 
-    order = [0] + far
+    order = [0] + ring
     early = order[: min(2, len(order) - 1)]
     for z in early:
         factor([z], [0, 1])
@@ -267,9 +270,12 @@
     sent = factor(order[-1:], theirs, bf16)
     kept = factor(order[-1:], mine, f32)
     pair, pair16 = run(
-        pair_body, [shape((2 * count, width), f32), shape((2 * count, width), bf16)], kept, swap(sent, "kvec", nq, 1)
-    )
-    got = [swap(pair16, "kvec", nq, s) for s in flips]
+        pair_body,
+        [shape((2 * count, width), f32), shape((2 * count, width), bf16)],
+        kept,
+        swap(sent, 1),
+    )
+    got = [swap(pair16, s) for s in flips]
     weight, head = run(
         lambda *refs: weight_body(half, nk, flips, scale_n, *refs),
         [shape((width, 2 * count), bf16), shape((2 * nk, width), f32)],
@@ -277,23 +283,24 @@
         *got,
         *fils,
     )
-    other = swap(weight, "kvec", nq, 1)
+    other = swap(weight, 1)
     parts = run(
         lambda *refs: mine_body(nz, half, *refs),
         [shape((width, natom), f32)] * nz,
         weight,
         *[tiles[s, t] for s in order for t in mine],
     )
+    parts = dict(zip(order, parts))
     landed = []
-    for s, part in zip(order[1:], parts[1:]):
+    for d in range(1, nz):
         (node,) = run(
             lambda *refs: node_body(half, *refs),
             [shape((natom, width), bf16)],
-            part,
+            parts[d],
             other,
-            *[tiles[s, t] for t in theirs],
+            *[tiles[d, t] for t in theirs],
         )
-        landed.append(swap(node, "atoms", nz, s))
+        landed.append(shift(node, d))
     own, filter_grad = run(
         lambda *refs: own_body(half, *refs),
         [shape((natom, width), f32), shape((nk, width), f32)],
@@ -304,9 +311,20 @@
         *[tiles[0, t] for t in theirs],
     )
     (node_grad,) = run(
-        lambda *refs: final_body(scale_k, *refs), [shape((natom, width), bf16)], own, *landed, keep_outs=False
+        lambda *refs: final_body(scale_k, *refs),
+        [shape((natom, width), bf16)],
+        own,
+        *landed,
+        keep_outs=False,
     )
     return (node_grad, filter_grad)
+
+
+def gather_order(nz):
+    order = []
+    for d in range(1, nz // 2 + 1):
+        order += [nz - d, d] if nz - d != d else [d]
+    return [d for d in order if d]
 
 
 def solution(mesh):

time: 33.5 us -> 32.8 us (0.979)
  waiting for transfers between devices: 11.8 us -> 10.4 us
  starting transfers between devices: 14.5 us -> 15.2 us
    ppermute x12, waiting for transfers between devices: 11.8 us -> 10.4 us  [the longest x6 8 us: swap(): return lax.ppermute(value, 'kvec', [(i, i ^ flip) for i in range(nq)])]
    ppermute x12, starting transfers between devices: 14.5 us -> 15.2 us  [the longest x6 11.3 us: shift(): return lax.ppermute(value, 'atoms', [(i, (i + by) % nz) for i in range(nz)])]
  transfers between devices with their start and end apart: 12 -> 12, of which waited for: 8 -> 6; matrix products, arithmetic and copies ran while one was open for 2% -> 2% of each run, Pallas kernels for 10% -> 10%
where the time goes in v2:
time: 32.8 us; the launch traced here: 32.6 us
  starting transfers between devices  15.2 us (46%)
  waiting for transfers between devices  10.4 us (32%)
  Pallas kernels  5.58 us (17%)
  between operations  0.78 us (2%)
  local copies, waits for them, and re-layouts  0.62 us (2%)
    ppermute x6, starting transfers between devices, shift(): return lax.ppermute(value, 'atoms', [(i, (i + by) % nz) for i in range(nz)])  11.3 us
    ppermute x6, waiting for transfers between devices, swap(): return lax.ppermute(value, 'kvec', [(i, i ^ flip) for i in range(nq)])  8 us
    pallas_call x18, Pallas kernels, call(): pl.pallas_call(body, out_shape=outs, in_specs=full_spec(len(args)), out_s...  5.58 us
    ppermute x6, starting transfers between devices, swap(): return lax.ppermute(value, 'kvec', [(i, i ^ flip) for i in range(nq)])  3.86 us
    ppermute x6, waiting for transfers between devices, shift(): return lax.ppermute(value, 'atoms', [(i, (i + by) % nz) for i in range(nz)])  2.41 us
  transfers between devices with their start and end apart: 12, of which 6 were waited for; matrix products, arithmetic and copies ran while one was open for 2% of the time, Pallas kernels for 10%

profile of v2, /device:TPU:0, one launch (start us, length us, event | category | flops | bytes accessed | tf_op | source)
XLA Modules:
  0.0 32.6 jit_solution(3608630383015921448)
XLA Ops:
  0.6 1.0 %shard_map.68 = (bf16[288,128]{1,0:T(8,128)(2,1)S(1)}, f32[8,128]{1,0:T(8,128)S(1)}) custom-call(s32[3,64]{1,0:T(4,128)} %lat_ref.1, f32[3,256]{1,0:T(4,128)} %pos_ref.1, bf16[256,128]{1,0:T(8,128)(2,1)} %cot_ref.1), custom_call_target="tpu_custom_call" | custom-call | tf_op jit(solution)/shard_map/pallas_call | solution.py:64
  1.6 3.1 %collective-permute-start.4 = (bf16[288,128]{1,0:T(8,128)(2,1)S(1)}, bf16[288,128]{1,0:T(8,128)(2,1)S(1)}, u32[]{:S(2)}, u32[]{:S(2)}) collective-permute-start(bf16[288,128]{1,0:T(8,128)(2,1)S(1)} %get-tuple-element.42.refs_0_), channel_id=1, source_target_pairs={{0,4},{4,8},{8,12},{12,0},{1,5},{5,9},{9,13},{13,1},{2,6},{6,10},{... | collective-permute-start | bytes 221192 | tf_op jit(solution)/shard_map/ppermute | solution.py:216
  4.7 2.0 %collective-permute-start.3 = (bf16[288,128]{1,0:T(8,128)(2,1)S(1)}, bf16[288,128]{1,0:T(8,128)(2,1)S(1)}, u32[]{:S(2)}, u32[]{:S(2)}) collective-permute-start(bf16[288,128]{1,0:T(8,128)(2,1)S(1)} %get-tuple-element.42.refs_0_), channel_id=1, source_target_pairs={{0,12},{4,0},{8,4},{12,8},{1,13},{5,1},{9,5},{13,9},{2,14},{6,2},{... | collective-permute-start | bytes 221192 | tf_op jit(solution)/shard_map/ppermute | solution.py:216
  6.7 1.0 %collective-permute-start = (bf16[288,128]{1,0:T(8,128)(2,1)S(1)}, bf16[288,128]{1,0:T(8,128)(2,1)S(1)}, u32[]{:S(2)}, u32[]{:S(2)}) collective-permute-start(bf16[288,128]{1,0:T(8,128)(2,1)S(1)} %get-tuple-element.42.refs_0_), channel_id=1, source_target_pairs={{0,8},{4,12},{8,0},{12,4},{1,9},{5,13},{9,1},{13,5},{2,10},{6,14},... | collective-permute-start | bytes 221192 | tf_op jit(solution)/shard_map/ppermute | solution.py:216
  7.7 1.2 %collective-permute-done.1.got_ref = f32[8,128]{1,0:T(8,128)S(1)} collective-permute-done((f32[8,128]{1,0:T(8,128)S(1)}, f32[8,128]{1,0:T(8,128)S(1)}, u32[]{:S(2)}, u32[]{:S(2)}) %collective-permute-start.1) | collective-permute-done | bytes 4128 | tf_op jit(solution)/shard_map/ppermute | solution.py:213
  8.9 1.5 %collective-permute-start.2 = (f32[16,128]{1,0:T(8,128)S(1)}, f32[16,128]{1,0:T(8,128)S(1)}, u32[]{:S(2)}, u32[]{:S(2)}) collective-permute-start(f32[16,128]{1,0:T(8,128)S(1)} %shard_map.69.refs_0_), channel_id=1, source_target_pairs={{0,2},{1,3},{2,0},{3,1},{4,6},{5,7},{6,4},{7,5},{8,10},{9,11},{10,... | collective-permute-start | bytes 24584 | tf_op jit(solution)/shard_map/ppermute | solution.py:213
  10.4 0.1 shard_map.70.refs_1_.refs_2_
  10.5 0.4 %shard_map.72 = (bf16[128,256]{1,0:T(8,128)(2,1)S(1)}, bf16[128,256]{1,0:T(8,128)(2,1)S(1)}, f32[128,128]{1,0:T(8,128)S(1)}, f32[128,128]{1,0:T(8,128)S(1)}) custom-call(bf16[288,128]{1,0:T(8,128)(2,1)S(1)} %get-tuple-element.42.refs_0_, bf16[128,16]{1,0:T(8,128)(2,1)S(1)} %shard_map.70.refs_1_.refs_2_, bf16[128,16]{1,0:T(8,128)(2,1)S(1)} %shard_map.70.refs_1_.refs_2_), custom_call_target="tpu_custom_call" | custom-call | tf_op jit(solution)/shard_map/pallas_call | solution.py:64
  10.8 1.7 %collective-permute-done.2.refs_0_ = f32[16,128]{1,0:T(8,128)S(1)} collective-permute-done((f32[16,128]{1,0:T(8,128)S(1)}, f32[16,128]{1,0:T(8,128)S(1)}, u32[]{:S(2)}, u32[]{:S(2)}) %collective-permute-start.2) | collective-permute-done | bytes 8224 | tf_op jit(solution)/shard_map/ppermute | solution.py:213
  12.5 0.1 shard_map.71.refs_2_.refs_3_.refs_4_
  12.6 0.5 %shard_map.74 = (bf16[128,256]{1,0:T(8,128)(2,1)S(1)}, bf16[128,256]{1,0:T(8,128)(2,1)S(1)}, bf16[128,256]{1,0:T(8,128)(2,1)S(1)}, bf16[128,256]{1,0:T(8,128)(2,...) custom-call(bf16[288,128]{1,0:T(8,128)(2,1)S(1)} %get-tuple-element.42.refs_0_, ...), custom_call_target="tpu_custom_call" | custom-call | tf_op jit(solution)/shard_map/pallas_call | solution.py:64
  13.1 0.4 %shard_map.73 = (bf16[128,256]{1,0:T(8,128)(2,1)S(1)}, bf16[128,256]{1,0:T(8,128)(2,1)S(1)}, f32[128,128]{1,0:T(8,128)S(1)}, f32[128,128]{1,0:T(8,128)S(1)}) custom-call(bf16[288,128]{1,0:T(8,128)(2,1)S(1)} %collective-permute-done.4.refs_0_.refs_1_, bf16[128,16]{1,0:T(8,128)(2,1)S(1)} %shard_map.70.refs_1_.refs_2_, ...), custom_call_target="tpu_custom_call" | custom-call | tf_op jit(solution)/shard_map/pallas_call | solution.py:64
  13.5 0.5 %shard_map.75 = (bf16[128,256]{1,0:T(8,128)(2,1)S(1)}, bf16[128,256]{1,0:T(8,128)(2,1)S(1)}, bf16[128,256]{1,0:T(8,128)(2,1)S(1)}, bf16[128,256]{1,0:T(8,128)(2,...) custom-call(bf16[288,128]{1,0:T(8,128)(2,1)S(1)} %collective-permute-, ...), custom_call_target="tpu_custom_call" | custom-call | tf_op jit(solution)/shard_map/pallas_call | solution.py:64
  14.0 0.4 %shard_map.77 = (bf16[128,256]{1,0:T(8,128)(2,1)S(1)}, bf16[128,256]{1,0:T(8,128)(2,1)S(1)}, bf16[256,128]{1,0:T(8,128)(2,1)S(1)}) custom-call(bf16[288,128]{1,0:T(8,128)(2,1)S(1)} %collective-permute-done.refs_0_, bf16[128,16]{1,0:T(8,128)(2,1)S(1)} %shard_map.70.refs_1_.refs_2_, bf16[128,16]{1,0:T(8,128)(2,1)S(1)} %shard_map.71.refs_2_.refs_3_.refs_4_, ...), custom_call_target="tpu_custom_call" | custom-call | tf_op jit(solution)/shard_map/pallas_call | solution.py:64
  14.5 0.4 %shard_map.76 = (bf16[128,256]{1,0:T(8,128)(2,1)S(1)}, bf16[128,256]{1,0:T(8,128)(2,1)S(1)}, f32[256,128]{1,0:T(8,128)S(1)}) custom-call(bf16[288,128]{1,0:T(8,128)(2,1)S(1)} %collective-permute-done.refs_0_, bf16[128,16]{1,0:T(8,128)(2,1)S(1)} %shard_map.70.refs_1_.refs_2_, bf16[128,16]{1,0:T(8,128)(2,1)S(1)} %shard_map.71.refs_2_.refs_3_.refs_4_, ...), custom_call_target="tpu_custom_call" | custom-call | tf_op jit(solution)/shard_map/pallas_call | solution.py:64
  14.8 0.9 %collective-permute-done.5.got_ref = bf16[256,128]{1,0:T(8,128)(2,1)S(1)} collective-permute-done((bf16[256,128]{1,0:T(8,128)(2,1)S(1)}, bf16[256,128]{1,0:T(8,128)(2,1)S(1)}, u32[]{:S(2)}, u32[]{:S(2)}) %collective-permute-start.5) | collective-permute-done | bytes 65568 | tf_op jit(solution)/shard_map/ppermute | solution.py:213
  15.7 1.6 %collective-permute-start.6 = (bf16[256,128]{1,0:T(8,128)(2,1)S(1)}, bf16[256,128]{1,0:T(8,128)(2,1)S(1)}, u32[]{:S(2)}, u32[]{:S(2)}) collective-permute-start(bf16[256,128]{1,0:T(8,128)(2,1)S(1)} %get-tuple-element.57), channel_id=1, source_target_pairs={{0,2},{1,3},{2,0},{3,1},{4,6},{5,7},{6,4},{7,5},{8,10},{9,11},{10,... | collective-permute-start | bytes 196616 | tf_op jit(solution)/shard_map/ppermute | solution.py:213
  17.3 0.7 %collective-permute-start.7 = (f32[64,128]{1,0:T(8,128)S(1)}, f32[64,128]{1,0:T(8,128)S(1)}, u32[]{:S(2)}, u32[]{:S(2)}) collective-permute-start(f32[64,128]{1,0:T(8,128)S(1)} %copy-done.1), channel_id=1, source_target_pairs={{0,2},{1,3},{2,0},{3,1},{4,6},{5,7},{6,4},{7,5},{8,10},{9,11},{10,... | collective-permute-start | bytes 98312 | tf_op jit(solution)/shard_map/ppermute | solution.py:213
  17.9 3.2 %collective-permute-done.7.refs_3_ = f32[64,128]{1,0:T(8,128)S(1)} collective-permute-done((f32[64,128]{1,0:T(8,128)S(1)}, f32[64,128]{1,0:T(8,128)S(1)}, u32[]{:S(2)}, u32[]{:S(2)}) %collective-permute-start.7) | collective-permute-done | bytes 32800 | tf_op jit(solution)/shard_map/ppermute | solution.py:213
  21.2 0.1 shard_map.79
  21.4 0.2 shard_map.80
  21.6 1.0 %collective-permute-done.8.refs_3_.refs_1_ = bf16[128,256]{1,0:T(8,128)(2,1)S(1)} collective-permute-done((bf16[128,256]{1,0:T(8,128)(2,1)S(1)}, bf16[128,256]{1,0:T(8,128)(2,1)S(1)}, u32[]{:S(2)}, u32[]{:S(2)}) %collective-permute-start.8) | collective-permute-done | bytes 65568 | tf_op jit(solution)/shard_map/ppermute | solution.py:213
  22.6 0.2 shard_map.82
  22.9 1.6 %collective-permute-start.9 = (bf16[256,128]{1,0:T(8,128)(2,1)S(1)}, bf16[256,128]{1,0:T(8,128)(2,1)S(1)}, u32[]{:S(2)}, u32[]{:S(2)}) collective-permute-start(bf16[256,128]{1,0:T(8,128)(2,1)S(1)} %shard_map.82), channel_id=1, source_target_pairs={{0,4},{4,8},{8,12},{12,0},{1,5},{5,9},{9,13},{13,1},{2,6},{6,10},{... | collective-permute-start | bytes 196616 | tf_op jit(solution)/shard_map/ppermute | solution.py:216
  24.5 0.2 shard_map.83
  24.8 0.7 %collective-permute-start.10 = (bf16[256,128]{1,0:T(8,128)(2,1)S(1)}, bf16[256,128]{1,0:T(8,128)(2,1)S(1)}, u32[]{:S(2)}, u32[]{:S(2)}) collective-permute-start(bf16[256,128]{1,0:T(8,128)(2,1)S(1)} %shard_map.83), channel_id=1, source_target_pairs={{0,8},{4,12},{8,0},{12,4},{1,9},{5,13},{9,1},{13,5},{2,10},{6,14},... | collective-permute-start | bytes 196616 | tf_op jit(solution)/shard_map/ppermute | solution.py:216
  25.5 0.2 shard_map.84
  25.8 2.9 %collective-permute-start.11 = (bf16[256,128]{1,0:T(8,128)(2,1)S(1)}, bf16[256,128]{1,0:T(8,128)(2,1)S(1)}, u32[]{:S(2)}, u32[]{:S(2)}) collective-permute-start(bf16[256,128]{1,0:T(8,128)(2,1)S(1)} %shard_map.84), channel_id=1, source_target_pairs={{0,12},{4,0},{8,4},{12,8},{1,13},{5,1},{9,5},{13,9},{2,14},{6,2},{... | collective-permute-start | bytes 196616 | tf_op jit(solution)/shard_map/ppermute | solution.py:216
  28.6 0.2 shard_map.81
  28.9 0.6 %copy.7 = f32[64,128]{1,0:T(8,128)} copy(f32[64,128]{1,0:T(8,128)S(1)} %get-tuple-element.83) | data formatting | bytes 65536
  29.5 2.4 %collective-permute-done.10.refs_2_ = bf16[256,128]{1,0:T(8,128)(2,1)S(1)} collective-permute-done((bf16[256,128]{1,0:T(8,128)(2,1)S(1)}, bf16[256,128]{1,0:T(8,128)(2,1)S(1)}, u32[]{:S(2)}, u32[]{:S(2)}) %collective-permute-start.10) | collective-permute-done | bytes 65568 | tf_op jit(solution)/shard_map/ppermute | solution.py:216
  31.9 0.7 %shard_map.85 = bf16[256,128]{1,0:T(8,128)(2,1)} custom-call(f32[256,128]{1,0:T(8,128)S(1)} %get-tuple-element.71.refs_0_, bf16[256,128]{1,0:T(8,128)(2,1)S(1)} %collective-permute-done.9.refs_1_, bf16[256,128]{1,0:T(8,128)(2,1)S(1)} %collective-permute-done.10.refs_2_, bf16[256,128]{1,0:T(8,128)(2,1)S(1)} %collective-permute-done.11.refs_3_), custom_call_target="tpu_custom_call" | custom-call | tf_op jit(solution)/shard_map/pallas_call | solution.py:64
  (15 shorter events, 0.2 us)
Async XLA Ops:
  1.6 11.0 %collective-permute-start.4 = (bf16[288,128]{1,0:T(8,128)(2,1)S(1)}, bf16[288,128]{1,0:T(8,128)(2,1)S(1)}, u32[]{:S(2)}, u32[]{:S(2)}) collective-permute-start(bf16[288,128]{1,0:T(8,128)(2,1)S(1)} %get-tuple-element.42.refs_0_), channel_id=1, source_target_pairs={{0,4},{4,8},{8,12},{12,0},{1,5},{5,9},{9,13},{13,1},{2,6},{6,10},{... | collective-permute-start | bytes 221192 | tf_op jit(solution)/shard_map/ppermute | solution.py:216
  4.7 8.8 %collective-permute-start.3 = (bf16[288,128]{1,0:T(8,128)(2,1)S(1)}, bf16[288,128]{1,0:T(8,128)(2,1)S(1)}, u32[]{:S(2)}, u32[]{:S(2)}) collective-permute-start(bf16[288,128]{1,0:T(8,128)(2,1)S(1)} %get-tuple-element.42.refs_0_), channel_id=1, source_target_pairs={{0,12},{4,0},{8,4},{12,8},{1,13},{5,1},{9,5},{13,9},{2,14},{6,2},{... | collective-permute-start | bytes 221192 | tf_op jit(solution)/shard_map/ppermute | solution.py:216
  6.7 7.3 %collective-permute-start = (bf16[288,128]{1,0:T(8,128)(2,1)S(1)}, bf16[288,128]{1,0:T(8,128)(2,1)S(1)}, u32[]{:S(2)}, u32[]{:S(2)}) collective-permute-start(bf16[288,128]{1,0:T(8,128)(2,1)S(1)} %get-tuple-element.42.refs_0_), channel_id=1, source_target_pairs={{0,8},{4,12},{8,0},{12,4},{1,9},{5,13},{9,1},{13,5},{2,10},{6,14},... | collective-permute-start | bytes 221192 | tf_op jit(solution)/shard_map/ppermute | solution.py:216
  7.7 1.2 %collective-permute-start.1 = (f32[8,128]{1,0:T(8,128)S(1)}, f32[8,128]{1,0:T(8,128)S(1)}, u32[]{:S(2)}, u32[]{:S(2)}) collective-permute-start(f32[8,128]{1,0:T(8,128)S(1)} %get-tuple-element.43.own_ref), channel_id=1, source_target_pairs={{0,1},{1,0},{2,3},{3,2},{4,5},{5,4},{6,7},{7,6},{8,9},{9,8},{10,11... | collective-permute-start | bytes 12296 | tf_op jit(solution)/shard_map/ppermute | solution.py:213
  8.9 3.7 %collective-permute-start.2 = (f32[16,128]{1,0:T(8,128)S(1)}, f32[16,128]{1,0:T(8,128)S(1)}, u32[]{:S(2)}, u32[]{:S(2)}) collective-permute-start(f32[16,128]{1,0:T(8,128)S(1)} %shard_map.69.refs_0_), channel_id=1, source_target_pairs={{0,2},{1,3},{2,0},{3,1},{4,6},{5,7},{6,4},{7,5},{8,10},{9,11},{10,... | collective-permute-start | bytes 24584 | tf_op jit(solution)/shard_map/ppermute | solution.py:213
  14.4 1.3 %collective-permute-start.5 = (bf16[256,128]{1,0:T(8,128)(2,1)S(1)}, bf16[256,128]{1,0:T(8,128)(2,1)S(1)}, u32[]{:S(2)}, u32[]{:S(2)}) collective-permute-start(bf16[256,128]{1,0:T(8,128)(2,1)S(1)} %get-tuple-element.55), channel_id=1, source_target_pairs={{0,1},{1,0},{2,3},{3,2},{4,5},{5,4},{6,7},{7,6},{8,9},{9,8},{10,11... | collective-permute-start | bytes 196616 | tf_op jit(solution)/shard_map/ppermute | solution.py:213
  15.7 1.6 %copy-start.1 = (f32[64,128]{1,0:T(8,128)S(1)}, f32[64,128]{1,0:T(8,128)}, u32[]{:S(2)}) copy-start(f32[64,128]{1,0:T(8,128)} %refs_2_.1) | copy-start | bytes 98308
  15.7 5.5 %collective-permute-start.6 = (bf16[256,128]{1,0:T(8,128)(2,1)S(1)}, bf16[256,128]{1,0:T(8,128)(2,1)S(1)}, u32[]{:S(2)}, u32[]{:S(2)}) collective-permute-start(bf16[256,128]{1,0:T(8,128)(2,1)S(1)} %get-tuple-element.57), channel_id=1, source_target_pairs={{0,2},{1,3},{2,0},{3,1},{4,6},{5,7},{6,4},{7,5},{8,10},{9,11},{10,... | collective-permute-start | bytes 196616 | tf_op jit(solution)/shard_map/ppermute | solution.py:213
  17.3 3.9 %collective-permute-start.7 = (f32[64,128]{1,0:T(8,128)S(1)}, f32[64,128]{1,0:T(8,128)S(1)}, u32[]{:S(2)}, u32[]{:S(2)}) collective-permute-start(f32[64,128]{1,0:T(8,128)S(1)} %copy-done.1), channel_id=1, source_target_pairs={{0,2},{1,3},{2,0},{3,1},{4,6},{5,7},{6,4},{7,5},{8,10},{9,11},{10,... | collective-permute-start | bytes 98312 | tf_op jit(solution)/shard_map/ppermute | solution.py:213
  21.3 1.3 %collective-permute-start.8 = (bf16[128,256]{1,0:T(8,128)(2,1)S(1)}, bf16[128,256]{1,0:T(8,128)(2,1)S(1)}, u32[]{:S(2)}, u32[]{:S(2)}) collective-permute-start(bf16[128,256]{1,0:T(8,128)(2,1)S(1)} %get-tuple-element.59.refs_0_), channel_id=1, source_target_pairs={{0,1},{1,0},{2,3},{3,2},{4,5},{5,4},{6,7},{7,6},{8,9},{9,8},{10,11... | collective-permute-start | bytes 196616 | tf_op jit(solution)/shard_map/ppermute | solution.py:213
  22.9 6.6 %collective-permute-start.9 = (bf16[256,128]{1,0:T(8,128)(2,1)S(1)}, bf16[256,128]{1,0:T(8,128)(2,1)S(1)}, u32[]{:S(2)}, u32[]{:S(2)}) collective-permute-start(bf16[256,128]{1,0:T(8,128)(2,1)S(1)} %shard_map.82), channel_id=1, source_target_pairs={{0,4},{4,8},{8,12},{12,0},{1,5},{5,9},{9,13},{13,1},{2,6},{6,10},{... | collective-permute-start | bytes 196616 | tf_op jit(solution)/shard_map/ppermute | solution.py:216
  24.8 7.1 %collective-permute-start.10 = (bf16[256,128]{1,0:T(8,128)(2,1)S(1)}, bf16[256,128]{1,0:T(8,128)(2,1)S(1)}, u32[]{:S(2)}, u32[]{:S(2)}) collective-permute-start(bf16[256,128]{1,0:T(8,128)(2,1)S(1)} %shard_map.83), channel_id=1, source_target_pairs={{0,8},{4,12},{8,0},{12,4},{1,9},{5,13},{9,1},{13,5},{2,10},{6,14},... | collective-permute-start | bytes 196616 | tf_op jit(solution)/shard_map/ppermute | solution.py:216
  25.5 3.1 %copy-start = (f32[2,64,128]{2,1,0:T(8,128)S(1)}, f32[2,64,128]{2,1,0:T(8,128)}, u32[]{:S(2)}) copy-start(f32[2,64,128]{2,1,0:T(8,128)} %refs_1_.1) | copy-start | bytes 196612
  25.8 6.2 %collective-permute-start.11 = (bf16[256,128]{1,0:T(8,128)(2,1)S(1)}, bf16[256,128]{1,0:T(8,128)(2,1)S(1)}, u32[]{:S(2)}, u32[]{:S(2)}) collective-permute-start(bf16[256,128]{1,0:T(8,128)(2,1)S(1)} %shard_map.84), channel_id=1, source_target_pairs={{0,12},{4,0},{8,4},{12,8},{1,13},{5,1},{9,5},{13,9},{2,14},{6,2},{... | collective-permute-start | bytes 196616 | tf_op jit(solution)/shard_map/ppermute | solution.py:216

commit v3 on v2

--- a/solution.py
+++ b/solution.py
@@ -69,10 +69,18 @@
     )(*args)
 
 
-def pack_body(lat_ref, pos_ref, cot_ref, out_ref, wide_ref):
-    natom, width = cot_ref.shape
+def pack_body(lat_hbm, pos_hbm, cot_hbm, fil_hbm, out_ref, wide_ref, fil_ref, lat_ref, pos_ref, sem):
+    natom, width = cot_hbm.shape
     nk = lat_ref.shape[1]
-    out_ref[0:natom, :] = cot_ref[...]
+    copies = [
+        pltpu.make_async_copy(pos_hbm, pos_ref, sem.at[0]),
+        pltpu.make_async_copy(lat_hbm, lat_ref, sem.at[1]),
+        pltpu.make_async_copy(cot_hbm, out_ref.at[pl.ds(0, natom)], sem.at[2]),
+        pltpu.make_async_copy(fil_hbm, fil_ref, sem.at[3]),
+    ]
+    for copy in copies:
+        copy.start()
+    copies[0].wait()
     x = pos_ref[...]
     hi = x.astype(bf16).astype(f32)
     rest = x - hi
@@ -82,12 +90,33 @@
     parts = jnp.concatenate([hi, mid, low, zero, zero, zero[:1]], 0).astype(bf16)
     for j in range(natom // width):
         out_ref[natom + 16 * j : natom + 16 * (j + 1), :] = parts[:, j * width : (j + 1) * width]
+    copies[1].wait()
     row = lax.broadcasted_iota(jnp.int32, (nk, width), 0)
     col = lax.broadcasted_iota(jnp.int32, (nk, width), 1)
     spread = (row == col % nk).astype(bf16)
     lat = lat_ref[...].astype(f32).astype(bf16)
     wide = jnp.dot(lat, spread, preferred_element_type=f32)
     wide_ref[...] = jnp.concatenate([wide, wide, wide[:2]], 0)
+    copies[2].wait()
+    copies[3].wait()
+
+
+def pack(keep, lattice, positions, cotangent, filters):
+    natom, width = cotangent.shape
+    outs = [shape((natom + 16 * (natom // width), width), bf16), shape((8, width), f32), shape(filters.shape, f32)]
+    if keep:
+        outs = [pltpu.VMEM(v.shape, v.dtype) for v in outs]
+    return pl.pallas_call(
+        pack_body,
+        out_shape=outs,
+        in_specs=[pl.BlockSpec(memory_space=pl.ANY)] * 4,
+        out_specs=full_spec(3),
+        scratch_shapes=[
+            pltpu.VMEM(lattice.shape, lattice.dtype),
+            pltpu.VMEM(positions.shape, positions.dtype),
+            pltpu.SemaphoreType.DMA((4,)),
+        ],
+    )(lattice, positions, cotangent, filters)
 
 
 def join_body(own_ref, got_ref, out_ref):
@@ -218,14 +247,7 @@
     def run(body, outs, *args, keep_args=keep, keep_outs=keep):
         return call(body, outs, *args, keep_args=keep_args, keep_outs=keep_outs)
 
-    zbuf, wide = run(
-        pack_body,
-        [shape((natom + 16 * (natom // width), width), bf16), shape((8, width), f32)],
-        lattice,
-        positions,
-        cotangent,
-        keep_args=False,
-    )
+    zbuf, wide, filters = pack(keep, lattice, positions, cotangent, filters)
     ring = gather_order(nz)
     flips = list(range(2, nq, 2))
     zb = {0: zbuf}
@@ -260,7 +282,7 @@
         return got[-1]
 
     order = [0] + ring
-    early = order[: min(2, len(order) - 1)]
+    early = order[: min(3, len(order) - 1)]
     for z in early:
         factor([z], [0, 1])
     for t in flips:
@@ -270,10 +292,7 @@
     sent = factor(order[-1:], theirs, bf16)
     kept = factor(order[-1:], mine, f32)
     pair, pair16 = run(
-        pair_body,
-        [shape((2 * count, width), f32), shape((2 * count, width), bf16)],
-        kept,
-        swap(sent, 1),
+        pair_body, [shape((2 * count, width), f32), shape((2 * count, width), bf16)], kept, swap(sent, 1)
     )
     got = [swap(pair16, s) for s in flips]
     weight, head = run(
@@ -311,11 +330,7 @@
         *[tiles[0, t] for t in theirs],
     )
     (node_grad,) = run(
-        lambda *refs: final_body(scale_k, *refs),
-        [shape((natom, width), bf16)],
-        own,
-        *landed,
-        keep_outs=False,
+        lambda *refs: final_body(scale_k, *refs), [shape((natom, width), bf16)], own, *landed, keep_outs=False
     )
     return (node_grad, filter_grad)
 

time: 32.8 us -> 32.8 us (level)
    pallas_call x18 -> x17, Pallas kernels: 5.58 us -> 4.64 us  [call(): pl.pallas_call(body, out_shape=outs, in_specs=full_spec(len(args)), out_s...]
    pallas_call x0 -> x1, Pallas kernels: none -> 0.91 us  [pack(): pl.pallas_call(pack_body, out_shape=outs, in_specs=[pl.BlockSpec(memory_s...]
where the time goes in v3:
time: 32.8 us; the launch traced here: 32.6 us
  starting transfers between devices  15.1 us (46%)
  waiting for transfers between devices  10.5 us (32%)
  Pallas kernels  5.55 us (17%)
  between operations  0.78 us (2%)
  local copies, waits for them, and re-layouts  0.62 us (2%)
    ppermute x6, starting transfers between devices, shift(): return lax.ppermute(value, 'atoms', [(i, (i + by) % nz) for i in range(nz)])  11.4 us
    ppermute x6, waiting for transfers between devices, swap(): return lax.ppermute(value, 'kvec', [(i, i ^ flip) for i in range(nq)])  8.13 us
    pallas_call x17, Pallas kernels, call(): pl.pallas_call(body, out_shape=outs, in_specs=full_spec(len(args)), out_s...  4.64 us
    ppermute x6, starting transfers between devices, swap(): return lax.ppermute(value, 'kvec', [(i, i ^ flip) for i in range(nq)])  3.73 us
    ppermute x6, waiting for transfers between devices, shift(): return lax.ppermute(value, 'atoms', [(i, (i + by) % nz) for i in range(nz)])  2.41 us
    pallas_call x1, Pallas kernels, pack(): pl.pallas_call(pack_body, out_shape=outs, in_specs=[pl.BlockSpec(memory_s...  0.91 us
  transfers between devices with their start and end apart: 12, of which 6 were waited for; matrix products, arithmetic and copies ran while one was open for 2% of the time, Pallas kernels for 10%

profile of v3, /device:TPU:0, one launch (start us, length us, event | category | flops | bytes accessed | tf_op | source)
XLA Modules:
  0.0 32.6 jit_solution(15768437088340042295)
XLA Ops:
  0.6 0.9 %shard_map.68 = (bf16[288,128]{1,0:T(8,128)(2,1)S(1)}, f32[8,128]{1,0:T(8,128)S(1)}, f32[64,128]{1,0:T(8,128)S(1)}) custom-call(s32[3,64]{1,0:T(4,128)} %lat_hbm.1, f32[3,256]{1,0:T(4,128)} %pos_hbm.1, bf16[256,128]{1,0:T(8,128)(2,1)} %cot_hbm.1, f32[64,128]{1,0:T(8,128)} %fil_hbm.1), custom_call_target="tpu_custom_call" | custom-call | tf_op jit(solution)/shard_map/pallas_call | solution.py:109
  1.5 3.1 %collective-permute-start.4 = (bf16[288,128]{1,0:T(8,128)(2,1)S(1)}, bf16[288,128]{1,0:T(8,128)(2,1)S(1)}, u32[]{:S(2)}, u32[]{:S(2)}) collective-permute-start(bf16[288,128]{1,0:T(8,128)(2,1)S(1)} %get-tuple-element.41.refs_0_), channel_id=1, source_target_pairs={{0,4},{4,8},{8,12},{12,0},{1,5},{5,9},{9,13},{13,1},{2,6},{6,10},{... | collective-permute-start | bytes 221192 | tf_op jit(solution)/shard_map/ppermute | solution.py:245
  4.7 2.1 %collective-permute-start.3 = (bf16[288,128]{1,0:T(8,128)(2,1)S(1)}, bf16[288,128]{1,0:T(8,128)(2,1)S(1)}, u32[]{:S(2)}, u32[]{:S(2)}) collective-permute-start(bf16[288,128]{1,0:T(8,128)(2,1)S(1)} %get-tuple-element.41.refs_0_), channel_id=1, source_target_pairs={{0,12},{4,0},{8,4},{12,8},{1,13},{5,1},{9,5},{13,9},{2,14},{6,2},{... | collective-permute-start | bytes 221192 | tf_op jit(solution)/shard_map/ppermute | solution.py:245
  6.7 0.9 %collective-permute-start = (bf16[288,128]{1,0:T(8,128)(2,1)S(1)}, bf16[288,128]{1,0:T(8,128)(2,1)S(1)}, u32[]{:S(2)}, u32[]{:S(2)}) collective-permute-start(bf16[288,128]{1,0:T(8,128)(2,1)S(1)} %get-tuple-element.41.refs_0_), channel_id=1, source_target_pairs={{0,8},{4,12},{8,0},{12,4},{1,9},{5,13},{9,1},{13,5},{2,10},{6,14},... | collective-permute-start | bytes 221192 | tf_op jit(solution)/shard_map/ppermute | solution.py:245
  7.7 1.2 %collective-permute-done.1.got_ref = f32[8,128]{1,0:T(8,128)S(1)} collective-permute-done((f32[8,128]{1,0:T(8,128)S(1)}, f32[8,128]{1,0:T(8,128)S(1)}, u32[]{:S(2)}, u32[]{:S(2)}) %collective-permute-start.1) | collective-permute-done | bytes 4128 | tf_op jit(solution)/shard_map/ppermute | solution.py:242
  8.9 1.5 %collective-permute-start.2 = (f32[16,128]{1,0:T(8,128)S(1)}, f32[16,128]{1,0:T(8,128)S(1)}, u32[]{:S(2)}, u32[]{:S(2)}) collective-permute-start(f32[16,128]{1,0:T(8,128)S(1)} %shard_map.69.refs_0_), channel_id=1, source_target_pairs={{0,2},{1,3},{2,0},{3,1},{4,6},{5,7},{6,4},{7,5},{8,10},{9,11},{10,... | collective-permute-start | bytes 24584 | tf_op jit(solution)/shard_map/ppermute | solution.py:242
  10.4 0.1 shard_map.70.refs_1_.refs_2_
  10.4 0.4 %shard_map.72 = (bf16[128,256]{1,0:T(8,128)(2,1)S(1)}, bf16[128,256]{1,0:T(8,128)(2,1)S(1)}, f32[128,128]{1,0:T(8,128)S(1)}, f32[128,128]{1,0:T(8,128)S(1)}) custom-call(bf16[288,128]{1,0:T(8,128)(2,1)S(1)} %get-tuple-element.41.refs_0_, bf16[128,16]{1,0:T(8,128)(2,1)S(1)} %shard_map.70.refs_1_.refs_2_, bf16[128,16]{1,0:T(8,128)(2,1)S(1)} %shard_map.70.refs_1_.refs_2_), custom_call_target="tpu_custom_call" | custom-call | tf_op jit(solution)/shard_map/pallas_call | solution.py:64
  10.8 1.7 %collective-permute-done.2.refs_0_ = f32[16,128]{1,0:T(8,128)S(1)} collective-permute-done((f32[16,128]{1,0:T(8,128)S(1)}, f32[16,128]{1,0:T(8,128)S(1)}, u32[]{:S(2)}, u32[]{:S(2)}) %collective-permute-start.2) | collective-permute-done | bytes 8224 | tf_op jit(solution)/shard_map/ppermute | solution.py:242
  12.5 0.1 shard_map.71.refs_3_.refs_4_.refs_2_
  12.6 0.4 %shard_map.73 = (bf16[128,256]{1,0:T(8,128)(2,1)S(1)}, bf16[128,256]{1,0:T(8,128)(2,1)S(1)}, f32[128,128]{1,0:T(8,128)S(1)}, f32[128,128]{1,0:T(8,128)S(1)}) custom-call(bf16[288,128]{1,0:T(8,128)(2,1)S(1)} %collective-permute-done.4.refs_0_.refs_2_, bf16[128,16]{1,0:T(8,128)(2,1)S(1)} %shard_map.70.refs_1_.refs_2_, ...), custom_call_target="tpu_custom_call" | custom-call | tf_op jit(solution)/shard_map/pallas_call | solution.py:64
  13.0 0.7 %shard_map.75 = (bf16[128,256]{1,0:T(8,128)(2,1)S(1)}, bf16[128,256]{1,0:T(8,128)(2,1)S(1)}, bf16[128,256]{1,0:T(8,128)(2,1)S(1)}, bf16[128,256]{1,0:T(8,128)(2,...) custom-call(bf16[288,128]{1,0:T(8,128)(2,1)S(1)} %get-tuple-element., ...), custom_call_target="tpu_custom_call" | custom-call | tf_op jit(solution)/shard_map/pallas_call | solution.py:64
  13.7 0.4 %shard_map.74 = (bf16[128,256]{1,0:T(8,128)(2,1)S(1)}, bf16[128,256]{1,0:T(8,128)(2,1)S(1)}, f32[128,128]{1,0:T(8,128)S(1)}, f32[128,128]{1,0:T(8,128)S(1)}) custom-call(bf16[288,128]{1,0:T(8,128)(2,1)S(1)} %collective-permute-done.3.refs_0_.refs_1_, bf16[128,16]{1,0:T(8,128)(2,1)S(1)} %shard_map.70.refs_1_.refs_2_, ...), custom_call_target="tpu_custom_call" | custom-call | tf_op jit(solution)/shard_map/pallas_call | solution.py:64
  14.0 0.4 %shard_map.77 = (bf16[128,256]{1,0:T(8,128)(2,1)S(1)}, bf16[128,256]{1,0:T(8,128)(2,1)S(1)}, bf16[256,128]{1,0:T(8,128)(2,1)S(1)}) custom-call(bf16[288,128]{1,0:T(8,128)(2,1)S(1)} %collective-permute-done.refs_0_, bf16[128,16]{1,0:T(8,128)(2,1)S(1)} %shard_map.70.refs_1_.refs_2_, bf16[128,16]{1,0:T(8,128)(2,1)S(1)} %shard_map.71.refs_3_.refs_4_.refs_2_, ...), custom_call_target="tpu_custom_call" | custom-call | tf_op jit(solution)/shard_map/pallas_call | solution.py:64
  14.5 0.4 %shard_map.76 = (bf16[128,256]{1,0:T(8,128)(2,1)S(1)}, bf16[128,256]{1,0:T(8,128)(2,1)S(1)}, f32[256,128]{1,0:T(8,128)S(1)}) custom-call(bf16[288,128]{1,0:T(8,128)(2,1)S(1)} %collective-permute-done.refs_0_, bf16[128,16]{1,0:T(8,128)(2,1)S(1)} %shard_map.70.refs_1_.refs_2_, bf16[128,16]{1,0:T(8,128)(2,1)S(1)} %shard_map.71.refs_3_.refs_4_.refs_2_, ...), custom_call_target="tpu_custom_call" | custom-call | tf_op jit(solution)/shard_map/pallas_call | solution.py:64
  14.8 0.9 %collective-permute-done.5.got_ref = bf16[256,128]{1,0:T(8,128)(2,1)S(1)} collective-permute-done((bf16[256,128]{1,0:T(8,128)(2,1)S(1)}, bf16[256,128]{1,0:T(8,128)(2,1)S(1)}, u32[]{:S(2)}, u32[]{:S(2)}) %collective-permute-start.5) | collective-permute-done | bytes 65568 | tf_op jit(solution)/shard_map/ppermute | solution.py:242
  15.8 1.6 %collective-permute-start.6 = (bf16[256,128]{1,0:T(8,128)(2,1)S(1)}, bf16[256,128]{1,0:T(8,128)(2,1)S(1)}, u32[]{:S(2)}, u32[]{:S(2)}) collective-permute-start(bf16[256,128]{1,0:T(8,128)(2,1)S(1)} %get-tuple-element.54), channel_id=1, source_target_pairs={{0,2},{1,3},{2,0},{3,1},{4,6},{5,7},{6,4},{7,5},{8,10},{9,11},{10,... | collective-permute-start | bytes 196616 | tf_op jit(solution)/shard_map/ppermute | solution.py:242
  17.3 0.5 %collective-permute-start.7 = (f32[64,128]{1,0:T(8,128)S(1)}, f32[64,128]{1,0:T(8,128)S(1)}, u32[]{:S(2)}, u32[]{:S(2)}) collective-permute-start(f32[64,128]{1,0:T(8,128)S(1)} %get-tuple-element.55.refs_2_), channel_id=1, source_target_pairs={{0,2},{1,3},{2,0},{3,1},{4,6},{5,7},{6,4},{7,5},{8,10},{9,11},{10,... | collective-permute-start | bytes 98312 | tf_op jit(solution)/shard_map/ppermute | solution.py:242
  17.8 3.4 %collective-permute-done.7.refs_3_ = f32[64,128]{1,0:T(8,128)S(1)} collective-permute-done((f32[64,128]{1,0:T(8,128)S(1)}, f32[64,128]{1,0:T(8,128)S(1)}, u32[]{:S(2)}, u32[]{:S(2)}) %collective-permute-start.7) | collective-permute-done | bytes 32800 | tf_op jit(solution)/shard_map/ppermute | solution.py:242
  21.2 0.1 shard_map.79
  21.4 0.2 shard_map.80
  21.7 1.0 %collective-permute-done.8.refs_3_.refs_1_ = bf16[128,256]{1,0:T(8,128)(2,1)S(1)} collective-permute-done((bf16[128,256]{1,0:T(8,128)(2,1)S(1)}, bf16[128,256]{1,0:T(8,128)(2,1)S(1)}, u32[]{:S(2)}, u32[]{:S(2)}) %collective-permute-start.8) | collective-permute-done | bytes 65568 | tf_op jit(solution)/shard_map/ppermute | solution.py:242
  22.7 0.2 shard_map.82
  22.9 1.6 %collective-permute-start.9 = (bf16[256,128]{1,0:T(8,128)(2,1)S(1)}, bf16[256,128]{1,0:T(8,128)(2,1)S(1)}, u32[]{:S(2)}, u32[]{:S(2)}) collective-permute-start(bf16[256,128]{1,0:T(8,128)(2,1)S(1)} %shard_map.82), channel_id=1, source_target_pairs={{0,4},{4,8},{8,12},{12,0},{1,5},{5,9},{9,13},{13,1},{2,6},{6,10},{... | collective-permute-start | bytes 196616 | tf_op jit(solution)/shard_map/ppermute | solution.py:245
  24.5 0.2 shard_map.83
  24.8 0.7 %collective-permute-start.10 = (bf16[256,128]{1,0:T(8,128)(2,1)S(1)}, bf16[256,128]{1,0:T(8,128)(2,1)S(1)}, u32[]{:S(2)}, u32[]{:S(2)}) collective-permute-start(bf16[256,128]{1,0:T(8,128)(2,1)S(1)} %shard_map.83), channel_id=1, source_target_pairs={{0,8},{4,12},{8,0},{12,4},{1,9},{5,13},{9,1},{13,5},{2,10},{6,14},... | collective-permute-start | bytes 196616 | tf_op jit(solution)/shard_map/ppermute | solution.py:245
  25.5 0.2 shard_map.84
  25.8 2.9 %collective-permute-start.11 = (bf16[256,128]{1,0:T(8,128)(2,1)S(1)}, bf16[256,128]{1,0:T(8,128)(2,1)S(1)}, u32[]{:S(2)}, u32[]{:S(2)}) collective-permute-start(bf16[256,128]{1,0:T(8,128)(2,1)S(1)} %shard_map.84), channel_id=1, source_target_pairs={{0,12},{4,0},{8,4},{12,8},{1,13},{5,1},{9,5},{13,9},{2,14},{6,2},{... | collective-permute-start | bytes 196616 | tf_op jit(solution)/shard_map/ppermute | solution.py:245
  28.7 0.2 shard_map.81
  28.9 0.6 %copy.7 = f32[64,128]{1,0:T(8,128)} copy(f32[64,128]{1,0:T(8,128)S(1)} %get-tuple-element.81) | data formatting | bytes 65536
  29.5 2.4 %collective-permute-done.10.refs_2_ = bf16[256,128]{1,0:T(8,128)(2,1)S(1)} collective-permute-done((bf16[256,128]{1,0:T(8,128)(2,1)S(1)}, bf16[256,128]{1,0:T(8,128)(2,1)S(1)}, u32[]{:S(2)}, u32[]{:S(2)}) %collective-permute-start.10) | collective-permute-done | bytes 65568 | tf_op jit(solution)/shard_map/ppermute | solution.py:245
  31.9 0.7 %shard_map.85 = bf16[256,128]{1,0:T(8,128)(2,1)} custom-call(f32[256,128]{1,0:T(8,128)S(1)} %get-tuple-element.69.refs_0_, bf16[256,128]{1,0:T(8,128)(2,1)S(1)} %collective-permute-done.9.refs_1_, bf16[256,128]{1,0:T(8,128)(2,1)S(1)} %collective-permute-done.10.refs_2_, bf16[256,128]{1,0:T(8,128)(2,1)S(1)} %collective-permute-done.11.refs_3_), custom_call_target="tpu_custom_call" | custom-call | tf_op jit(solution)/shard_map/pallas_call | solution.py:64
  (13 shorter events, 0.2 us)
Async XLA Ops:
  1.5 11.1 %collective-permute-start.4 = (bf16[288,128]{1,0:T(8,128)(2,1)S(1)}, bf16[288,128]{1,0:T(8,128)(2,1)S(1)}, u32[]{:S(2)}, u32[]{:S(2)}) collective-permute-start(bf16[288,128]{1,0:T(8,128)(2,1)S(1)} %get-tuple-element.41.refs_0_), channel_id=1, source_target_pairs={{0,4},{4,8},{8,12},{12,0},{1,5},{5,9},{9,13},{13,1},{2,6},{6,10},{... | collective-permute-start | bytes 221192 | tf_op jit(solution)/shard_map/ppermute | solution.py:245
  4.7 8.3 %collective-permute-start.3 = (bf16[288,128]{1,0:T(8,128)(2,1)S(1)}, bf16[288,128]{1,0:T(8,128)(2,1)S(1)}, u32[]{:S(2)}, u32[]{:S(2)}) collective-permute-start(bf16[288,128]{1,0:T(8,128)(2,1)S(1)} %get-tuple-element.41.refs_0_), channel_id=1, source_target_pairs={{0,12},{4,0},{8,4},{12,8},{1,13},{5,1},{9,5},{13,9},{2,14},{6,2},{... | collective-permute-start | bytes 221192 | tf_op jit(solution)/shard_map/ppermute | solution.py:245
  6.7 7.3 %collective-permute-start = (bf16[288,128]{1,0:T(8,128)(2,1)S(1)}, bf16[288,128]{1,0:T(8,128)(2,1)S(1)}, u32[]{:S(2)}, u32[]{:S(2)}) collective-permute-start(bf16[288,128]{1,0:T(8,128)(2,1)S(1)} %get-tuple-element.41.refs_0_), channel_id=1, source_target_pairs={{0,8},{4,12},{8,0},{12,4},{1,9},{5,13},{9,1},{13,5},{2,10},{6,14},... | collective-permute-start | bytes 221192 | tf_op jit(solution)/shard_map/ppermute | solution.py:245
  7.7 1.2 %collective-permute-start.1 = (f32[8,128]{1,0:T(8,128)S(1)}, f32[8,128]{1,0:T(8,128)S(1)}, u32[]{:S(2)}, u32[]{:S(2)}) collective-permute-start(f32[8,128]{1,0:T(8,128)S(1)} %get-tuple-element.42.own_ref), channel_id=1, source_target_pairs={{0,1},{1,0},{2,3},{3,2},{4,5},{5,4},{6,7},{7,6},{8,9},{9,8},{10,11... | collective-permute-start | bytes 12296 | tf_op jit(solution)/shard_map/ppermute | solution.py:242
  8.9 3.7 %collective-permute-start.2 = (f32[16,128]{1,0:T(8,128)S(1)}, f32[16,128]{1,0:T(8,128)S(1)}, u32[]{:S(2)}, u32[]{:S(2)}) collective-permute-start(f32[16,128]{1,0:T(8,128)S(1)} %shard_map.69.refs_0_), channel_id=1, source_target_pairs={{0,2},{1,3},{2,0},{3,1},{4,6},{5,7},{6,4},{7,5},{8,10},{9,11},{10,... | collective-permute-start | bytes 24584 | tf_op jit(solution)/shard_map/ppermute | solution.py:242
  14.4 1.3 %collective-permute-start.5 = (bf16[256,128]{1,0:T(8,128)(2,1)S(1)}, bf16[256,128]{1,0:T(8,128)(2,1)S(1)}, u32[]{:S(2)}, u32[]{:S(2)}) collective-permute-start(bf16[256,128]{1,0:T(8,128)(2,1)S(1)} %get-tuple-element.52), channel_id=1, source_target_pairs={{0,1},{1,0},{2,3},{3,2},{4,5},{5,4},{6,7},{7,6},{8,9},{9,8},{10,11... | collective-permute-start | bytes 196616 | tf_op jit(solution)/shard_map/ppermute | solution.py:242
  15.8 5.5 %collective-permute-start.6 = (bf16[256,128]{1,0:T(8,128)(2,1)S(1)}, bf16[256,128]{1,0:T(8,128)(2,1)S(1)}, u32[]{:S(2)}, u32[]{:S(2)}) collective-permute-start(bf16[256,128]{1,0:T(8,128)(2,1)S(1)} %get-tuple-element.54), channel_id=1, source_target_pairs={{0,2},{1,3},{2,0},{3,1},{4,6},{5,7},{6,4},{7,5},{8,10},{9,11},{10,... | collective-permute-start | bytes 196616 | tf_op jit(solution)/shard_map/ppermute | solution.py:242
  17.3 3.9 %collective-permute-start.7 = (f32[64,128]{1,0:T(8,128)S(1)}, f32[64,128]{1,0:T(8,128)S(1)}, u32[]{:S(2)}, u32[]{:S(2)}) collective-permute-start(f32[64,128]{1,0:T(8,128)S(1)} %get-tuple-element.55.refs_2_), channel_id=1, source_target_pairs={{0,2},{1,3},{2,0},{3,1},{4,6},{5,7},{6,4},{7,5},{8,10},{9,11},{10,... | collective-permute-start | bytes 98312 | tf_op jit(solution)/shard_map/ppermute | solution.py:242
  21.3 1.3 %collective-permute-start.8 = (bf16[128,256]{1,0:T(8,128)(2,1)S(1)}, bf16[128,256]{1,0:T(8,128)(2,1)S(1)}, u32[]{:S(2)}, u32[]{:S(2)}) collective-permute-start(bf16[128,256]{1,0:T(8,128)(2,1)S(1)} %get-tuple-element.57.refs_0_), channel_id=1, source_target_pairs={{0,1},{1,0},{2,3},{3,2},{4,5},{5,4},{6,7},{7,6},{8,9},{9,8},{10,11... | collective-permute-start | bytes 196616 | tf_op jit(solution)/shard_map/ppermute | solution.py:242
  22.9 6.6 %collective-permute-start.9 = (bf16[256,128]{1,0:T(8,128)(2,1)S(1)}, bf16[256,128]{1,0:T(8,128)(2,1)S(1)}, u32[]{:S(2)}, u32[]{:S(2)}) collective-permute-start(bf16[256,128]{1,0:T(8,128)(2,1)S(1)} %shard_map.82), channel_id=1, source_target_pairs={{0,4},{4,8},{8,12},{12,0},{1,5},{5,9},{9,13},{13,1},{2,6},{6,10},{... | collective-permute-start | bytes 196616 | tf_op jit(solution)/shard_map/ppermute | solution.py:245
  24.8 7.1 %collective-permute-start.10 = (bf16[256,128]{1,0:T(8,128)(2,1)S(1)}, bf16[256,128]{1,0:T(8,128)(2,1)S(1)}, u32[]{:S(2)}, u32[]{:S(2)}) collective-permute-start(bf16[256,128]{1,0:T(8,128)(2,1)S(1)} %shard_map.83), channel_id=1, source_target_pairs={{0,8},{4,12},{8,0},{12,4},{1,9},{5,13},{9,1},{13,5},{2,10},{6,14},... | collective-permute-start | bytes 196616 | tf_op jit(solution)/shard_map/ppermute | solution.py:245
  25.5 3.1 %copy-start = (f32[2,64,128]{2,1,0:T(8,128)S(1)}, f32[2,64,128]{2,1,0:T(8,128)}, u32[]{:S(2)}) copy-start(f32[2,64,128]{2,1,0:T(8,128)} %refs_1_.1) | copy-start | bytes 196612
  25.8 6.2 %collective-permute-start.11 = (bf16[256,128]{1,0:T(8,128)(2,1)S(1)}, bf16[256,128]{1,0:T(8,128)(2,1)S(1)}, u32[]{:S(2)}, u32[]{:S(2)}) collective-permute-start(bf16[256,128]{1,0:T(8,128)(2,1)S(1)} %shard_map.84), channel_id=1, source_target_pairs={{0,12},{4,0},{8,4},{12,8},{1,13},{5,1},{9,5},{13,9},{2,14},{6,2},{... | collective-permute-start | bytes 196616 | tf_op jit(solution)/shard_map/ppermute | solution.py:245

commit v4 on v3

--- a/solution.py
+++ b/solution.py
@@ -204,14 +204,29 @@
         refs[nz * half + z][...] = part_of(weight_ref, refs[z * half : (z + 1) * half])
 
 
-def node_body(half, part_ref, weight_ref, *refs):
-    total = part_ref[...] + part_of(weight_ref, refs[:half])
-    refs[half][...] = total.T.astype(refs[half].dtype)
-
-
-def own_body(half, head_ref, saved_ref, part_ref, weight_ref, *refs):
-    node_body(half, part_ref, weight_ref, *refs)
-    grad_ref = refs[half + 1]
+def node_body(half, choices, *refs):
+    weight_ref, refs = refs[0], refs[1:]
+    out_ref = refs[-1]
+
+    def one(part_ref, *tiles):
+        total = part_ref[...] + part_of(weight_ref, tiles)
+        out_ref[...] = total.T.astype(out_ref.dtype)
+
+    groups = [refs[i * (half + 1) : (i + 1) * (half + 1)] for i in range(len(choices))]
+    if len(choices) == 1:
+        one(*groups[0])
+        return
+    plane = lax.axis_index("atoms")
+    for planes, group in zip(choices, groups):
+        taken = plane == planes[0]
+        for other in planes[1:]:
+            taken = taken | (plane == other)
+        pl.when(taken)(lambda group=group: one(*group))
+
+
+def own_body(half, head_ref, saved_ref, weight_ref, *refs):
+    node_body(half, [None], weight_ref, *refs[:-1])
+    grad_ref = refs[-1]
     nk = grad_ref.shape[0]
     grad_ref[...] = head_ref[0:nk] * saved_ref[0] + head_ref[nk : 2 * nk] * saved_ref[1]
 
@@ -241,8 +256,8 @@
     def swap(value, flip):
         return lax.ppermute(value, "kvec", [(i, i ^ flip) for i in range(nq)])
 
-    def shift(value, by):
-        return lax.ppermute(value, "atoms", [(i, (i + by) % nz) for i in range(nz)])
+    def send(value, targets):
+        return lax.ppermute(value, "atoms", list(enumerate(targets)))
 
     def run(body, outs, *args, keep_args=keep, keep_outs=keep):
         return call(body, outs, *args, keep_args=keep_args, keep_outs=keep_outs)
@@ -252,7 +267,7 @@
     flips = list(range(2, nq, 2))
     zb = {0: zbuf}
     for d in ring:
-        zb[d] = shift(zbuf, -d)
+        zb[d] = send(zbuf, [(i - d) % nz for i in range(nz)])
     (cores,) = run(join_body, [shape((16, width), f32)], wide, swap(wide, 1))
     lats = [cores] + [swap(cores, s) for s in flips]
     fils = [filters] + [swap(filters, s) for s in flips]
@@ -311,22 +326,24 @@
     )
     parts = dict(zip(order, parts))
     landed = []
-    for d in range(1, nz):
+    for targets in reduce_rounds(nz):
+        planes = {}
+        for i, target in enumerate(targets):
+            planes.setdefault((target - i) % nz, []).append(i)
         (node,) = run(
-            lambda *refs: node_body(half, *refs),
+            lambda *refs: node_body(half, list(planes.values()), *refs),
             [shape((natom, width), bf16)],
-            parts[d],
             other,
-            *[tiles[d, t] for t in theirs],
+            *[v for d in planes for v in [parts[d], *[tiles[d, t] for t in theirs]]],
         )
-        landed.append(shift(node, d))
+        landed.append(send(node, targets))
     own, filter_grad = run(
         lambda *refs: own_body(half, *refs),
         [shape((natom, width), f32), shape((nk, width), f32)],
         head,
         saved_factor,
+        other,
         parts[0],
-        other,
         *[tiles[0, t] for t in theirs],
     )
     (node_grad,) = run(
@@ -336,10 +353,15 @@
 
 
 def gather_order(nz):
-    order = []
-    for d in range(1, nz // 2 + 1):
-        order += [nz - d, d] if nz - d != d else [d]
-    return [d for d in order if d]
+    return list(range(nz - 1, 0, -1))
+
+
+def reduce_rounds(nz):
+    ring = list(range(nz))
+    if nz <= 4:
+        ring = ring[:1] + ring[1::2] + ring[2::2][::-1]
+    place = {z: i for i, z in enumerate(ring)}
+    return [[ring[(place[z] + by) % nz] for z in range(nz)] for by in range(1, nz)]
 
 
 def solution(mesh):

time: 32.8 us -> 33.6 us (1.024)
  starting transfers between devices: 15.1 us -> 15.6 us
  waiting for transfers between devices: 10.5 us -> 10.9 us
    ppermute x6, starting transfers between devices: 11.4 us -> 11.8 us  [send(): return lax.ppermute(value, 'atoms', list(enumerate(targets)))]
    ppermute x6, waiting for transfers between devices: 2.41 us -> 2.76 us  [send(): return lax.ppermute(value, 'atoms', list(enumerate(targets)))]
  transfers between devices with their start and end apart: 12 -> 12, of which waited for: 6 -> 8; matrix products, arithmetic and copies ran while one was open for 2% -> 2% of each run, Pallas kernels for 10% -> 10%
where the time goes in v4:
time: 33.6 us; the launch traced here: 33.4 us
  starting transfers between devices  15.6 us (46%)
  waiting for transfers between devices  10.9 us (32%)
  Pallas kernels  5.58 us (17%)
  between operations  0.8 us (2%)
  local copies, waits for them, and re-layouts  0.62 us (2%)
    ppermute x6, starting transfers between devices, send(): return lax.ppermute(value, 'atoms', list(enumerate(targets)))  11.8 us
    ppermute x6, waiting for transfers between devices, swap(): return lax.ppermute(value, 'kvec', [(i, i ^ flip) for i in range(nq)])  8.14 us
    pallas_call x17, Pallas kernels, call(): pl.pallas_call(body, out_shape=outs, in_specs=full_spec(len(args)), out_s...  4.67 us
    ppermute x6, starting transfers between devices, swap(): return lax.ppermute(value, 'kvec', [(i, i ^ flip) for i in range(nq)])  3.73 us
    ppermute x6, waiting for transfers between devices, send(): return lax.ppermute(value, 'atoms', list(enumerate(targets)))  2.76 us
    pallas_call x1, Pallas kernels, pack(): pl.pallas_call(pack_body, out_shape=outs, in_specs=[pl.BlockSpec(memory_s...  0.91 us
  transfers between devices with their start and end apart: 12, of which 8 were waited for; matrix products, arithmetic and copies ran while one was open for 2% of the time, Pallas kernels for 10%

profile of v4, /device:TPU:0, one launch (start us, length us, event | category | flops | bytes accessed | tf_op | source)
XLA Modules:
  0.0 33.4 jit_solution(16688141074146552269)
XLA Ops:
  0.6 0.9 %shard_map.68 = (bf16[288,128]{1,0:T(8,128)(2,1)S(1)}, f32[8,128]{1,0:T(8,128)S(1)}, f32[64,128]{1,0:T(8,128)S(1)}) custom-call(s32[3,64]{1,0:T(4,128)} %lat_hbm.1, f32[3,256]{1,0:T(4,128)} %pos_hbm.1, bf16[256,128]{1,0:T(8,128)(2,1)} %cot_hbm.1, f32[64,128]{1,0:T(8,128)} %fil_hbm.1), custom_call_target="tpu_custom_call" | custom-call | tf_op jit(solution)/shard_map/pallas_call | solution.py:109
  1.5 3.1 %collective-permute-start.4 = (bf16[288,128]{1,0:T(8,128)(2,1)S(1)}, bf16[288,128]{1,0:T(8,128)(2,1)S(1)}, u32[]{:S(2)}, u32[]{:S(2)}) collective-permute-start(bf16[288,128]{1,0:T(8,128)(2,1)S(1)} %get-tuple-element.41.refs_0_), channel_id=1, source_target_pairs={{0,4},{4,8},{8,12},{12,0},{1,5},{5,9},{9,13},{13,1},{2,6},{6,10},{... | collective-permute-start | bytes 221192 | tf_op jit(solution)/shard_map/ppermute | solution.py:260
  4.7 2.6 %collective-permute-start.3 = (bf16[288,128]{1,0:T(8,128)(2,1)S(1)}, bf16[288,128]{1,0:T(8,128)(2,1)S(1)}, u32[]{:S(2)}, u32[]{:S(2)}) collective-permute-start(bf16[288,128]{1,0:T(8,128)(2,1)S(1)} %get-tuple-element.41.refs_0_), channel_id=1, source_target_pairs={{0,8},{4,12},{8,0},{12,4},{1,9},{5,13},{9,1},{13,5},{2,10},{6,14},... | collective-permute-start | bytes 221192 | tf_op jit(solution)/shard_map/ppermute | solution.py:260
  7.2 1.3 %collective-permute-start = (bf16[288,128]{1,0:T(8,128)(2,1)S(1)}, bf16[288,128]{1,0:T(8,128)(2,1)S(1)}, u32[]{:S(2)}, u32[]{:S(2)}) collective-permute-start(bf16[288,128]{1,0:T(8,128)(2,1)S(1)} %get-tuple-element.41.refs_0_), channel_id=1, source_target_pairs={{0,12},{4,0},{8,4},{12,8},{1,13},{5,1},{9,5},{13,9},{2,14},{6,2},{... | collective-permute-start | bytes 221192 | tf_op jit(solution)/shard_map/ppermute | solution.py:260
  8.6 1.2 %collective-permute-done.1.got_ref = f32[8,128]{1,0:T(8,128)S(1)} collective-permute-done((f32[8,128]{1,0:T(8,128)S(1)}, f32[8,128]{1,0:T(8,128)S(1)}, u32[]{:S(2)}, u32[]{:S(2)}) %collective-permute-start.1) | collective-permute-done | bytes 4128 | tf_op jit(solution)/shard_map/ppermute | solution.py:257
  9.8 1.5 %collective-permute-start.2 = (f32[16,128]{1,0:T(8,128)S(1)}, f32[16,128]{1,0:T(8,128)S(1)}, u32[]{:S(2)}, u32[]{:S(2)}) collective-permute-start(f32[16,128]{1,0:T(8,128)S(1)} %shard_map.69.refs_0_), channel_id=1, source_target_pairs={{0,2},{1,3},{2,0},{3,1},{4,6},{5,7},{6,4},{7,5},{8,10},{9,11},{10,... | collective-permute-start | bytes 24584 | tf_op jit(solution)/shard_map/ppermute | solution.py:257
  11.3 0.1 shard_map.70.refs_1_.refs_2_
  11.3 0.4 %shard_map.72 = (bf16[128,256]{1,0:T(8,128)(2,1)S(1)}, bf16[128,256]{1,0:T(8,128)(2,1)S(1)}, f32[128,128]{1,0:T(8,128)S(1)}, f32[128,128]{1,0:T(8,128)S(1)}) custom-call(bf16[288,128]{1,0:T(8,128)(2,1)S(1)} %get-tuple-element.41.refs_0_, bf16[128,16]{1,0:T(8,128)(2,1)S(1)} %shard_map.70.refs_1_.refs_2_, bf16[128,16]{1,0:T(8,128)(2,1)S(1)} %shard_map.70.refs_1_.refs_2_), custom_call_target="tpu_custom_call" | custom-call | tf_op jit(solution)/shard_map/pallas_call | solution.py:64
  11.7 1.7 %collective-permute-done.2.refs_0_ = f32[16,128]{1,0:T(8,128)S(1)} collective-permute-done((f32[16,128]{1,0:T(8,128)S(1)}, f32[16,128]{1,0:T(8,128)S(1)}, u32[]{:S(2)}, u32[]{:S(2)}) %collective-permute-start.2) | collective-permute-done | bytes 8224 | tf_op jit(solution)/shard_map/ppermute | solution.py:257
  13.5 0.4 %shard_map.73 = (bf16[128,256]{1,0:T(8,128)(2,1)S(1)}, bf16[128,256]{1,0:T(8,128)(2,1)S(1)}, f32[128,128]{1,0:T(8,128)S(1)}, f32[128,128]{1,0:T(8,128)S(1)}) custom-call(bf16[288,128]{1,0:T(8,128)(2,1)S(1)} %collective-permute-done.4.refs_0_.refs_2_, bf16[128,16]{1,0:T(8,128)(2,1)S(1)} %shard_map.70.refs_1_.refs_2_, ...), custom_call_target="tpu_custom_call" | custom-call | tf_op jit(solution)/shard_map/pallas_call | solution.py:64
  13.9 0.7 %shard_map.75 = (bf16[128,256]{1,0:T(8,128)(2,1)S(1)}, bf16[128,256]{1,0:T(8,128)(2,1)S(1)}, bf16[128,256]{1,0:T(8,128)(2,1)S(1)}, bf16[128,256]{1,0:T(8,128)(2,...) custom-call(bf16[288,128]{1,0:T(8,128)(2,1)S(1)} %get-tuple-element., ...), custom_call_target="tpu_custom_call" | custom-call | tf_op jit(solution)/shard_map/pallas_call | solution.py:64
  14.6 0.4 %shard_map.74 = (bf16[128,256]{1,0:T(8,128)(2,1)S(1)}, bf16[128,256]{1,0:T(8,128)(2,1)S(1)}, f32[128,128]{1,0:T(8,128)S(1)}, f32[128,128]{1,0:T(8,128)S(1)}) custom-call(bf16[288,128]{1,0:T(8,128)(2,1)S(1)} %collective-permute-done.3.refs_0_.refs_1_, bf16[128,16]{1,0:T(8,128)(2,1)S(1)} %shard_map.70.refs_1_.refs_2_, ...), custom_call_target="tpu_custom_call" | custom-call | tf_op jit(solution)/shard_map/pallas_call | solution.py:64
  14.9 0.4 %shard_map.77 = (bf16[128,256]{1,0:T(8,128)(2,1)S(1)}, bf16[128,256]{1,0:T(8,128)(2,1)S(1)}, bf16[256,128]{1,0:T(8,128)(2,1)S(1)}) custom-call(bf16[288,128]{1,0:T(8,128)(2,1)S(1)} %collective-permute-done.refs_0_, bf16[128,16]{1,0:T(8,128)(2,1)S(1)} %shard_map.70.refs_1_.refs_2_, bf16[128,16]{1,0:T(8,128)(2,1)S(1)} %shard_map.71.refs_3_.refs_4_.refs_2_, ...), custom_call_target="tpu_custom_call" | custom-call | tf_op jit(solution)/shard_map/pallas_call | solution.py:64
  15.4 0.4 %shard_map.76 = (bf16[128,256]{1,0:T(8,128)(2,1)S(1)}, bf16[128,256]{1,0:T(8,128)(2,1)S(1)}, f32[256,128]{1,0:T(8,128)S(1)}) custom-call(bf16[288,128]{1,0:T(8,128)(2,1)S(1)} %collective-permute-done.refs_0_, bf16[128,16]{1,0:T(8,128)(2,1)S(1)} %shard_map.70.refs_1_.refs_2_, bf16[128,16]{1,0:T(8,128)(2,1)S(1)} %shard_map.71.refs_3_.refs_4_.refs_2_, ...), custom_call_target="tpu_custom_call" | custom-call | tf_op jit(solution)/shard_map/pallas_call | solution.py:64
  15.7 0.9 %collective-permute-done.5.got_ref = bf16[256,128]{1,0:T(8,128)(2,1)S(1)} collective-permute-done((bf16[256,128]{1,0:T(8,128)(2,1)S(1)}, bf16[256,128]{1,0:T(8,128)(2,1)S(1)}, u32[]{:S(2)}, u32[]{:S(2)}) %collective-permute-start.5) | collective-permute-done | bytes 65568 | tf_op jit(solution)/shard_map/ppermute | solution.py:257
  16.6 1.6 %collective-permute-start.6 = (bf16[256,128]{1,0:T(8,128)(2,1)S(1)}, bf16[256,128]{1,0:T(8,128)(2,1)S(1)}, u32[]{:S(2)}, u32[]{:S(2)}) collective-permute-start(bf16[256,128]{1,0:T(8,128)(2,1)S(1)} %get-tuple-element.54), channel_id=1, source_target_pairs={{0,2},{1,3},{2,0},{3,1},{4,6},{5,7},{6,4},{7,5},{8,10},{9,11},{10,... | collective-permute-start | bytes 196616 | tf_op jit(solution)/shard_map/ppermute | solution.py:257
  18.2 0.5 %collective-permute-start.7 = (f32[64,128]{1,0:T(8,128)S(1)}, f32[64,128]{1,0:T(8,128)S(1)}, u32[]{:S(2)}, u32[]{:S(2)}) collective-permute-start(f32[64,128]{1,0:T(8,128)S(1)} %get-tuple-element.55.refs_2_), channel_id=1, source_target_pairs={{0,2},{1,3},{2,0},{3,1},{4,6},{5,7},{6,4},{7,5},{8,10},{9,11},{10,... | collective-permute-start | bytes 98312 | tf_op jit(solution)/shard_map/ppermute | solution.py:257
  18.7 3.4 %collective-permute-done.7.refs_3_ = f32[64,128]{1,0:T(8,128)S(1)} collective-permute-done((f32[64,128]{1,0:T(8,128)S(1)}, f32[64,128]{1,0:T(8,128)S(1)}, u32[]{:S(2)}, u32[]{:S(2)}) %collective-permute-start.7) | collective-permute-done | bytes 32800 | tf_op jit(solution)/shard_map/ppermute | solution.py:257
  22.1 0.1 shard_map.79
  22.3 0.2 shard_map.80
  22.6 1.0 %collective-permute-done.8.refs_2_.refs_0_ = bf16[128,256]{1,0:T(8,128)(2,1)S(1)} collective-permute-done((bf16[128,256]{1,0:T(8,128)(2,1)S(1)}, bf16[128,256]{1,0:T(8,128)(2,1)S(1)}, u32[]{:S(2)}, u32[]{:S(2)}) %collective-permute-start.8) | collective-permute-done | bytes 65568 | tf_op jit(solution)/shard_map/ppermute | solution.py:257
  23.6 0.2 shard_map.83
  23.8 1.8 %collective-permute-start.10 = (bf16[256,128]{1,0:T(8,128)(2,1)S(1)}, bf16[256,128]{1,0:T(8,128)(2,1)S(1)}, u32[]{:S(2)}, u32[]{:S(2)}) collective-permute-start(bf16[256,128]{1,0:T(8,128)(2,1)S(1)} %shard_map.83), channel_id=1, source_target_pairs={{0,12},{4,8},{8,4},{12,0},{1,13},{5,9},{9,5},{13,1},{2,14},{6,10},... | collective-permute-start | bytes 196616 | tf_op jit(solution)/shard_map/ppermute | solution.py:260
  25.6 0.3 shard_map.82
  25.9 0.3 shard_map.84
  26.2 2.9 %collective-permute-start.11 = (bf16[256,128]{1,0:T(8,128)(2,1)S(1)}, bf16[256,128]{1,0:T(8,128)(2,1)S(1)}, u32[]{:S(2)}, u32[]{:S(2)}) collective-permute-start(bf16[256,128]{1,0:T(8,128)(2,1)S(1)} %shard_map.84), channel_id=1, source_target_pairs={{0,8},{4,0},{8,12},{12,4},{1,9},{5,1},{9,13},{13,5},{2,10},{6,2},{... | collective-permute-start | bytes 196616 | tf_op jit(solution)/shard_map/ppermute | solution.py:260
  29.2 0.2 shard_map.81
  29.4 0.6 %copy.7 = f32[64,128]{1,0:T(8,128)} copy(f32[64,128]{1,0:T(8,128)S(1)} %get-tuple-element.81) | data formatting | bytes 65536
  30.0 0.7 %collective-permute-done.10.refs_2_ = bf16[256,128]{1,0:T(8,128)(2,1)S(1)} collective-permute-done((bf16[256,128]{1,0:T(8,128)(2,1)S(1)}, bf16[256,128]{1,0:T(8,128)(2,1)S(1)}, u32[]{:S(2)}, u32[]{:S(2)}) %collective-permute-start.10) | collective-permute-done | bytes 65568 | tf_op jit(solution)/shard_map/ppermute | solution.py:260
  30.7 0.7 %collective-permute-done.9.refs_1_ = bf16[256,128]{1,0:T(8,128)(2,1)S(1)} collective-permute-done((bf16[256,128]{1,0:T(8,128)(2,1)S(1)}, bf16[256,128]{1,0:T(8,128)(2,1)S(1)}, u32[]{:S(2)}, u32[]{:S(2)}) %collective-permute-start.9) | collective-permute-done | bytes 65568 | tf_op jit(solution)/shard_map/ppermute | solution.py:260
  31.5 1.3 %collective-permute-done.11.refs_3_ = bf16[256,128]{1,0:T(8,128)(2,1)S(1)} collective-permute-done((bf16[256,128]{1,0:T(8,128)(2,1)S(1)}, bf16[256,128]{1,0:T(8,128)(2,1)S(1)}, u32[]{:S(2)}, u32[]{:S(2)}) %collective-permute-start.11) | collective-permute-done | bytes 65568 | tf_op jit(solution)/shard_map/ppermute | solution.py:260
  32.8 0.7 %shard_map.85 = bf16[256,128]{1,0:T(8,128)(2,1)} custom-call(f32[256,128]{1,0:T(8,128)S(1)} %get-tuple-element.69.refs_0_, bf16[256,128]{1,0:T(8,128)(2,1)S(1)} %collective-permute-done.9.refs_1_, bf16[256,128]{1,0:T(8,128)(2,1)S(1)} %collective-permute-done.10.refs_2_, bf16[256,128]{1,0:T(8,128)(2,1)S(1)} %collective-permute-done.11.refs_3_), custom_call_target="tpu_custom_call" | custom-call | tf_op jit(solution)/shard_map/pallas_call | solution.py:64
  (13 shorter events, 0.3 us)
Async XLA Ops:
  1.5 12.0 %collective-permute-start.4 = (bf16[288,128]{1,0:T(8,128)(2,1)S(1)}, bf16[288,128]{1,0:T(8,128)(2,1)S(1)}, u32[]{:S(2)}, u32[]{:S(2)}) collective-permute-start(bf16[288,128]{1,0:T(8,128)(2,1)S(1)} %get-tuple-element.41.refs_0_), channel_id=1, source_target_pairs={{0,4},{4,8},{8,12},{12,0},{1,5},{5,9},{9,13},{13,1},{2,6},{6,10},{... | collective-permute-start | bytes 221192 | tf_op jit(solution)/shard_map/ppermute | solution.py:260
  4.7 9.2 %collective-permute-start.3 = (bf16[288,128]{1,0:T(8,128)(2,1)S(1)}, bf16[288,128]{1,0:T(8,128)(2,1)S(1)}, u32[]{:S(2)}, u32[]{:S(2)}) collective-permute-start(bf16[288,128]{1,0:T(8,128)(2,1)S(1)} %get-tuple-element.41.refs_0_), channel_id=1, source_target_pairs={{0,8},{4,12},{8,0},{12,4},{1,9},{5,13},{9,1},{13,5},{2,10},{6,14},... | collective-permute-start | bytes 221192 | tf_op jit(solution)/shard_map/ppermute | solution.py:260
  7.2 7.7 %collective-permute-start = (bf16[288,128]{1,0:T(8,128)(2,1)S(1)}, bf16[288,128]{1,0:T(8,128)(2,1)S(1)}, u32[]{:S(2)}, u32[]{:S(2)}) collective-permute-start(bf16[288,128]{1,0:T(8,128)(2,1)S(1)} %get-tuple-element.41.refs_0_), channel_id=1, source_target_pairs={{0,12},{4,0},{8,4},{12,8},{1,13},{5,1},{9,5},{13,9},{2,14},{6,2},{... | collective-permute-start | bytes 221192 | tf_op jit(solution)/shard_map/ppermute | solution.py:260
  8.6 1.2 %collective-permute-start.1 = (f32[8,128]{1,0:T(8,128)S(1)}, f32[8,128]{1,0:T(8,128)S(1)}, u32[]{:S(2)}, u32[]{:S(2)}) collective-permute-start(f32[8,128]{1,0:T(8,128)S(1)} %get-tuple-element.42.own_ref), channel_id=1, source_target_pairs={{0,1},{1,0},{2,3},{3,2},{4,5},{5,4},{6,7},{7,6},{8,9},{9,8},{10,11... | collective-permute-start | bytes 12296 | tf_op jit(solution)/shard_map/ppermute | solution.py:257
  9.8 3.7 %collective-permute-start.2 = (f32[16,128]{1,0:T(8,128)S(1)}, f32[16,128]{1,0:T(8,128)S(1)}, u32[]{:S(2)}, u32[]{:S(2)}) collective-permute-start(f32[16,128]{1,0:T(8,128)S(1)} %shard_map.69.refs_0_), channel_id=1, source_target_pairs={{0,2},{1,3},{2,0},{3,1},{4,6},{5,7},{6,4},{7,5},{8,10},{9,11},{10,... | collective-permute-start | bytes 24584 | tf_op jit(solution)/shard_map/ppermute | solution.py:257
  15.3 1.3 %collective-permute-start.5 = (bf16[256,128]{1,0:T(8,128)(2,1)S(1)}, bf16[256,128]{1,0:T(8,128)(2,1)S(1)}, u32[]{:S(2)}, u32[]{:S(2)}) collective-permute-start(bf16[256,128]{1,0:T(8,128)(2,1)S(1)} %get-tuple-element.52), channel_id=1, source_target_pairs={{0,1},{1,0},{2,3},{3,2},{4,5},{5,4},{6,7},{7,6},{8,9},{9,8},{10,11... | collective-permute-start | bytes 196616 | tf_op jit(solution)/shard_map/ppermute | solution.py:257
  16.6 5.5 %collective-permute-start.6 = (bf16[256,128]{1,0:T(8,128)(2,1)S(1)}, bf16[256,128]{1,0:T(8,128)(2,1)S(1)}, u32[]{:S(2)}, u32[]{:S(2)}) collective-permute-start(bf16[256,128]{1,0:T(8,128)(2,1)S(1)} %get-tuple-element.54), channel_id=1, source_target_pairs={{0,2},{1,3},{2,0},{3,1},{4,6},{5,7},{6,4},{7,5},{8,10},{9,11},{10,... | collective-permute-start | bytes 196616 | tf_op jit(solution)/shard_map/ppermute | solution.py:257
  18.2 3.9 %collective-permute-start.7 = (f32[64,128]{1,0:T(8,128)S(1)}, f32[64,128]{1,0:T(8,128)S(1)}, u32[]{:S(2)}, u32[]{:S(2)}) collective-permute-start(f32[64,128]{1,0:T(8,128)S(1)} %get-tuple-element.55.refs_2_), channel_id=1, source_target_pairs={{0,2},{1,3},{2,0},{3,1},{4,6},{5,7},{6,4},{7,5},{8,10},{9,11},{10,... | collective-permute-start | bytes 98312 | tf_op jit(solution)/shard_map/ppermute | solution.py:257
  22.2 1.3 %collective-permute-start.8 = (bf16[128,256]{1,0:T(8,128)(2,1)S(1)}, bf16[128,256]{1,0:T(8,128)(2,1)S(1)}, u32[]{:S(2)}, u32[]{:S(2)}) collective-permute-start(bf16[128,256]{1,0:T(8,128)(2,1)S(1)} %get-tuple-element.57.refs_0_), channel_id=1, source_target_pairs={{0,1},{1,0},{2,3},{3,2},{4,5},{5,4},{6,7},{7,6},{8,9},{9,8},{10,11... | collective-permute-start | bytes 196616 | tf_op jit(solution)/shard_map/ppermute | solution.py:257
  23.8 6.9 %collective-permute-start.10 = (bf16[256,128]{1,0:T(8,128)(2,1)S(1)}, bf16[256,128]{1,0:T(8,128)(2,1)S(1)}, u32[]{:S(2)}, u32[]{:S(2)}) collective-permute-start(bf16[256,128]{1,0:T(8,128)(2,1)S(1)} %shard_map.83), channel_id=1, source_target_pairs={{0,12},{4,8},{8,4},{12,0},{1,13},{5,9},{9,5},{13,1},{2,14},{6,10},... | collective-permute-start | bytes 196616 | tf_op jit(solution)/shard_map/ppermute | solution.py:260
  25.9 3.3 %copy-start = (f32[2,64,128]{2,1,0:T(8,128)S(1)}, f32[2,64,128]{2,1,0:T(8,128)}, u32[]{:S(2)}) copy-start(f32[2,64,128]{2,1,0:T(8,128)} %refs_1_.1) | copy-start | bytes 196612
  25.9 5.6 %collective-permute-start.9 = (bf16[256,128]{1,0:T(8,128)(2,1)S(1)}, bf16[256,128]{1,0:T(8,128)(2,1)S(1)}, u32[]{:S(2)}, u32[]{:S(2)}) collective-permute-start(bf16[256,128]{1,0:T(8,128)(2,1)S(1)} %shard_map.82), channel_id=1, source_target_pairs={{0,4},{4,12},{8,0},{12,8},{1,5},{5,13},{9,1},{13,9},{2,6},{6,14},{... | collective-permute-start | bytes 196616 | tf_op jit(solution)/shard_map/ppermute | solution.py:260
  26.2 6.6 %collective-permute-start.11 = (bf16[256,128]{1,0:T(8,128)(2,1)S(1)}, bf16[256,128]{1,0:T(8,128)(2,1)S(1)}, u32[]{:S(2)}, u32[]{:S(2)}) collective-permute-start(bf16[256,128]{1,0:T(8,128)(2,1)S(1)} %shard_map.84), channel_id=1, source_target_pairs={{0,8},{4,0},{8,12},{12,4},{1,9},{5,1},{9,13},{13,5},{2,10},{6,2},{... | collective-permute-start | bytes 196616 | tf_op jit(solution)/shard_map/ppermute | solution.py:260

commit v5 on v4

--- a/solution.py
+++ b/solution.py
@@ -86,10 +86,12 @@
     rest = x - hi
     mid = rest.astype(bf16).astype(f32)
     low = rest - mid
-    zero = jnp.zeros_like(x)
-    parts = jnp.concatenate([hi, mid, low, zero, zero, zero[:1]], 0).astype(bf16)
-    for j in range(natom // width):
-        out_ref[natom + 16 * j : natom + 16 * (j + 1), :] = parts[:, j * width : (j + 1) * width]
+    parts = jnp.concatenate([hi, mid, low], 0)
+    rows = [parts[:, j * width : (j + 1) * width] for j in range(natom // width)]
+    spare = out_ref.shape[0] - natom - 9 * len(rows)
+    if spare:
+        rows.append(jnp.zeros((spare, width), f32))
+    out_ref[natom:, :] = jnp.concatenate(rows, 0).astype(bf16)
     copies[1].wait()
     row = lax.broadcasted_iota(jnp.int32, (nk, width), 0)
     col = lax.broadcasted_iota(jnp.int32, (nk, width), 1)
@@ -103,7 +105,8 @@
 
 def pack(keep, lattice, positions, cotangent, filters):
     natom, width = cotangent.shape
-    outs = [shape((natom + 16 * (natom // width), width), bf16), shape((8, width), f32), shape(filters.shape, f32)]
+    rows = -(-9 * (natom // width) // 8) * 8
+    outs = [shape((natom + rows, width), bf16), shape((8, width), f32), shape(filters.shape, f32)]
     if keep:
         outs = [pltpu.VMEM(v.shape, v.dtype) for v in outs]
     return pl.pallas_call(
@@ -125,12 +128,21 @@
 
 
 def table_body(nk, lat_ref, out_ref):
-    width = lat_ref.shape[1]
-    zero = jnp.zeros((3, width), f32)
     for h in range(2):
-        lat = lat_ref[8 * h : 8 * h + 3, :]
-        cols = jnp.concatenate([lat, lat, lat, zero, zero, zero[:1]], 0).T
-        out_ref[h * nk : (h + 1) * nk, :] = cols[0:nk].astype(bf16)
+        out_ref[h * nk : (h + 1) * nk, :] = lat_ref[8 * h : 8 * (h + 1), :].T[0:nk]
+
+
+def coordinates(block, natom):
+    rows = block[natom:, :].astype(f32)
+    chunks = natom // block.shape[1]
+    out = []
+    for d in range(3):
+        pieces = []
+        for j in range(chunks):
+            at = [9 * j + 3 * p + d for p in range(3)]
+            pieces.append((rows[at[0] : at[0] + 1] + rows[at[1] : at[1] + 1]) + rows[at[2] : at[2] + 1])
+        out.append(jnp.concatenate(pieces, 1))
+    return out
 
 
 def factor_body(natom, nk, pairs, blocks, started, last, *refs):
@@ -139,22 +151,20 @@
     tables, refs = dict(zip(blocks, refs)), refs[len(blocks) :]
     before, refs = (dict(zip(blocks, refs)), refs[len(blocks) :]) if started else ({}, refs)
     tiles, outs = dict(zip(pairs, refs)), refs[len(pairs) :]
-    width = zb[atoms[0]].shape[1]
-    parts = {
-        z: jnp.concatenate([ref[natom + 16 * j : natom + 16 * (j + 1), :] for j in range(natom // width)], 1)
-        for z, ref in zb.items()
-    }
-    phases = {}
-    for z, t in pairs:
-        table = tables[t][(t % 2) * nk : (t % 2 + 1) * nk, :]
-        phases[z, t] = jnp.dot(table, parts[z], preferred_element_type=f32)
+    where = {z: coordinates(ref, natom) for z, ref in zb.items()}
+
+    def phase(z, t, i):
+        at = (t % 2) * nk + i
+        cols = [tables[t][at : at + step, d : d + 1] for d in range(3)]
+        return cols[0] * where[z][0] + cols[1] * where[z][1] + cols[2] * where[z][2]
+
     cot = {z: ref[0:natom, :] for z, ref in zb.items()}
     step = 32
     for b, t in enumerate(blocks):
         for i in range(0, nk, step):
             sums = [None, None]
             for z in atoms:
-                for k, value in enumerate(cos_sin(phases[z, t][i : i + step])):
+                for k, value in enumerate(cos_sin(phase(z, t, i))):
                     value = value.astype(bf16)
                     tiles[z, t][k * nk + i : k * nk + i + step, :] = value
                     part = jnp.dot(value, cot[z], preferred_element_type=f32)
@@ -273,7 +283,7 @@
     fils = [filters] + [swap(filters, s) for s in flips]
     table = {}
     for s, lat in zip([0] + flips, lats):
-        (both,) = run(lambda *refs: table_body(nk, *refs), [shape((2 * nk, 16), bf16)], lat)
+        (both,) = run(lambda *refs: table_body(nk, *refs), [shape((2 * nk, 8), f32)], lat)
         table[s] = table[s + 1] = both
     mine = list(range(0, nq, 2))
     theirs = list(range(1, nq, 2))
@@ -297,17 +307,21 @@
         return got[-1]
 
     order = [0] + ring
-    early = order[: min(3, len(order) - 1)]
+    cut = max(1, len(order) - 2)
+    early = order[: min(2, cut)]
     for z in early:
         factor([z], [0, 1])
     for t in flips:
         factor(early, [t, t + 1])
-    for z in order[len(early) : -1]:
+    for z in order[len(early) : cut]:
         factor([z], list(range(nq)))
-    sent = factor(order[-1:], theirs, bf16)
-    kept = factor(order[-1:], mine, f32)
+    sent = factor(order[cut:], theirs, bf16)
+    kept = factor(order[cut:], mine, f32)
     pair, pair16 = run(
-        pair_body, [shape((2 * count, width), f32), shape((2 * count, width), bf16)], kept, swap(sent, 1)
+        pair_body,
+        [shape((2 * count, width), f32), shape((2 * count, width), bf16)],
+        kept,
+        swap(sent, 1),
     )
     got = [swap(pair16, s) for s in flips]
     weight, head = run(
@@ -347,7 +361,11 @@
         *[tiles[0, t] for t in theirs],
     )
     (node_grad,) = run(
-        lambda *refs: final_body(scale_k, *refs), [shape((natom, width), bf16)], own, *landed, keep_outs=False
+        lambda *refs: final_body(scale_k, *refs),
+        [shape((natom, width), bf16)],
+        own,
+        *landed,
+        keep_outs=False,
     )
     return (node_grad, filter_grad)
 

time: 33.6 us -> 33.3 us (level)
  starting transfers between devices: 15.6 us -> 13.9 us
  waiting for transfers between devices: 10.9 us -> 12.6 us
  Pallas kernels: 5.58 us -> 5.15 us
    ppermute x6, waiting for transfers between devices: 2.76 us -> 4.55 us  [send(): return lax.ppermute(value, 'atoms', list(enumerate(targets)))]
    ppermute x6, starting transfers between devices: 11.8 us -> 10.2 us  [send(): return lax.ppermute(value, 'atoms', list(enumerate(targets)))]
    pallas_call x17 -> x16, Pallas kernels: 4.67 us -> 4.24 us  [call(): pl.pallas_call(body, out_shape=outs, in_specs=full_spec(len(args)), out_s...]
  transfers between devices with their start and end apart: 12 -> 12, of which waited for: 8 -> 8; matrix products, arithmetic and copies ran while one was open for 2% -> 2% of each run, Pallas kernels for 10% -> 8%
where the time goes in v5:
time: 33.3 us; the launch traced here: 33.1 us
  starting transfers between devices  13.9 us (42%)
  waiting for transfers between devices  12.6 us (38%)
  Pallas kernels  5.15 us (15%)
  between operations  0.81 us (2%)
  local copies, waits for them, and re-layouts  0.62 us (2%)
    ppermute x6, starting transfers between devices, send(): return lax.ppermute(value, 'atoms', list(enumerate(targets)))  10.2 us
    ppermute x6, waiting for transfers between devices, swap(): return lax.ppermute(value, 'kvec', [(i, i ^ flip) for i in range(nq)])  8.05 us
    ppermute x6, waiting for transfers between devices, send(): return lax.ppermute(value, 'atoms', list(enumerate(targets)))  4.55 us
    pallas_call x16, Pallas kernels, call(): pl.pallas_call(body, out_shape=outs, in_specs=full_spec(len(args)), out_s...  4.24 us
    ppermute x6, starting transfers between devices, swap(): return lax.ppermute(value, 'kvec', [(i, i ^ flip) for i in range(nq)])  3.73 us
    pallas_call x1, Pallas kernels, pack(): pl.pallas_call(pack_body, out_shape=outs, in_specs=[pl.BlockSpec(memory_s...  0.91 us
  transfers between devices with their start and end apart: 12, of which 8 were waited for; matrix products, arithmetic and copies ran while one was open for 2% of the time, Pallas kernels for 8%

profile of v5, /device:TPU:0, one launch (start us, length us, event | category | flops | bytes accessed | tf_op | source)
XLA Modules:
  0.0 33.1 jit_solution(11112332102579638900)
XLA Ops:
  0.6 0.9 %shard_map.68 = (bf16[280,128]{1,0:T(8,128)(2,1)S(1)}, f32[8,128]{1,0:T(8,128)S(1)}, f32[64,128]{1,0:T(8,128)S(1)}) custom-call(s32[3,64]{1,0:T(4,128)} %lat_hbm.1, f32[3,256]{1,0:T(4,128)} %pos_hbm.1, bf16[256,128]{1,0:T(8,128)(2,1)} %cot_hbm.1, f32[64,128]{1,0:T(8,128)} %fil_hbm.1), custom_call_target="tpu_custom_call" | custom-call | tf_op jit(solution)/shard_map/pallas_call | solution.py:112
  1.5 3.1 %collective-permute-start.4 = (bf16[280,128]{1,0:T(8,128)(2,1)S(1)}, bf16[280,128]{1,0:T(8,128)(2,1)S(1)}, u32[]{:S(2)}, u32[]{:S(2)}) collective-permute-start(bf16[280,128]{1,0:T(8,128)(2,1)S(1)} %get-tuple-element.39.refs_0_), channel_id=1, source_target_pairs={{0,4},{4,8},{8,12},{12,0},{1,5},{5,9},{9,13},{13,1},{2,6},{6,10},{... | collective-permute-start | bytes 215048 | tf_op jit(solution)/shard_map/ppermute | solution.py:270
  4.7 2.1 %collective-permute-start = (bf16[280,128]{1,0:T(8,128)(2,1)S(1)}, bf16[280,128]{1,0:T(8,128)(2,1)S(1)}, u32[]{:S(2)}, u32[]{:S(2)}) collective-permute-start(bf16[280,128]{1,0:T(8,128)(2,1)S(1)} %get-tuple-element.39.refs_0_), channel_id=1, source_target_pairs={{0,12},{4,0},{8,4},{12,8},{1,13},{5,1},{9,5},{13,9},{2,14},{6,2},{... | collective-permute-start | bytes 215048 | tf_op jit(solution)/shard_map/ppermute | solution.py:270
  6.7 0.9 %collective-permute-start.1 = (bf16[280,128]{1,0:T(8,128)(2,1)S(1)}, bf16[280,128]{1,0:T(8,128)(2,1)S(1)}, u32[]{:S(2)}, u32[]{:S(2)}) collective-permute-start(bf16[280,128]{1,0:T(8,128)(2,1)S(1)} %get-tuple-element.39.refs_0_), channel_id=1, source_target_pairs={{0,8},{4,12},{8,0},{12,4},{1,9},{5,13},{9,1},{13,5},{2,10},{6,14},... | collective-permute-start | bytes 215048 | tf_op jit(solution)/shard_map/ppermute | solution.py:270
  7.7 1.2 %collective-permute-done.2.got_ref = f32[8,128]{1,0:T(8,128)S(1)} collective-permute-done((f32[8,128]{1,0:T(8,128)S(1)}, f32[8,128]{1,0:T(8,128)S(1)}, u32[]{:S(2)}, u32[]{:S(2)}) %collective-permute-start.2) | collective-permute-done | bytes 4128 | tf_op jit(solution)/shard_map/ppermute | solution.py:267
  8.9 1.5 %collective-permute-start.3 = (f32[16,128]{1,0:T(8,128)S(1)}, f32[16,128]{1,0:T(8,128)S(1)}, u32[]{:S(2)}, u32[]{:S(2)}) collective-permute-start(f32[16,128]{1,0:T(8,128)S(1)} %shard_map.69.refs_0_), channel_id=1, source_target_pairs={{0,2},{1,3},{2,0},{3,1},{4,6},{5,7},{6,4},{7,5},{8,10},{9,11},{10,... | collective-permute-start | bytes 24584 | tf_op jit(solution)/shard_map/ppermute | solution.py:267
  10.4 0.1 shard_map.70.refs_1_.refs_2_
  10.4 0.3 shard_map.72
  10.8 1.7 %collective-permute-done.3.refs_0_ = f32[16,128]{1,0:T(8,128)S(1)} collective-permute-done((f32[16,128]{1,0:T(8,128)S(1)}, f32[16,128]{1,0:T(8,128)S(1)}, u32[]{:S(2)}, u32[]{:S(2)}) %collective-permute-start.3) | collective-permute-done | bytes 8224 | tf_op jit(solution)/shard_map/ppermute | solution.py:267
  12.5 0.1 shard_map.71.refs_2_.refs_3_
  12.6 0.5 %shard_map.74 = (bf16[128,256]{1,0:T(8,128)(2,1)S(1)}, bf16[128,256]{1,0:T(8,128)(2,1)S(1)}, bf16[128,256]{1,0:T(8,128)(2,1)S(1)}, bf16[128,256]{1,0:T(8,128)(2,...) custom-call(bf16[280,128]{1,0:T(8,128)(2,1)S(1)} %get-tuple-element.39.refs_0_, ...), custom_call_target="tpu_custom_call" | custom-call | tf_op jit(solution)/shard_map/pallas_call | solution.py:64
  13.1 0.3 shard_map.73
  13.4 0.1 collective-permute-done.1.refs_1_
  13.5 0.5 %shard_map.76 = (bf16[128,256]{1,0:T(8,128)(2,1)S(1)}, bf16[128,256]{1,0:T(8,128)(2,1)S(1)}, bf16[128,256]{1,0:T(8,128)(2,1)S(1)}, bf16[128,256]{1,0:T(8,128)(2,1)S(1)}, bf16[256,128]{1,0:T(8,128)(2,1)S(1)}) custom-call(bf16[280,128]{1,0:T(8,128)(2,1)S(1)} %collective-permute-done.refs_0_, bf16[280,128]{1,0:T(8,128)(2,1)S(1)} %collective-permute-done.1.refs_1_, ...), custom_call_target="tpu_custom_call" | custom-call | tf_op jit(solution)/shard_map/pallas_call | solution.py:64
  14.1 0.5 %shard_map.75 = (bf16[128,256]{1,0:T(8,128)(2,1)S(1)}, bf16[128,256]{1,0:T(8,128)(2,1)S(1)}, bf16[128,256]{1,0:T(8,128)(2,1)S(1)}, bf16[128,256]{1,0:T(8,128)(2,1)S(1)}, f32[256,128]{1,0:T(8,128)S(1)}) custom-call(bf16[280,128]{1,0:T(8,128)(2,1)S(1)} %collective-permute-done.refs_0_, bf16[280,128]{1,0:T(8,128)(2,1)S(1)} %collective-permute-done.1.refs_1_, ...), custom_call_target="tpu_custom_call" | custom-call | tf_op jit(solution)/shard_map/pallas_call | solution.py:64
  14.5 0.8 %collective-permute-done.5.got_ref = bf16[256,128]{1,0:T(8,128)(2,1)S(1)} collective-permute-done((bf16[256,128]{1,0:T(8,128)(2,1)S(1)}, bf16[256,128]{1,0:T(8,128)(2,1)S(1)}, u32[]{:S(2)}, u32[]{:S(2)}) %collective-permute-start.5) | collective-permute-done | bytes 65568 | tf_op jit(solution)/shard_map/ppermute | solution.py:267
  15.3 1.6 %collective-permute-start.6 = (bf16[256,128]{1,0:T(8,128)(2,1)S(1)}, bf16[256,128]{1,0:T(8,128)(2,1)S(1)}, u32[]{:S(2)}, u32[]{:S(2)}) collective-permute-start(bf16[256,128]{1,0:T(8,128)(2,1)S(1)} %get-tuple-element.50), channel_id=1, source_target_pairs={{0,2},{1,3},{2,0},{3,1},{4,6},{5,7},{6,4},{7,5},{8,10},{9,11},{10,... | collective-permute-start | bytes 196616 | tf_op jit(solution)/shard_map/ppermute | solution.py:267
  16.9 0.5 %collective-permute-start.7 = (f32[64,128]{1,0:T(8,128)S(1)}, f32[64,128]{1,0:T(8,128)S(1)}, u32[]{:S(2)}, u32[]{:S(2)}) collective-permute-start(f32[64,128]{1,0:T(8,128)S(1)} %get-tuple-element.51.refs_2_), channel_id=1, source_target_pairs={{0,2},{1,3},{2,0},{3,1},{4,6},{5,7},{6,4},{7,5},{8,10},{9,11},{10,... | collective-permute-start | bytes 98312 | tf_op jit(solution)/shard_map/ppermute | solution.py:267
  17.4 3.4 %collective-permute-done.7.refs_3_ = f32[64,128]{1,0:T(8,128)S(1)} collective-permute-done((f32[64,128]{1,0:T(8,128)S(1)}, f32[64,128]{1,0:T(8,128)S(1)}, u32[]{:S(2)}, u32[]{:S(2)}) %collective-permute-start.7) | collective-permute-done | bytes 32800 | tf_op jit(solution)/shard_map/ppermute | solution.py:267
  20.8 0.1 shard_map.78
  21.0 0.2 shard_map.79
  21.2 1.0 %collective-permute-done.8.refs_2_.refs_0_ = bf16[128,256]{1,0:T(8,128)(2,1)S(1)} collective-permute-done((bf16[128,256]{1,0:T(8,128)(2,1)S(1)}, bf16[128,256]{1,0:T(8,128)(2,1)S(1)}, u32[]{:S(2)}, u32[]{:S(2)}) %collective-permute-start.8) | collective-permute-done | bytes 65568 | tf_op jit(solution)/shard_map/ppermute | solution.py:267
  22.2 0.3 shard_map.83
  22.5 2.1 %collective-permute-start.11 = (bf16[256,128]{1,0:T(8,128)(2,1)S(1)}, bf16[256,128]{1,0:T(8,128)(2,1)S(1)}, u32[]{:S(2)}, u32[]{:S(2)}) collective-permute-start(bf16[256,128]{1,0:T(8,128)(2,1)S(1)} %shard_map.83), channel_id=1, source_target_pairs={{0,8},{4,0},{8,12},{12,4},{1,9},{5,1},{9,13},{13,5},{2,10},{6,2},{... | collective-permute-start | bytes 196616 | tf_op jit(solution)/shard_map/ppermute | solution.py:270
  24.6 0.2 shard_map.82
  24.9 1.9 %collective-permute-start.10 = (bf16[256,128]{1,0:T(8,128)(2,1)S(1)}, bf16[256,128]{1,0:T(8,128)(2,1)S(1)}, u32[]{:S(2)}, u32[]{:S(2)}) collective-permute-start(bf16[256,128]{1,0:T(8,128)(2,1)S(1)} %shard_map.82), channel_id=1, source_target_pairs={{0,12},{4,8},{8,4},{12,0},{1,13},{5,9},{9,5},{13,1},{2,14},{6,10},... | collective-permute-start | bytes 196616 | tf_op jit(solution)/shard_map/ppermute | solution.py:270
  26.7 0.3 shard_map.81
  27.1 0.2 shard_map.80
  27.3 0.6 %copy.7 = f32[64,128]{1,0:T(8,128)} copy(f32[64,128]{1,0:T(8,128)S(1)} %get-tuple-element.77) | data formatting | bytes 65536
  28.0 3.4 %collective-permute-done.10.refs_2_ = bf16[256,128]{1,0:T(8,128)(2,1)S(1)} collective-permute-done((bf16[256,128]{1,0:T(8,128)(2,1)S(1)}, bf16[256,128]{1,0:T(8,128)(2,1)S(1)}, u32[]{:S(2)}, u32[]{:S(2)}) %collective-permute-start.10) | collective-permute-done | bytes 65568 | tf_op jit(solution)/shard_map/ppermute | solution.py:270
  31.3 1.1 %collective-permute-done.9.refs_1_ = bf16[256,128]{1,0:T(8,128)(2,1)S(1)} collective-permute-done((bf16[256,128]{1,0:T(8,128)(2,1)S(1)}, bf16[256,128]{1,0:T(8,128)(2,1)S(1)}, u32[]{:S(2)}, u32[]{:S(2)}) %collective-permute-start.9) | collective-permute-done | bytes 65568 | tf_op jit(solution)/shard_map/ppermute | solution.py:270
  32.4 0.7 %shard_map.84 = bf16[256,128]{1,0:T(8,128)(2,1)} custom-call(f32[256,128]{1,0:T(8,128)S(1)} %get-tuple-element.65.refs_0_, bf16[256,128]{1,0:T(8,128)(2,1)S(1)} %collective-permute-done.9.refs_1_, bf16[256,128]{1,0:T(8,128)(2,1)S(1)} %collective-permute-done.10.refs_2_, bf16[256,128]{1,0:T(8,128)(2,1)S(1)} %collective-permute-done.11.refs_3_), custom_call_target="tpu_custom_call" | custom-call | tf_op jit(solution)/shard_map/pallas_call | solution.py:64
  (12 shorter events, 0.2 us)
Async XLA Ops:
  1.5 11.1 %collective-permute-start.4 = (bf16[280,128]{1,0:T(8,128)(2,1)S(1)}, bf16[280,128]{1,0:T(8,128)(2,1)S(1)}, u32[]{:S(2)}, u32[]{:S(2)}) collective-permute-start(bf16[280,128]{1,0:T(8,128)(2,1)S(1)} %get-tuple-element.39.refs_0_), channel_id=1, source_target_pairs={{0,4},{4,8},{8,12},{12,0},{1,5},{5,9},{9,13},{13,1},{2,6},{6,10},{... | collective-permute-start | bytes 215048 | tf_op jit(solution)/shard_map/ppermute | solution.py:270
  4.7 8.8 %collective-permute-start = (bf16[280,128]{1,0:T(8,128)(2,1)S(1)}, bf16[280,128]{1,0:T(8,128)(2,1)S(1)}, u32[]{:S(2)}, u32[]{:S(2)}) collective-permute-start(bf16[280,128]{1,0:T(8,128)(2,1)S(1)} %get-tuple-element.39.refs_0_), channel_id=1, source_target_pairs={{0,12},{4,0},{8,4},{12,8},{1,13},{5,1},{9,5},{13,9},{2,14},{6,2},{... | collective-permute-start | bytes 215048 | tf_op jit(solution)/shard_map/ppermute | solution.py:270
  6.7 6.8 %collective-permute-start.1 = (bf16[280,128]{1,0:T(8,128)(2,1)S(1)}, bf16[280,128]{1,0:T(8,128)(2,1)S(1)}, u32[]{:S(2)}, u32[]{:S(2)}) collective-permute-start(bf16[280,128]{1,0:T(8,128)(2,1)S(1)} %get-tuple-element.39.refs_0_), channel_id=1, source_target_pairs={{0,8},{4,12},{8,0},{12,4},{1,9},{5,13},{9,1},{13,5},{2,10},{6,14},... | collective-permute-start | bytes 215048 | tf_op jit(solution)/shard_map/ppermute | solution.py:270
  7.7 1.2 %collective-permute-start.2 = (f32[8,128]{1,0:T(8,128)S(1)}, f32[8,128]{1,0:T(8,128)S(1)}, u32[]{:S(2)}, u32[]{:S(2)}) collective-permute-start(f32[8,128]{1,0:T(8,128)S(1)} %get-tuple-element.40.own_ref), channel_id=1, source_target_pairs={{0,1},{1,0},{2,3},{3,2},{4,5},{5,4},{6,7},{7,6},{8,9},{9,8},{10,11... | collective-permute-start | bytes 12296 | tf_op jit(solution)/shard_map/ppermute | solution.py:267
  8.9 3.7 %collective-permute-start.3 = (f32[16,128]{1,0:T(8,128)S(1)}, f32[16,128]{1,0:T(8,128)S(1)}, u32[]{:S(2)}, u32[]{:S(2)}) collective-permute-start(f32[16,128]{1,0:T(8,128)S(1)} %shard_map.69.refs_0_), channel_id=1, source_target_pairs={{0,2},{1,3},{2,0},{3,1},{4,6},{5,7},{6,4},{7,5},{8,10},{9,11},{10,... | collective-permute-start | bytes 24584 | tf_op jit(solution)/shard_map/ppermute | solution.py:267
  14.0 1.3 %collective-permute-start.5 = (bf16[256,128]{1,0:T(8,128)(2,1)S(1)}, bf16[256,128]{1,0:T(8,128)(2,1)S(1)}, u32[]{:S(2)}, u32[]{:S(2)}) collective-permute-start(bf16[256,128]{1,0:T(8,128)(2,1)S(1)} %get-tuple-element.48), channel_id=1, source_target_pairs={{0,1},{1,0},{2,3},{3,2},{4,5},{5,4},{6,7},{7,6},{8,9},{9,8},{10,11... | collective-permute-start | bytes 196616 | tf_op jit(solution)/shard_map/ppermute | solution.py:267
  15.3 5.5 %collective-permute-start.6 = (bf16[256,128]{1,0:T(8,128)(2,1)S(1)}, bf16[256,128]{1,0:T(8,128)(2,1)S(1)}, u32[]{:S(2)}, u32[]{:S(2)}) collective-permute-start(bf16[256,128]{1,0:T(8,128)(2,1)S(1)} %get-tuple-element.50), channel_id=1, source_target_pairs={{0,2},{1,3},{2,0},{3,1},{4,6},{5,7},{6,4},{7,5},{8,10},{9,11},{10,... | collective-permute-start | bytes 196616 | tf_op jit(solution)/shard_map/ppermute | solution.py:267
  16.9 3.9 %collective-permute-start.7 = (f32[64,128]{1,0:T(8,128)S(1)}, f32[64,128]{1,0:T(8,128)S(1)}, u32[]{:S(2)}, u32[]{:S(2)}) collective-permute-start(f32[64,128]{1,0:T(8,128)S(1)} %get-tuple-element.51.refs_2_), channel_id=1, source_target_pairs={{0,2},{1,3},{2,0},{3,1},{4,6},{5,7},{6,4},{7,5},{8,10},{9,11},{10,... | collective-permute-start | bytes 98312 | tf_op jit(solution)/shard_map/ppermute | solution.py:267
  20.9 1.3 %collective-permute-start.8 = (bf16[128,256]{1,0:T(8,128)(2,1)S(1)}, bf16[128,256]{1,0:T(8,128)(2,1)S(1)}, u32[]{:S(2)}, u32[]{:S(2)}) collective-permute-start(bf16[128,256]{1,0:T(8,128)(2,1)S(1)} %get-tuple-element.53.refs_0_), channel_id=1, source_target_pairs={{0,1},{1,0},{2,3},{3,2},{4,5},{5,4},{6,7},{7,6},{8,9},{9,8},{10,11... | collective-permute-start | bytes 196616 | tf_op jit(solution)/shard_map/ppermute | solution.py:267
  22.5 5.5 %collective-permute-start.11 = (bf16[256,128]{1,0:T(8,128)(2,1)S(1)}, bf16[256,128]{1,0:T(8,128)(2,1)S(1)}, u32[]{:S(2)}, u32[]{:S(2)}) collective-permute-start(bf16[256,128]{1,0:T(8,128)(2,1)S(1)} %shard_map.83), channel_id=1, source_target_pairs={{0,8},{4,0},{8,12},{12,4},{1,9},{5,1},{9,13},{13,5},{2,10},{6,2},{... | collective-permute-start | bytes 196616 | tf_op jit(solution)/shard_map/ppermute | solution.py:270
  24.9 2.2 %copy-start = (f32[2,64,128]{2,1,0:T(8,128)S(1)}, f32[2,64,128]{2,1,0:T(8,128)}, u32[]{:S(2)}) copy-start(f32[2,64,128]{2,1,0:T(8,128)} %refs_1_.1) | copy-start | bytes 196612
  24.9 6.4 %collective-permute-start.10 = (bf16[256,128]{1,0:T(8,128)(2,1)S(1)}, bf16[256,128]{1,0:T(8,128)(2,1)S(1)}, u32[]{:S(2)}, u32[]{:S(2)}) collective-permute-start(bf16[256,128]{1,0:T(8,128)(2,1)S(1)} %shard_map.82), channel_id=1, source_target_pairs={{0,12},{4,8},{8,4},{12,0},{1,13},{5,9},{9,5},{13,1},{2,14},{6,10},... | collective-permute-start | bytes 196616 | tf_op jit(solution)/shard_map/ppermute | solution.py:270
  27.0 5.4 %collective-permute-start.9 = (bf16[256,128]{1,0:T(8,128)(2,1)S(1)}, bf16[256,128]{1,0:T(8,128)(2,1)S(1)}, u32[]{:S(2)}, u32[]{:S(2)}) collective-permute-start(bf16[256,128]{1,0:T(8,128)(2,1)S(1)} %shard_map.81), channel_id=1, source_target_pairs={{0,4},{4,12},{8,0},{12,8},{1,5},{5,13},{9,1},{13,9},{2,6},{6,14},{... | collective-permute-start | bytes 196616 | tf_op jit(solution)/shard_map/ppermute | solution.py:270

commit v6 on v5

--- a/solution.py
+++ b/solution.py
@@ -54,6 +54,7 @@
 
 
 VMEM_BUDGET = 4 * 1024 * 1024
+PIECES = 4
 
 
 def call(body, outs, *args, keep_args=True, keep_outs=True):
@@ -75,9 +76,12 @@
     copies = [
         pltpu.make_async_copy(pos_hbm, pos_ref, sem.at[0]),
         pltpu.make_async_copy(lat_hbm, lat_ref, sem.at[1]),
-        pltpu.make_async_copy(cot_hbm, out_ref.at[pl.ds(0, natom)], sem.at[2]),
-        pltpu.make_async_copy(fil_hbm, fil_ref, sem.at[3]),
+        pltpu.make_async_copy(fil_hbm, fil_ref, sem.at[2]),
     ]
+    piece = natom // PIECES
+    for j in range(PIECES):
+        rows = pl.ds(j * piece, piece)
+        copies.append(pltpu.make_async_copy(cot_hbm.at[rows], out_ref.at[rows], sem.at[3 + j]))
     for copy in copies:
         copy.start()
     copies[0].wait()
@@ -99,8 +103,8 @@
     lat = lat_ref[...].astype(f32).astype(bf16)
     wide = jnp.dot(lat, spread, preferred_element_type=f32)
     wide_ref[...] = jnp.concatenate([wide, wide, wide[:2]], 0)
-    copies[2].wait()
-    copies[3].wait()
+    for copy in copies[2:]:
+        copy.wait()
 
 
 def pack(keep, lattice, positions, cotangent, filters):
@@ -117,7 +121,7 @@
         scratch_shapes=[
             pltpu.VMEM(lattice.shape, lattice.dtype),
             pltpu.VMEM(positions.shape, positions.dtype),
-            pltpu.SemaphoreType.DMA((4,)),
+            pltpu.SemaphoreType.DMA((3 + PIECES,)),
         ],
     )(lattice, positions, cotangent, filters)
 
@@ -220,7 +224,7 @@
 
     def one(part_ref, *tiles):
         total = part_ref[...] + part_of(weight_ref, tiles)
-        out_ref[...] = total.T.astype(out_ref.dtype)
+        out_ref[...] = total.astype(out_ref.dtype)
 
     groups = [refs[i * (half + 1) : (i + 1) * (half + 1)] for i in range(len(choices))]
     if len(choices) == 1:
@@ -245,7 +249,7 @@
     total = refs[0][...]
     for ref in refs[1:-1]:
         total = total + ref[...].astype(f32)
-    refs[-1][...] = (total * scale).astype(bf16)
+    refs[-1][...] = (total * scale).T.astype(bf16)
 
 
 def shape(dims, kind):
@@ -346,14 +350,14 @@
             planes.setdefault((target - i) % nz, []).append(i)
         (node,) = run(
             lambda *refs: node_body(half, list(planes.values()), *refs),
-            [shape((natom, width), bf16)],
+            [shape((width, natom), bf16)],
             other,
             *[v for d in planes for v in [parts[d], *[tiles[d, t] for t in theirs]]],
         )
         landed.append(send(node, targets))
     own, filter_grad = run(
         lambda *refs: own_body(half, *refs),
-        [shape((natom, width), f32), shape((nk, width), f32)],
+        [shape((width, natom), f32), shape((nk, width), f32)],
         head,
         saved_factor,
         other,

time: 33.3 us -> 33.3 us (level)
  no operation moved by 1% of the time
where the time goes in v6:
time: 33.3 us; the launch traced here: 33 us
  starting transfers between devices  13.9 us (42%)
  waiting for transfers between devices  12.8 us (38%)
  Pallas kernels  4.88 us (15%)
  between operations  0.8 us (2%)
  local copies, waits for them, and re-layouts  0.63 us (2%)
    ppermute x6, starting transfers between devices, send(): return lax.ppermute(value, 'atoms', list(enumerate(targets)))  10.2 us
    ppermute x6, waiting for transfers between devices, swap(): return lax.ppermute(value, 'kvec', [(i, i ^ flip) for i in range(nq)])  8.05 us
    ppermute x6, waiting for transfers between devices, send(): return lax.ppermute(value, 'atoms', list(enumerate(targets)))  4.73 us
    pallas_call x16, Pallas kernels, call(): pl.pallas_call(body, out_shape=outs, in_specs=full_spec(len(args)), out_s...  3.97 us
    ppermute x6, starting transfers between devices, swap(): return lax.ppermute(value, 'kvec', [(i, i ^ flip) for i in range(nq)])  3.73 us
    pallas_call x1, Pallas kernels, pack(): pl.pallas_call(pack_body, out_shape=outs, in_specs=[pl.BlockSpec(memory_s...  0.9 us
  transfers between devices with their start and end apart: 12, of which 8 were waited for; matrix products, arithmetic and copies ran while one was open for 2% of the time, Pallas kernels for 8%

profile of v6, /device:TPU:0, one launch (start us, length us, event | category | flops | bytes accessed | tf_op | source)
XLA Modules:
  0.0 33.0 jit_solution(17465630532819739736)
XLA Ops:
  0.6 0.9 %shard_map.68 = (bf16[280,128]{1,0:T(8,128)(2,1)S(1)}, f32[8,128]{1,0:T(8,128)S(1)}, f32[64,128]{1,0:T(8,128)S(1)}) custom-call(s32[3,64]{1,0:T(4,128)} %lat_hbm.1, f32[3,256]{1,0:T(4,128)} %pos_hbm.1, bf16[256,128]{1,0:T(8,128)(2,1)} %cot_hbm.1, f32[64,128]{1,0:T(8,128)} %fil_hbm.1), custom_call_target="tpu_custom_call" | custom-call | tf_op jit(solution)/shard_map/pallas_call | solution.py:116
  1.5 3.1 %collective-permute-start.4 = (bf16[280,128]{1,0:T(8,128)(2,1)S(1)}, bf16[280,128]{1,0:T(8,128)(2,1)S(1)}, u32[]{:S(2)}, u32[]{:S(2)}) collective-permute-start(bf16[280,128]{1,0:T(8,128)(2,1)S(1)} %get-tuple-element.39.refs_0_), channel_id=1, source_target_pairs={{0,4},{4,8},{8,12},{12,0},{1,5},{5,9},{9,13},{13,1},{2,6},{6,10},{... | collective-permute-start | bytes 215048 | tf_op jit(solution)/shard_map/ppermute | solution.py:274
  4.6 2.1 %collective-permute-start = (bf16[280,128]{1,0:T(8,128)(2,1)S(1)}, bf16[280,128]{1,0:T(8,128)(2,1)S(1)}, u32[]{:S(2)}, u32[]{:S(2)}) collective-permute-start(bf16[280,128]{1,0:T(8,128)(2,1)S(1)} %get-tuple-element.39.refs_0_), channel_id=1, source_target_pairs={{0,12},{4,0},{8,4},{12,8},{1,13},{5,1},{9,5},{13,9},{2,14},{6,2},{... | collective-permute-start | bytes 215048 | tf_op jit(solution)/shard_map/ppermute | solution.py:274
  6.7 0.9 %collective-permute-start.1 = (bf16[280,128]{1,0:T(8,128)(2,1)S(1)}, bf16[280,128]{1,0:T(8,128)(2,1)S(1)}, u32[]{:S(2)}, u32[]{:S(2)}) collective-permute-start(bf16[280,128]{1,0:T(8,128)(2,1)S(1)} %get-tuple-element.39.refs_0_), channel_id=1, source_target_pairs={{0,8},{4,12},{8,0},{12,4},{1,9},{5,13},{9,1},{13,5},{2,10},{6,14},... | collective-permute-start | bytes 215048 | tf_op jit(solution)/shard_map/ppermute | solution.py:274
  7.7 1.2 %collective-permute-done.2.got_ref = f32[8,128]{1,0:T(8,128)S(1)} collective-permute-done((f32[8,128]{1,0:T(8,128)S(1)}, f32[8,128]{1,0:T(8,128)S(1)}, u32[]{:S(2)}, u32[]{:S(2)}) %collective-permute-start.2) | collective-permute-done | bytes 4128 | tf_op jit(solution)/shard_map/ppermute | solution.py:271
  8.9 1.5 %collective-permute-start.3 = (f32[16,128]{1,0:T(8,128)S(1)}, f32[16,128]{1,0:T(8,128)S(1)}, u32[]{:S(2)}, u32[]{:S(2)}) collective-permute-start(f32[16,128]{1,0:T(8,128)S(1)} %shard_map.69.refs_0_), channel_id=1, source_target_pairs={{0,2},{1,3},{2,0},{3,1},{4,6},{5,7},{6,4},{7,5},{8,10},{9,11},{10,... | collective-permute-start | bytes 24584 | tf_op jit(solution)/shard_map/ppermute | solution.py:271
  10.3 0.1 shard_map.70.refs_1_.refs_2_
  10.4 0.3 shard_map.72
  10.8 1.7 %collective-permute-done.3.refs_0_ = f32[16,128]{1,0:T(8,128)S(1)} collective-permute-done((f32[16,128]{1,0:T(8,128)S(1)}, f32[16,128]{1,0:T(8,128)S(1)}, u32[]{:S(2)}, u32[]{:S(2)}) %collective-permute-start.3) | collective-permute-done | bytes 8224 | tf_op jit(solution)/shard_map/ppermute | solution.py:271
  12.5 0.1 shard_map.71.refs_2_.refs_3_
  12.6 0.5 %shard_map.74 = (bf16[128,256]{1,0:T(8,128)(2,1)S(1)}, bf16[128,256]{1,0:T(8,128)(2,1)S(1)}, bf16[128,256]{1,0:T(8,128)(2,1)S(1)}, bf16[128,256]{1,0:T(8,128)(2,...) custom-call(bf16[280,128]{1,0:T(8,128)(2,1)S(1)} %get-tuple-element.39.refs_0_, ...), custom_call_target="tpu_custom_call" | custom-call | tf_op jit(solution)/shard_map/pallas_call | solution.py:65
  13.1 0.3 shard_map.73
  13.4 0.1 collective-permute-done.1.refs_1_
  13.5 0.5 %shard_map.76 = (bf16[128,256]{1,0:T(8,128)(2,1)S(1)}, bf16[128,256]{1,0:T(8,128)(2,1)S(1)}, bf16[128,256]{1,0:T(8,128)(2,1)S(1)}, bf16[128,256]{1,0:T(8,128)(2,1)S(1)}, bf16[256,128]{1,0:T(8,128)(2,1)S(1)}) custom-call(bf16[280,128]{1,0:T(8,128)(2,1)S(1)} %collective-permute-done.refs_0_, bf16[280,128]{1,0:T(8,128)(2,1)S(1)} %collective-permute-done.1.refs_1_, ...), custom_call_target="tpu_custom_call" | custom-call | tf_op jit(solution)/shard_map/pallas_call | solution.py:65
  14.1 0.5 %shard_map.75 = (bf16[128,256]{1,0:T(8,128)(2,1)S(1)}, bf16[128,256]{1,0:T(8,128)(2,1)S(1)}, bf16[128,256]{1,0:T(8,128)(2,1)S(1)}, bf16[128,256]{1,0:T(8,128)(2,1)S(1)}, f32[256,128]{1,0:T(8,128)S(1)}) custom-call(bf16[280,128]{1,0:T(8,128)(2,1)S(1)} %collective-permute-done.refs_0_, bf16[280,128]{1,0:T(8,128)(2,1)S(1)} %collective-permute-done.1.refs_1_, ...), custom_call_target="tpu_custom_call" | custom-call | tf_op jit(solution)/shard_map/pallas_call | solution.py:65
  14.5 0.8 %collective-permute-done.5.got_ref = bf16[256,128]{1,0:T(8,128)(2,1)S(1)} collective-permute-done((bf16[256,128]{1,0:T(8,128)(2,1)S(1)}, bf16[256,128]{1,0:T(8,128)(2,1)S(1)}, u32[]{:S(2)}, u32[]{:S(2)}) %collective-permute-start.5) | collective-permute-done | bytes 65568 | tf_op jit(solution)/shard_map/ppermute | solution.py:271
  15.3 1.6 %collective-permute-start.6 = (bf16[256,128]{1,0:T(8,128)(2,1)S(1)}, bf16[256,128]{1,0:T(8,128)(2,1)S(1)}, u32[]{:S(2)}, u32[]{:S(2)}) collective-permute-start(bf16[256,128]{1,0:T(8,128)(2,1)S(1)} %get-tuple-element.50), channel_id=1, source_target_pairs={{0,2},{1,3},{2,0},{3,1},{4,6},{5,7},{6,4},{7,5},{8,10},{9,11},{10,... | collective-permute-start | bytes 196616 | tf_op jit(solution)/shard_map/ppermute | solution.py:271
  16.9 0.5 %collective-permute-start.7 = (f32[64,128]{1,0:T(8,128)S(1)}, f32[64,128]{1,0:T(8,128)S(1)}, u32[]{:S(2)}, u32[]{:S(2)}) collective-permute-start(f32[64,128]{1,0:T(8,128)S(1)} %get-tuple-element.51.refs_2_), channel_id=1, source_target_pairs={{0,2},{1,3},{2,0},{3,1},{4,6},{5,7},{6,4},{7,5},{8,10},{9,11},{10,... | collective-permute-start | bytes 98312 | tf_op jit(solution)/shard_map/ppermute | solution.py:271
  17.4 3.4 %collective-permute-done.7.refs_3_ = f32[64,128]{1,0:T(8,128)S(1)} collective-permute-done((f32[64,128]{1,0:T(8,128)S(1)}, f32[64,128]{1,0:T(8,128)S(1)}, u32[]{:S(2)}, u32[]{:S(2)}) %collective-permute-start.7) | collective-permute-done | bytes 32800 | tf_op jit(solution)/shard_map/ppermute | solution.py:271
  20.8 0.1 shard_map.78
  21.0 0.2 shard_map.79
  21.2 1.0 %collective-permute-done.8.refs_2_.refs_0_ = bf16[128,256]{1,0:T(8,128)(2,1)S(1)} collective-permute-done((bf16[128,256]{1,0:T(8,128)(2,1)S(1)}, bf16[128,256]{1,0:T(8,128)(2,1)S(1)}, u32[]{:S(2)}, u32[]{:S(2)}) %collective-permute-start.8) | collective-permute-done | bytes 65568 | tf_op jit(solution)/shard_map/ppermute | solution.py:271
  22.2 0.2 shard_map.83
  22.4 2.1 %collective-permute-start.11 = (bf16[128,256]{1,0:T(8,128)(2,1)S(1)}, bf16[128,256]{1,0:T(8,128)(2,1)S(1)}, u32[]{:S(2)}, u32[]{:S(2)}) collective-permute-start(bf16[128,256]{1,0:T(8,128)(2,1)S(1)} %shard_map.83), channel_id=1, source_target_pairs={{0,8},{4,0},{8,12},{12,4},{1,9},{5,1},{9,13},{13,5},{2,10},{6,2},{... | collective-permute-start | bytes 196616 | tf_op jit(solution)/shard_map/ppermute | solution.py:274
  24.5 0.2 shard_map.82
  24.7 1.9 %collective-permute-start.10 = (bf16[128,256]{1,0:T(8,128)(2,1)S(1)}, bf16[128,256]{1,0:T(8,128)(2,1)S(1)}, u32[]{:S(2)}, u32[]{:S(2)}) collective-permute-start(bf16[128,256]{1,0:T(8,128)(2,1)S(1)} %shard_map.82), channel_id=1, source_target_pairs={{0,12},{4,8},{8,4},{12,0},{1,13},{5,9},{9,5},{13,1},{2,14},{6,10},... | collective-permute-start | bytes 196616 | tf_op jit(solution)/shard_map/ppermute | solution.py:274
  26.6 0.2 shard_map.81
  26.8 0.2 shard_map.80
  27.0 0.6 %copy.7 = f32[64,128]{1,0:T(8,128)} copy(f32[64,128]{1,0:T(8,128)S(1)} %get-tuple-element.77) | data formatting | bytes 65536
  27.6 3.5 %collective-permute-done.10.refs_2_ = bf16[128,256]{1,0:T(8,128)(2,1)S(1)} collective-permute-done((bf16[128,256]{1,0:T(8,128)(2,1)S(1)}, bf16[128,256]{1,0:T(8,128)(2,1)S(1)}, u32[]{:S(2)}, u32[]{:S(2)}) %collective-permute-start.10) | collective-permute-done | bytes 65568 | tf_op jit(solution)/shard_map/ppermute | solution.py:274
  31.1 1.1 %collective-permute-done.9.refs_1_ = bf16[128,256]{1,0:T(8,128)(2,1)S(1)} collective-permute-done((bf16[128,256]{1,0:T(8,128)(2,1)S(1)}, bf16[128,256]{1,0:T(8,128)(2,1)S(1)}, u32[]{:S(2)}, u32[]{:S(2)}) %collective-permute-start.9) | collective-permute-done | bytes 65568 | tf_op jit(solution)/shard_map/ppermute | solution.py:274
  32.2 0.7 %shard_map.84 = bf16[256,128]{1,0:T(8,128)(2,1)} custom-call(f32[128,256]{1,0:T(8,128)S(1)} %get-tuple-element.65.refs_0_, bf16[128,256]{1,0:T(8,128)(2,1)S(1)} %collective-permute-done.9.refs_1_, bf16[128,256]{1,0:T(8,128)(2,1)S(1)} %collective-permute-done.10.refs_2_, bf16[128,256]{1,0:T(8,128)(2,1)S(1)} %collective-permute-done.11.refs_3_), custom_call_target="tpu_custom_call" | custom-call | tf_op jit(solution)/shard_map/pallas_call | solution.py:65
  (12 shorter events, 0.2 us)
Async XLA Ops:
  1.5 11.1 %collective-permute-start.4 = (bf16[280,128]{1,0:T(8,128)(2,1)S(1)}, bf16[280,128]{1,0:T(8,128)(2,1)S(1)}, u32[]{:S(2)}, u32[]{:S(2)}) collective-permute-start(bf16[280,128]{1,0:T(8,128)(2,1)S(1)} %get-tuple-element.39.refs_0_), channel_id=1, source_target_pairs={{0,4},{4,8},{8,12},{12,0},{1,5},{5,9},{9,13},{13,1},{2,6},{6,10},{... | collective-permute-start | bytes 215048 | tf_op jit(solution)/shard_map/ppermute | solution.py:274
  4.6 8.8 %collective-permute-start = (bf16[280,128]{1,0:T(8,128)(2,1)S(1)}, bf16[280,128]{1,0:T(8,128)(2,1)S(1)}, u32[]{:S(2)}, u32[]{:S(2)}) collective-permute-start(bf16[280,128]{1,0:T(8,128)(2,1)S(1)} %get-tuple-element.39.refs_0_), channel_id=1, source_target_pairs={{0,12},{4,0},{8,4},{12,8},{1,13},{5,1},{9,5},{13,9},{2,14},{6,2},{... | collective-permute-start | bytes 215048 | tf_op jit(solution)/shard_map/ppermute | solution.py:274
  6.7 6.8 %collective-permute-start.1 = (bf16[280,128]{1,0:T(8,128)(2,1)S(1)}, bf16[280,128]{1,0:T(8,128)(2,1)S(1)}, u32[]{:S(2)}, u32[]{:S(2)}) collective-permute-start(bf16[280,128]{1,0:T(8,128)(2,1)S(1)} %get-tuple-element.39.refs_0_), channel_id=1, source_target_pairs={{0,8},{4,12},{8,0},{12,4},{1,9},{5,13},{9,1},{13,5},{2,10},{6,14},... | collective-permute-start | bytes 215048 | tf_op jit(solution)/shard_map/ppermute | solution.py:274
  7.7 1.2 %collective-permute-start.2 = (f32[8,128]{1,0:T(8,128)S(1)}, f32[8,128]{1,0:T(8,128)S(1)}, u32[]{:S(2)}, u32[]{:S(2)}) collective-permute-start(f32[8,128]{1,0:T(8,128)S(1)} %get-tuple-element.40.own_ref), channel_id=1, source_target_pairs={{0,1},{1,0},{2,3},{3,2},{4,5},{5,4},{6,7},{7,6},{8,9},{9,8},{10,11... | collective-permute-start | bytes 12296 | tf_op jit(solution)/shard_map/ppermute | solution.py:271
  8.9 3.7 %collective-permute-start.3 = (f32[16,128]{1,0:T(8,128)S(1)}, f32[16,128]{1,0:T(8,128)S(1)}, u32[]{:S(2)}, u32[]{:S(2)}) collective-permute-start(f32[16,128]{1,0:T(8,128)S(1)} %shard_map.69.refs_0_), channel_id=1, source_target_pairs={{0,2},{1,3},{2,0},{3,1},{4,6},{5,7},{6,4},{7,5},{8,10},{9,11},{10,... | collective-permute-start | bytes 24584 | tf_op jit(solution)/shard_map/ppermute | solution.py:271
  14.0 1.3 %collective-permute-start.5 = (bf16[256,128]{1,0:T(8,128)(2,1)S(1)}, bf16[256,128]{1,0:T(8,128)(2,1)S(1)}, u32[]{:S(2)}, u32[]{:S(2)}) collective-permute-start(bf16[256,128]{1,0:T(8,128)(2,1)S(1)} %get-tuple-element.48), channel_id=1, source_target_pairs={{0,1},{1,0},{2,3},{3,2},{4,5},{5,4},{6,7},{7,6},{8,9},{9,8},{10,11... | collective-permute-start | bytes 196616 | tf_op jit(solution)/shard_map/ppermute | solution.py:271
  15.3 5.5 %collective-permute-start.6 = (bf16[256,128]{1,0:T(8,128)(2,1)S(1)}, bf16[256,128]{1,0:T(8,128)(2,1)S(1)}, u32[]{:S(2)}, u32[]{:S(2)}) collective-permute-start(bf16[256,128]{1,0:T(8,128)(2,1)S(1)} %get-tuple-element.50), channel_id=1, source_target_pairs={{0,2},{1,3},{2,0},{3,1},{4,6},{5,7},{6,4},{7,5},{8,10},{9,11},{10,... | collective-permute-start | bytes 196616 | tf_op jit(solution)/shard_map/ppermute | solution.py:271
  16.9 3.9 %collective-permute-start.7 = (f32[64,128]{1,0:T(8,128)S(1)}, f32[64,128]{1,0:T(8,128)S(1)}, u32[]{:S(2)}, u32[]{:S(2)}) collective-permute-start(f32[64,128]{1,0:T(8,128)S(1)} %get-tuple-element.51.refs_2_), channel_id=1, source_target_pairs={{0,2},{1,3},{2,0},{3,1},{4,6},{5,7},{6,4},{7,5},{8,10},{9,11},{10,... | collective-permute-start | bytes 98312 | tf_op jit(solution)/shard_map/ppermute | solution.py:271
  20.9 1.3 %collective-permute-start.8 = (bf16[128,256]{1,0:T(8,128)(2,1)S(1)}, bf16[128,256]{1,0:T(8,128)(2,1)S(1)}, u32[]{:S(2)}, u32[]{:S(2)}) collective-permute-start(bf16[128,256]{1,0:T(8,128)(2,1)S(1)} %get-tuple-element.53.refs_0_), channel_id=1, source_target_pairs={{0,1},{1,0},{2,3},{3,2},{4,5},{5,4},{6,7},{7,6},{8,9},{9,8},{10,11... | collective-permute-start | bytes 196616 | tf_op jit(solution)/shard_map/ppermute | solution.py:271
  22.4 5.2 %collective-permute-start.11 = (bf16[128,256]{1,0:T(8,128)(2,1)S(1)}, bf16[128,256]{1,0:T(8,128)(2,1)S(1)}, u32[]{:S(2)}, u32[]{:S(2)}) collective-permute-start(bf16[128,256]{1,0:T(8,128)(2,1)S(1)} %shard_map.83), channel_id=1, source_target_pairs={{0,8},{4,0},{8,12},{12,4},{1,9},{5,1},{9,13},{13,5},{2,10},{6,2},{... | collective-permute-start | bytes 196616 | tf_op jit(solution)/shard_map/ppermute | solution.py:274
  24.7 2.1 %copy-start = (f32[2,64,128]{2,1,0:T(8,128)S(1)}, f32[2,64,128]{2,1,0:T(8,128)}, u32[]{:S(2)}) copy-start(f32[2,64,128]{2,1,0:T(8,128)} %refs_1_.1) | copy-start | bytes 196612
  24.7 6.4 %collective-permute-start.10 = (bf16[128,256]{1,0:T(8,128)(2,1)S(1)}, bf16[128,256]{1,0:T(8,128)(2,1)S(1)}, u32[]{:S(2)}, u32[]{:S(2)}) collective-permute-start(bf16[128,256]{1,0:T(8,128)(2,1)S(1)} %shard_map.82), channel_id=1, source_target_pairs={{0,12},{4,8},{8,4},{12,0},{1,13},{5,9},{9,5},{13,1},{2,14},{6,10},... | collective-permute-start | bytes 196616 | tf_op jit(solution)/shard_map/ppermute | solution.py:274
  26.7 5.5 %collective-permute-start.9 = (bf16[128,256]{1,0:T(8,128)(2,1)S(1)}, bf16[128,256]{1,0:T(8,128)(2,1)S(1)}, u32[]{:S(2)}, u32[]{:S(2)}) collective-permute-start(bf16[128,256]{1,0:T(8,128)(2,1)S(1)} %shard_map.81), channel_id=1, source_target_pairs={{0,4},{4,12},{8,0},{12,8},{1,5},{5,13},{9,1},{13,9},{2,6},{6,14},{... | collective-permute-start | bytes 196616 | tf_op jit(solution)/shard_map/ppermute | solution.py:274

commit v7 on v6

--- a/solution.py
+++ b/solution.py
@@ -178,31 +178,30 @@
                 if started:
                     total = total + before[t][row : row + step, :]
                 if last:
-                    outs[0][2 * nk * b + row : 2 * nk * b + row + step, :] = total.astype(outs[0].dtype)
+                    for out in outs:
+                        out[2 * nk * b + row : 2 * nk * b + row + step, :] = total.astype(out.dtype)
                 else:
                     outs[b][row : row + step, :] = total
 
 
-def shuffled(ref, flip, half, nk):
-    rows = [ref[2 * nk * (t ^ flip) : 2 * nk * ((t ^ flip) + 1), :] for t in range(half)]
+def shuffled(ref, flip, nq, nk):
+    rows = [ref[2 * nk * (t ^ flip) : 2 * nk * ((t ^ flip) + 1), :] for t in range(nq)]
     return jnp.concatenate(rows, 0).astype(f32)
 
 
-def pair_body(own_ref, got_ref, f_ref, fb_ref):
-    total = own_ref[...] + got_ref[...].astype(f32)
-    f_ref[...] = total
-    fb_ref[...] = total.astype(bf16)
-
-
-def weight_body(half, nk, flips, scale, *refs):
-    total = refs[0][...]
-    for ref, flip in zip(refs[1:], flips):
-        total = total + shuffled(ref, flip // 2, half, nk)
-    total = total * scale
-    fb = refs[1 + len(flips) : 1 + len(flips) + half]
-    weight_ref, head_ref = refs[1 + len(flips) + half :]
-    for t in range(half):
-        fil = fb[t][...]
+def pair_body(nq, nk, flips, own_ref, *refs):
+    total = own_ref[...]
+    for ref, flip in zip(refs, flips):
+        total = total + shuffled(ref, flip, nq, nk)
+    for out in refs[len(flips) :]:
+        out[...] = total.astype(out.dtype)
+
+
+def weight_body(nq, nk, scale, own_ref, got_ref, *refs):
+    total = (own_ref[...] + shuffled(got_ref, 1, nq, nk)) * scale
+    weight_ref, head_ref = refs[nq:]
+    for t in range(nq):
+        fil = refs[t][...]
         rows = total[2 * nk * t : 2 * nk * (t + 1)] * jnp.concatenate([fil, fil], 0)
         weight_ref[:, 2 * nk * t : 2 * nk * (t + 1)] = rows.T.astype(bf16)
     head_ref[...] = total[0 : 2 * nk]
@@ -213,20 +212,13 @@
     return jnp.dot(weight_ref[...], tile, preferred_element_type=f32)
 
 
-def mine_body(nz, half, weight_ref, *refs):
-    for z in range(nz):
-        refs[nz * half + z][...] = part_of(weight_ref, refs[z * half : (z + 1) * half])
-
-
-def node_body(half, choices, *refs):
-    weight_ref, refs = refs[0], refs[1:]
+def node_body(nq, choices, weight_ref, *refs):
     out_ref = refs[-1]
 
-    def one(part_ref, *tiles):
-        total = part_ref[...] + part_of(weight_ref, tiles)
-        out_ref[...] = total.astype(out_ref.dtype)
-
-    groups = [refs[i * (half + 1) : (i + 1) * (half + 1)] for i in range(len(choices))]
+    def one(*tiles):
+        out_ref[...] = part_of(weight_ref, tiles).astype(out_ref.dtype)
+
+    groups = [refs[i * nq : (i + 1) * nq] for i in range(len(choices))]
     if len(choices) == 1:
         one(*groups[0])
         return
@@ -238,8 +230,8 @@
         pl.when(taken)(lambda group=group: one(*group))
 
 
-def own_body(half, head_ref, saved_ref, weight_ref, *refs):
-    node_body(half, [None], weight_ref, *refs[:-1])
+def own_body(nq, head_ref, saved_ref, weight_ref, *refs):
+    node_body(nq, [None], weight_ref, *refs[:-1])
     grad_ref = refs[-1]
     nk = grad_ref.shape[0]
     grad_ref[...] = head_ref[0:nk] * saved_ref[0] + head_ref[nk : 2 * nk] * saved_ref[1]
@@ -261,11 +253,9 @@
     nq = lax.axis_size("kvec")
     natom, width = cotangent.shape
     nk = lattice.shape[1]
-    half = nq // 2
-    count = half * nk
     scale_n = 1.0 / math.sqrt(natom * nz * nq)
     scale_k = 1.0 / math.sqrt(nk * nz * nq)
-    keep = nz * natom * 4 * count * 2 <= VMEM_BUDGET
+    keep = nz * natom * 2 * nk * nq * 2 <= VMEM_BUDGET
 
     def swap(value, flip):
         return lax.ppermute(value, "kvec", [(i, i ^ flip) for i in range(nq)])
@@ -285,30 +275,28 @@
     (cores,) = run(join_body, [shape((16, width), f32)], wide, swap(wide, 1))
     lats = [cores] + [swap(cores, s) for s in flips]
     fils = [filters] + [swap(filters, s) for s in flips]
+    fils = [f for near in fils for f in (near, swap(near, 1))]
     table = {}
     for s, lat in zip([0] + flips, lats):
         (both,) = run(lambda *refs: table_body(nk, *refs), [shape((2 * nk, 8), f32)], lat)
         table[s] = table[s + 1] = both
-    mine = list(range(0, nq, 2))
-    theirs = list(range(1, nq, 2))
     tiles = {}
     total = {}
 
-    def factor(atoms, blocks, last=None):
+    def factor(atoms, blocks, last=False):
         pairs = [(z, t) for z in sorted(atoms) for t in blocks]
         outs = [shape((2 * nk, natom), bf16)] * len(pairs)
-        if last is None:
+        if last:
+            outs += [shape((2 * nk * len(blocks), width), kind) for kind in (f32, bf16)]
+        else:
             outs += [shape((2 * nk, width), f32)] * len(blocks)
-        else:
-            outs.append(shape((2 * nk * len(blocks), width), last))
         started = blocks[0] in total
         args = [zb[z] for z in sorted(atoms)] + [table[t] for t in blocks] + [total[t] for t in blocks if started]
-        body = lambda *refs: factor_body(natom, nk, pairs, blocks, started, last is not None, *refs)
+        body = lambda *refs: factor_body(natom, nk, pairs, blocks, started, last, *refs)
         got = run(body, outs, *args)
         tiles.update(zip(pairs, got))
-        if last is None:
-            total.update(zip(blocks, got[len(pairs) :]))
-        return got[-1]
+        total.update(zip(blocks, got[len(pairs) :]))
+        return got[len(pairs) :]
 
     order = [0] + ring
     cut = max(1, len(order) - 2)
@@ -319,50 +307,40 @@
         factor(early, [t, t + 1])
     for z in order[len(early) : cut]:
         factor([z], list(range(nq)))
-    sent = factor(order[cut:], theirs, bf16)
-    kept = factor(order[cut:], mine, f32)
+    kept, sent = factor(order[cut:], list(range(nq)), last=True)
+    dims = (2 * nk * nq, width)
     pair, pair16 = run(
-        pair_body,
-        [shape((2 * count, width), f32), shape((2 * count, width), bf16)],
+        lambda *refs: pair_body(nq, nk, flips, *refs),
+        [shape(dims, f32), shape(dims, bf16)],
         kept,
-        swap(sent, 1),
-    )
-    got = [swap(pair16, s) for s in flips]
+        *[swap(sent, s) for s in flips],
+    )
     weight, head = run(
-        lambda *refs: weight_body(half, nk, flips, scale_n, *refs),
-        [shape((width, 2 * count), bf16), shape((2 * nk, width), f32)],
+        lambda *refs: weight_body(nq, nk, scale_n, *refs),
+        [shape((width, 2 * nk * nq), bf16), shape((2 * nk, width), f32)],
         pair,
-        *got,
+        swap(pair16, 1),
         *fils,
     )
-    other = swap(weight, 1)
-    parts = run(
-        lambda *refs: mine_body(nz, half, *refs),
-        [shape((width, natom), f32)] * nz,
-        weight,
-        *[tiles[s, t] for s in order for t in mine],
-    )
-    parts = dict(zip(order, parts))
     landed = []
     for targets in reduce_rounds(nz):
         planes = {}
         for i, target in enumerate(targets):
             planes.setdefault((target - i) % nz, []).append(i)
         (node,) = run(
-            lambda *refs: node_body(half, list(planes.values()), *refs),
+            lambda *refs: node_body(nq, list(planes.values()), *refs),
             [shape((width, natom), bf16)],
-            other,
-            *[v for d in planes for v in [parts[d], *[tiles[d, t] for t in theirs]]],
+            weight,
+            *[tiles[d, t] for d in planes for t in range(nq)],
         )
         landed.append(send(node, targets))
     own, filter_grad = run(
-        lambda *refs: own_body(half, *refs),
+        lambda *refs: own_body(nq, *refs),
         [shape((width, natom), f32), shape((nk, width), f32)],
         head,
         saved_factor,
-        other,
-        parts[0],
-        *[tiles[0, t] for t in theirs],
+        weight,
+        *[tiles[0, t] for t in range(nq)],
     )
     (node_grad,) = run(
         lambda *refs: final_body(scale_k, *refs),

time: 33.3 us -> 36.2 us (1.087)
  waiting for transfers between devices: 12.8 us -> 15.4 us
  starting transfers between devices: 13.9 us -> 14.5 us
    ppermute x6 -> x7, waiting for transfers between devices: 8.05 us -> 10.3 us  [swap(): return lax.ppermute(value, 'kvec', [(i, i ^ flip) for i in range(nq)])]
    ppermute x6 -> x7, starting transfers between devices: 3.73 us -> 4.65 us  [swap(): return lax.ppermute(value, 'kvec', [(i, i ^ flip) for i in range(nq)])]
    ppermute x6, waiting for transfers between devices: 4.73 us -> 5.16 us  [send(): return lax.ppermute(value, 'atoms', list(enumerate(targets)))]
    pallas_call x16 -> x14, Pallas kernels: 3.97 us -> 3.74 us  [call(): pl.pallas_call(body, out_shape=outs, in_specs=full_spec(len(args)), out_s...]
  transfers between devices with their start and end apart: 12 -> 13, of which waited for: 8 -> 8; matrix products, arithmetic and copies ran while one was open for 2% -> 2% of each run, Pallas kernels for 8% -> 4%
where the time goes in v7:
time: 36.2 us; the launch traced here: 36 us
  waiting for transfers between devices  15.4 us (43%)
  starting transfers between devices  14.5 us (40%)
  Pallas kernels  4.64 us (13%)
  between operations  0.77 us (2%)
  local copies, waits for them, and re-layouts  0.62 us (2%)
    ppermute x7, waiting for transfers between devices, swap(): return lax.ppermute(value, 'kvec', [(i, i ^ flip) for i in range(nq)])  10.3 us
    ppermute x6, starting transfers between devices, send(): return lax.ppermute(value, 'atoms', list(enumerate(targets)))  9.85 us
    ppermute x6, waiting for transfers between devices, send(): return lax.ppermute(value, 'atoms', list(enumerate(targets)))  5.16 us
    ppermute x7, starting transfers between devices, swap(): return lax.ppermute(value, 'kvec', [(i, i ^ flip) for i in range(nq)])  4.65 us
    pallas_call x14, Pallas kernels, call(): pl.pallas_call(body, out_shape=outs, in_specs=full_spec(len(args)), out_s...  3.74 us
    pallas_call x1, Pallas kernels, pack(): pl.pallas_call(pack_body, out_shape=outs, in_specs=[pl.BlockSpec(memory_s...  0.9 us
  transfers between devices with their start and end apart: 13, of which 8 were waited for; matrix products, arithmetic and copies ran while one was open for 2% of the time, Pallas kernels for 4%

profile of v7, /device:TPU:0, one launch (start us, length us, event | category | flops | bytes accessed | tf_op | source)
XLA Modules:
  0.0 36.0 jit_solution(4078292444624694841)
XLA Ops:
  0.6 0.9 %shard_map.68 = (bf16[280,128]{1,0:T(8,128)(2,1)S(1)}, f32[8,128]{1,0:T(8,128)S(1)}, f32[64,128]{1,0:T(8,128)S(1)}) custom-call(s32[3,64]{1,0:T(4,128)} %lat_hbm.1, f32[3,256]{1,0:T(4,128)} %pos_hbm.1, bf16[256,128]{1,0:T(8,128)(2,1)} %cot_hbm.1, f32[64,128]{1,0:T(8,128)} %fil_hbm.1), custom_call_target="tpu_custom_call" | custom-call | tf_op jit(solution)/shard_map/pallas_call | solution.py:116
  1.5 3.1 %collective-permute-start.4 = (bf16[280,128]{1,0:T(8,128)(2,1)S(1)}, bf16[280,128]{1,0:T(8,128)(2,1)S(1)}, u32[]{:S(2)}, u32[]{:S(2)}) collective-permute-start(bf16[280,128]{1,0:T(8,128)(2,1)S(1)} %get-tuple-element.35.refs_0_), channel_id=1, source_target_pairs={{0,4},{4,8},{8,12},{12,0},{1,5},{5,9},{9,13},{13,1},{2,6},{6,10},{... | collective-permute-start | bytes 215048 | tf_op jit(solution)/shard_map/ppermute | solution.py:264
  4.6 2.1 %collective-permute-start = (bf16[280,128]{1,0:T(8,128)(2,1)S(1)}, bf16[280,128]{1,0:T(8,128)(2,1)S(1)}, u32[]{:S(2)}, u32[]{:S(2)}) collective-permute-start(bf16[280,128]{1,0:T(8,128)(2,1)S(1)} %get-tuple-element.35.refs_0_), channel_id=1, source_target_pairs={{0,12},{4,0},{8,4},{12,8},{1,13},{5,1},{9,5},{13,9},{2,14},{6,2},{... | collective-permute-start | bytes 215048 | tf_op jit(solution)/shard_map/ppermute | solution.py:264
  6.7 0.9 %collective-permute-start.1 = (bf16[280,128]{1,0:T(8,128)(2,1)S(1)}, bf16[280,128]{1,0:T(8,128)(2,1)S(1)}, u32[]{:S(2)}, u32[]{:S(2)}) collective-permute-start(bf16[280,128]{1,0:T(8,128)(2,1)S(1)} %get-tuple-element.35.refs_0_), channel_id=1, source_target_pairs={{0,8},{4,12},{8,0},{12,4},{1,9},{5,13},{9,1},{13,5},{2,10},{6,14},... | collective-permute-start | bytes 215048 | tf_op jit(solution)/shard_map/ppermute | solution.py:264
  7.7 1.2 %collective-permute-done.2.got_ref = f32[8,128]{1,0:T(8,128)S(1)} collective-permute-done((f32[8,128]{1,0:T(8,128)S(1)}, f32[8,128]{1,0:T(8,128)S(1)}, u32[]{:S(2)}, u32[]{:S(2)}) %collective-permute-start.2) | collective-permute-done | bytes 4128 | tf_op jit(solution)/shard_map/ppermute | solution.py:261
  8.9 1.5 %collective-permute-start.3 = (f32[16,128]{1,0:T(8,128)S(1)}, f32[16,128]{1,0:T(8,128)S(1)}, u32[]{:S(2)}, u32[]{:S(2)}) collective-permute-start(f32[16,128]{1,0:T(8,128)S(1)} %shard_map.69.refs_0_), channel_id=1, source_target_pairs={{0,2},{1,3},{2,0},{3,1},{4,6},{5,7},{6,4},{7,5},{8,10},{9,11},{10,... | collective-permute-start | bytes 24584 | tf_op jit(solution)/shard_map/ppermute | solution.py:261
  10.3 0.1 shard_map.70.refs_1_.refs_2_.refs_3_
  10.4 0.3 shard_map.72
  10.8 1.7 %collective-permute-done.3.refs_0_ = f32[16,128]{1,0:T(8,128)S(1)} collective-permute-done((f32[16,128]{1,0:T(8,128)S(1)}, f32[16,128]{1,0:T(8,128)S(1)}, u32[]{:S(2)}, u32[]{:S(2)}) %collective-permute-start.3) | collective-permute-done | bytes 8224 | tf_op jit(solution)/shard_map/ppermute | solution.py:261
  12.5 0.1 shard_map.71.refs_2_.refs_3_.refs_4_.refs_5_
  12.6 0.5 %shard_map.74 = (bf16[128,256]{1,0:T(8,128)(2,1)S(1)}, bf16[128,256]{1,0:T(8,128)(2,1)S(1)}, bf16[128,256]{1,0:T(8,128)(2,1)S(1)}, bf16[128,256]{1,0:T(8,128)(2,...) custom-call(bf16[280,128]{1,0:T(8,128)(2,1)S(1)} %get-tuple-element.35.refs_0_, ...), custom_call_target="tpu_custom_call" | custom-call | tf_op jit(solution)/shard_map/pallas_call | solution.py:65
  13.1 0.3 shard_map.73
  13.4 0.1 collective-permute-done.1.refs_1_
  13.5 0.8 %shard_map.75 = (bf16[128,256]{1,0:T(8,128)(2,1)S(1)}, bf16[128,256]{1,0:T(8,128)(2,1)S(1)}, bf16[128,256]{1,0:T(8,128)(2,1)S(1)}, bf16[128,256]{1,0:T(8,128)(2,...) custom-call(bf16[280,128]{1,0:T(8,128)(2,1)S(1)} %collective-permute, ...), custom_call_target="tpu_custom_call" | custom-call | tf_op jit(solution)/shard_map/pallas_call | solution.py:65
  14.3 1.6 %collective-permute-start.5 = (bf16[512,128]{1,0:T(8,128)(2,1)S(1)}, bf16[512,128]{1,0:T(8,128)(2,1)S(1)}, u32[]{:S(2)}, u32[]{:S(2)}) collective-permute-start(bf16[512,128]{1,0:T(8,128)(2,1)S(1)} %get-tuple-element.44), channel_id=1, source_target_pairs={{0,2},{1,3},{2,0},{3,1},{4,6},{5,7},{6,4},{7,5},{8,10},{9,11},{10,... | collective-permute-start | bytes 393224 | tf_op jit(solution)/shard_map/ppermute | solution.py:261
  15.8 3.7 %collective-permute-done.5.refs_1_ = bf16[512,128]{1,0:T(8,128)(2,1)S(1)} collective-permute-done((bf16[512,128]{1,0:T(8,128)(2,1)S(1)}, bf16[512,128]{1,0:T(8,128)(2,1)S(1)}, u32[]{:S(2)}, u32[]{:S(2)}) %collective-permute-start.5) | collective-permute-done | bytes 131104 | tf_op jit(solution)/shard_map/ppermute | solution.py:261
  19.6 0.1 collective-permute-start.6
  19.6 1.4 %collective-permute-start.8 = (f32[64,128]{1,0:T(8,128)S(1)}, f32[64,128]{1,0:T(8,128)S(1)}, u32[]{:S(2)}, u32[]{:S(2)}) collective-permute-start(f32[64,128]{1,0:T(8,128)S(1)} %get-tuple-element.47.refs_2_), channel_id=1, source_target_pairs={{0,2},{1,3},{2,0},{3,1},{4,6},{5,7},{6,4},{7,5},{8,10},{9,11},{10,... | collective-permute-start | bytes 98312 | tf_op jit(solution)/shard_map/ppermute | solution.py:261
  21.0 0.2 collective-permute-start.7
  21.2 2.5 %collective-permute-done.8.refs_4_ = f32[64,128]{1,0:T(8,128)S(1)} collective-permute-done((f32[64,128]{1,0:T(8,128)S(1)}, f32[64,128]{1,0:T(8,128)S(1)}, u32[]{:S(2)}, u32[]{:S(2)}) %collective-permute-start.8) | collective-permute-done | bytes 32800 | tf_op jit(solution)/shard_map/ppermute | solution.py:261
  23.6 1.2 %collective-permute-done.9.refs_5_ = f32[64,128]{1,0:T(8,128)S(1)} collective-permute-done((f32[64,128]{1,0:T(8,128)S(1)}, f32[64,128]{1,0:T(8,128)S(1)}, u32[]{:S(2)}, u32[]{:S(2)}) %collective-permute-start.9) | collective-permute-done | bytes 32800 | tf_op jit(solution)/shard_map/ppermute | solution.py:261
  24.8 0.1 shard_map.77
  24.9 0.2 shard_map.80
  25.2 0.2 shard_map.81
  25.4 0.2 shard_map.79
  25.6 1.7 %collective-permute-start.12 = (bf16[128,256]{1,0:T(8,128)(2,1)S(1)}, bf16[128,256]{1,0:T(8,128)(2,1)S(1)}, u32[]{:S(2)}, u32[]{:S(2)}) collective-permute-start(bf16[128,256]{1,0:T(8,128)(2,1)S(1)} %shard_map.81), channel_id=1, source_target_pairs={{0,8},{4,0},{8,12},{12,4},{1,9},{5,1},{9,13},{13,5},{2,10},{6,2},{... | collective-permute-start | bytes 196616 | tf_op jit(solution)/shard_map/ppermute | solution.py:264
  27.4 2.0 %collective-permute-start.11 = (bf16[128,256]{1,0:T(8,128)(2,1)S(1)}, bf16[128,256]{1,0:T(8,128)(2,1)S(1)}, u32[]{:S(2)}, u32[]{:S(2)}) collective-permute-start(bf16[128,256]{1,0:T(8,128)(2,1)S(1)} %shard_map.80), channel_id=1, source_target_pairs={{0,12},{4,8},{8,4},{12,0},{1,13},{5,9},{9,5},{13,1},{2,14},{6,10},... | collective-permute-start | bytes 196616 | tf_op jit(solution)/shard_map/ppermute | solution.py:264
  29.3 0.2 shard_map.78
  29.5 0.6 %copy.7 = f32[64,128]{1,0:T(8,128)} copy(f32[64,128]{1,0:T(8,128)S(1)} %get-tuple-element.69) | data formatting | bytes 65536
  30.1 3.6 %collective-permute-done.11.refs_2_ = bf16[128,256]{1,0:T(8,128)(2,1)S(1)} collective-permute-done((bf16[128,256]{1,0:T(8,128)(2,1)S(1)}, bf16[128,256]{1,0:T(8,128)(2,1)S(1)}, u32[]{:S(2)}, u32[]{:S(2)}) %collective-permute-start.11) | collective-permute-done | bytes 65568 | tf_op jit(solution)/shard_map/ppermute | solution.py:264
  33.7 1.5 %collective-permute-done.10.refs_1_ = bf16[128,256]{1,0:T(8,128)(2,1)S(1)} collective-permute-done((bf16[128,256]{1,0:T(8,128)(2,1)S(1)}, bf16[128,256]{1,0:T(8,128)(2,1)S(1)}, u32[]{:S(2)}, u32[]{:S(2)}) %collective-permute-start.10) | collective-permute-done | bytes 65568 | tf_op jit(solution)/shard_map/ppermute | solution.py:264
  35.2 0.7 %shard_map.82 = bf16[256,128]{1,0:T(8,128)(2,1)} custom-call(f32[128,256]{1,0:T(8,128)S(1)} %get-tuple-element.54.refs_0_, bf16[128,256]{1,0:T(8,128)(2,1)S(1)} %collective-permute-done.10.refs_1_, bf16[128,256]{1,0:T(8,128)(2,1)S(1)} %collective-permute-done.11.refs_2_, bf16[128,256]{1,0:T(8,128)(2,1)S(1)} %collective-permute-done.12.refs_3_), custom_call_target="tpu_custom_call" | custom-call | tf_op jit(solution)/shard_map/pallas_call | solution.py:65
  (12 shorter events, 0.1 us)
Async XLA Ops:
  1.5 11.1 %collective-permute-start.4 = (bf16[280,128]{1,0:T(8,128)(2,1)S(1)}, bf16[280,128]{1,0:T(8,128)(2,1)S(1)}, u32[]{:S(2)}, u32[]{:S(2)}) collective-permute-start(bf16[280,128]{1,0:T(8,128)(2,1)S(1)} %get-tuple-element.35.refs_0_), channel_id=1, source_target_pairs={{0,4},{4,8},{8,12},{12,0},{1,5},{5,9},{9,13},{13,1},{2,6},{6,10},{... | collective-permute-start | bytes 215048 | tf_op jit(solution)/shard_map/ppermute | solution.py:264
  4.6 8.8 %collective-permute-start = (bf16[280,128]{1,0:T(8,128)(2,1)S(1)}, bf16[280,128]{1,0:T(8,128)(2,1)S(1)}, u32[]{:S(2)}, u32[]{:S(2)}) collective-permute-start(bf16[280,128]{1,0:T(8,128)(2,1)S(1)} %get-tuple-element.35.refs_0_), channel_id=1, source_target_pairs={{0,12},{4,0},{8,4},{12,8},{1,13},{5,1},{9,5},{13,9},{2,14},{6,2},{... | collective-permute-start | bytes 215048 | tf_op jit(solution)/shard_map/ppermute | solution.py:264
  6.7 6.8 %collective-permute-start.1 = (bf16[280,128]{1,0:T(8,128)(2,1)S(1)}, bf16[280,128]{1,0:T(8,128)(2,1)S(1)}, u32[]{:S(2)}, u32[]{:S(2)}) collective-permute-start(bf16[280,128]{1,0:T(8,128)(2,1)S(1)} %get-tuple-element.35.refs_0_), channel_id=1, source_target_pairs={{0,8},{4,12},{8,0},{12,4},{1,9},{5,13},{9,1},{13,5},{2,10},{6,14},... | collective-permute-start | bytes 215048 | tf_op jit(solution)/shard_map/ppermute | solution.py:264
  7.7 1.2 %collective-permute-start.2 = (f32[8,128]{1,0:T(8,128)S(1)}, f32[8,128]{1,0:T(8,128)S(1)}, u32[]{:S(2)}, u32[]{:S(2)}) collective-permute-start(f32[8,128]{1,0:T(8,128)S(1)} %get-tuple-element.36.own_ref), channel_id=1, source_target_pairs={{0,1},{1,0},{2,3},{3,2},{4,5},{5,4},{6,7},{7,6},{8,9},{9,8},{10,11... | collective-permute-start | bytes 12296 | tf_op jit(solution)/shard_map/ppermute | solution.py:261
  8.9 3.7 %collective-permute-start.3 = (f32[16,128]{1,0:T(8,128)S(1)}, f32[16,128]{1,0:T(8,128)S(1)}, u32[]{:S(2)}, u32[]{:S(2)}) collective-permute-start(f32[16,128]{1,0:T(8,128)S(1)} %shard_map.69.refs_0_), channel_id=1, source_target_pairs={{0,2},{1,3},{2,0},{3,1},{4,6},{5,7},{6,4},{7,5},{8,10},{9,11},{10,... | collective-permute-start | bytes 24584 | tf_op jit(solution)/shard_map/ppermute | solution.py:261
  14.3 5.3 %collective-permute-start.5 = (bf16[512,128]{1,0:T(8,128)(2,1)S(1)}, bf16[512,128]{1,0:T(8,128)(2,1)S(1)}, u32[]{:S(2)}, u32[]{:S(2)}) collective-permute-start(bf16[512,128]{1,0:T(8,128)(2,1)S(1)} %get-tuple-element.44), channel_id=1, source_target_pairs={{0,2},{1,3},{2,0},{3,1},{4,6},{5,7},{6,4},{7,5},{8,10},{9,11},{10,... | collective-permute-start | bytes 393224 | tf_op jit(solution)/shard_map/ppermute | solution.py:261
  19.6 5.3 %collective-permute-start.6 = (bf16[512,128]{1,0:T(8,128)(2,1)S(1)}, bf16[512,128]{1,0:T(8,128)(2,1)S(1)}, u32[]{:S(2)}, u32[]{:S(2)}) collective-permute-start(bf16[512,128]{1,0:T(8,128)(2,1)S(1)} %get-tuple-element.46), channel_id=1, source_target_pairs={{0,1},{1,0},{2,3},{3,2},{4,5},{5,4},{6,7},{7,6},{8,9},{9,8},{10,11... | collective-permute-start | bytes 393224 | tf_op jit(solution)/shard_map/ppermute | solution.py:261
  19.6 4.0 %collective-permute-start.8 = (f32[64,128]{1,0:T(8,128)S(1)}, f32[64,128]{1,0:T(8,128)S(1)}, u32[]{:S(2)}, u32[]{:S(2)}) collective-permute-start(f32[64,128]{1,0:T(8,128)S(1)} %get-tuple-element.47.refs_2_), channel_id=1, source_target_pairs={{0,2},{1,3},{2,0},{3,1},{4,6},{5,7},{6,4},{7,5},{8,10},{9,11},{10,... | collective-permute-start | bytes 98312 | tf_op jit(solution)/shard_map/ppermute | solution.py:261
  21.0 2.6 %collective-permute-start.7 = (f32[64,128]{1,0:T(8,128)S(1)}, f32[64,128]{1,0:T(8,128)S(1)}, u32[]{:S(2)}, u32[]{:S(2)}) collective-permute-start(f32[64,128]{1,0:T(8,128)S(1)} %get-tuple-element.47.refs_2_), channel_id=1, source_target_pairs={{0,1},{1,0},{2,3},{3,2},{4,5},{5,4},{6,7},{7,6},{8,9},{9,8},{10,11... | collective-permute-start | bytes 98312 | tf_op jit(solution)/shard_map/ppermute | solution.py:261
  23.6 1.2 %collective-permute-start.9 = (f32[64,128]{1,0:T(8,128)S(1)}, f32[64,128]{1,0:T(8,128)S(1)}, u32[]{:S(2)}, u32[]{:S(2)}) collective-permute-start(f32[64,128]{1,0:T(8,128)S(1)} %collective-permute-done.8.refs_4_), channel_id=1, source_target_pairs={{0,1},{1,0},{2,3},{3,2},{4,5},{5,4},{6,7},{7,6},{8,9},{9,8},{10,11... | collective-permute-start | bytes 98312 | tf_op jit(solution)/shard_map/ppermute | solution.py:261
  25.4 3.9 %copy-start = (f32[2,64,128]{2,1,0:T(8,128)S(1)}, f32[2,64,128]{2,1,0:T(8,128)}, u32[]{:S(2)}) copy-start(f32[2,64,128]{2,1,0:T(8,128)} %refs_1_.1) | copy-start | bytes 196612
  25.6 4.5 %collective-permute-start.12 = (bf16[128,256]{1,0:T(8,128)(2,1)S(1)}, bf16[128,256]{1,0:T(8,128)(2,1)S(1)}, u32[]{:S(2)}, u32[]{:S(2)}) collective-permute-start(bf16[128,256]{1,0:T(8,128)(2,1)S(1)} %shard_map.81), channel_id=1, source_target_pairs={{0,8},{4,0},{8,12},{12,4},{1,9},{5,1},{9,13},{13,5},{2,10},{6,2},{... | collective-permute-start | bytes 196616 | tf_op jit(solution)/shard_map/ppermute | solution.py:264
  27.4 6.4 %collective-permute-start.11 = (bf16[128,256]{1,0:T(8,128)(2,1)S(1)}, bf16[128,256]{1,0:T(8,128)(2,1)S(1)}, u32[]{:S(2)}, u32[]{:S(2)}) collective-permute-start(bf16[128,256]{1,0:T(8,128)(2,1)S(1)} %shard_map.80), channel_id=1, source_target_pairs={{0,12},{4,8},{8,4},{12,0},{1,13},{5,9},{9,5},{13,1},{2,14},{6,10},... | collective-permute-start | bytes 196616 | tf_op jit(solution)/shard_map/ppermute | solution.py:264
  29.3 5.9 %collective-permute-start.10 = (bf16[128,256]{1,0:T(8,128)(2,1)S(1)}, bf16[128,256]{1,0:T(8,128)(2,1)S(1)}, u32[]{:S(2)}, u32[]{:S(2)}) collective-permute-start(bf16[128,256]{1,0:T(8,128)(2,1)S(1)} %shard_map.79), channel_id=1, source_target_pairs={{0,4},{4,12},{8,0},{12,8},{1,5},{5,13},{9,1},{13,9},{2,6},{6,14},{... | collective-permute-start | bytes 196616 | tf_op jit(solution)/shard_map/ppermute | solution.py:264

commit v8 on v6

--- a/solution.py
+++ b/solution.py
@@ -381,9 +381,13 @@
 def reduce_rounds(nz):
     ring = list(range(nz))
     if nz <= 4:
-        ring = ring[:1] + ring[1::2] + ring[2::2][::-1]
+        middle = (nz + 1) // 2
+        ring = sorted(ring, key=lambda z: (z % middle, z))
     place = {z: i for i, z in enumerate(ring)}
-    return [[ring[(place[z] + by) % nz] for z in range(nz)] for by in range(1, nz)]
+    steps = list(range(1, nz))
+    if nz <= 4:
+        steps.sort(key=lambda by: (min(by, nz - by), by))
+    return [[ring[(place[z] + by) % nz] for z in range(nz)] for by in steps]
 
 
 def solution(mesh):

time: 33.3 us -> 33.6 us (level)
  starting transfers between devices: 13.9 us -> 14.5 us
    ppermute x6, starting transfers between devices: 10.2 us -> 10.7 us  [send(): return lax.ppermute(value, 'atoms', list(enumerate(targets)))]
  transfers between devices with their start and end apart: 12 -> 12, of which waited for: 8 -> 8; matrix products, arithmetic and copies ran while one was open for 2% -> 2% of each run, Pallas kernels for 8% -> 7%
where the time goes in v8:
time: 33.6 us; the launch traced here: 33.4 us
  starting transfers between devices  14.5 us (43%)
  waiting for transfers between devices  12.6 us (38%)
  Pallas kernels  4.87 us (14%)
  between operations  0.78 us (2%)
  local copies, waits for them, and re-layouts  0.63 us (2%)
    ppermute x6, starting transfers between devices, send(): return lax.ppermute(value, 'atoms', list(enumerate(targets)))  10.7 us
    ppermute x6, waiting for transfers between devices, swap(): return lax.ppermute(value, 'kvec', [(i, i ^ flip) for i in range(nq)])  8.05 us
    ppermute x6, waiting for transfers between devices, send(): return lax.ppermute(value, 'atoms', list(enumerate(targets)))  4.55 us
    pallas_call x16, Pallas kernels, call(): pl.pallas_call(body, out_shape=outs, in_specs=full_spec(len(args)), out_s...  3.97 us
    ppermute x6, starting transfers between devices, swap(): return lax.ppermute(value, 'kvec', [(i, i ^ flip) for i in range(nq)])  3.73 us
    pallas_call x1, Pallas kernels, pack(): pl.pallas_call(pack_body, out_shape=outs, in_specs=[pl.BlockSpec(memory_s...  0.9 us
  transfers between devices with their start and end apart: 12, of which 8 were waited for; matrix products, arithmetic and copies ran while one was open for 2% of the time, Pallas kernels for 7%

profile of v8, /device:TPU:0, one launch (start us, length us, event | category | flops | bytes accessed | tf_op | source)
XLA Modules:
  0.0 33.4 jit_solution(3228072453806680649)
XLA Ops:
  0.6 0.9 %shard_map.68 = (bf16[280,128]{1,0:T(8,128)(2,1)S(1)}, f32[8,128]{1,0:T(8,128)S(1)}, f32[64,128]{1,0:T(8,128)S(1)}) custom-call(s32[3,64]{1,0:T(4,128)} %lat_hbm.1, f32[3,256]{1,0:T(4,128)} %pos_hbm.1, bf16[256,128]{1,0:T(8,128)(2,1)} %cot_hbm.1, f32[64,128]{1,0:T(8,128)} %fil_hbm.1), custom_call_target="tpu_custom_call" | custom-call | tf_op jit(solution)/shard_map/pallas_call | solution.py:116
  1.5 3.1 %collective-permute-start.4 = (bf16[280,128]{1,0:T(8,128)(2,1)S(1)}, bf16[280,128]{1,0:T(8,128)(2,1)S(1)}, u32[]{:S(2)}, u32[]{:S(2)}) collective-permute-start(bf16[280,128]{1,0:T(8,128)(2,1)S(1)} %get-tuple-element.39.refs_0_), channel_id=1, source_target_pairs={{0,4},{4,8},{8,12},{12,0},{1,5},{5,9},{9,13},{13,1},{2,6},{6,10},{... | collective-permute-start | bytes 215048 | tf_op jit(solution)/shard_map/ppermute | solution.py:274
  4.6 2.1 %collective-permute-start = (bf16[280,128]{1,0:T(8,128)(2,1)S(1)}, bf16[280,128]{1,0:T(8,128)(2,1)S(1)}, u32[]{:S(2)}, u32[]{:S(2)}) collective-permute-start(bf16[280,128]{1,0:T(8,128)(2,1)S(1)} %get-tuple-element.39.refs_0_), channel_id=1, source_target_pairs={{0,12},{4,0},{8,4},{12,8},{1,13},{5,1},{9,5},{13,9},{2,14},{6,2},{... | collective-permute-start | bytes 215048 | tf_op jit(solution)/shard_map/ppermute | solution.py:274
  6.7 0.9 %collective-permute-start.1 = (bf16[280,128]{1,0:T(8,128)(2,1)S(1)}, bf16[280,128]{1,0:T(8,128)(2,1)S(1)}, u32[]{:S(2)}, u32[]{:S(2)}) collective-permute-start(bf16[280,128]{1,0:T(8,128)(2,1)S(1)} %get-tuple-element.39.refs_0_), channel_id=1, source_target_pairs={{0,8},{4,12},{8,0},{12,4},{1,9},{5,13},{9,1},{13,5},{2,10},{6,14},... | collective-permute-start | bytes 215048 | tf_op jit(solution)/shard_map/ppermute | solution.py:274
  7.7 1.2 %collective-permute-done.2.got_ref = f32[8,128]{1,0:T(8,128)S(1)} collective-permute-done((f32[8,128]{1,0:T(8,128)S(1)}, f32[8,128]{1,0:T(8,128)S(1)}, u32[]{:S(2)}, u32[]{:S(2)}) %collective-permute-start.2) | collective-permute-done | bytes 4128 | tf_op jit(solution)/shard_map/ppermute | solution.py:271
  8.9 1.5 %collective-permute-start.3 = (f32[16,128]{1,0:T(8,128)S(1)}, f32[16,128]{1,0:T(8,128)S(1)}, u32[]{:S(2)}, u32[]{:S(2)}) collective-permute-start(f32[16,128]{1,0:T(8,128)S(1)} %shard_map.69.refs_0_), channel_id=1, source_target_pairs={{0,2},{1,3},{2,0},{3,1},{4,6},{5,7},{6,4},{7,5},{8,10},{9,11},{10,... | collective-permute-start | bytes 24584 | tf_op jit(solution)/shard_map/ppermute | solution.py:271
  10.3 0.1 shard_map.70.refs_1_.refs_2_
  10.4 0.3 shard_map.72
  10.8 1.7 %collective-permute-done.3.refs_0_ = f32[16,128]{1,0:T(8,128)S(1)} collective-permute-done((f32[16,128]{1,0:T(8,128)S(1)}, f32[16,128]{1,0:T(8,128)S(1)}, u32[]{:S(2)}, u32[]{:S(2)}) %collective-permute-start.3) | collective-permute-done | bytes 8224 | tf_op jit(solution)/shard_map/ppermute | solution.py:271
  12.5 0.1 shard_map.71.refs_2_.refs_3_
  12.6 0.5 %shard_map.74 = (bf16[128,256]{1,0:T(8,128)(2,1)S(1)}, bf16[128,256]{1,0:T(8,128)(2,1)S(1)}, bf16[128,256]{1,0:T(8,128)(2,1)S(1)}, bf16[128,256]{1,0:T(8,128)(2,...) custom-call(bf16[280,128]{1,0:T(8,128)(2,1)S(1)} %get-tuple-element.39.refs_0_, ...), custom_call_target="tpu_custom_call" | custom-call | tf_op jit(solution)/shard_map/pallas_call | solution.py:65
  13.1 0.3 shard_map.73
  13.5 0.5 %shard_map.76 = (bf16[128,256]{1,0:T(8,128)(2,1)S(1)}, bf16[128,256]{1,0:T(8,128)(2,1)S(1)}, bf16[128,256]{1,0:T(8,128)(2,1)S(1)}, bf16[128,256]{1,0:T(8,128)(2,1)S(1)}, bf16[256,128]{1,0:T(8,128)(2,1)S(1)}) custom-call(bf16[280,128]{1,0:T(8,128)(2,1)S(1)} %collective-permute-done.refs_0_, bf16[280,128]{1,0:T(8,128)(2,1)S(1)} %collective-permute-done.1.refs_1_, ...), custom_call_target="tpu_custom_call" | custom-call | tf_op jit(solution)/shard_map/pallas_call | solution.py:65
  14.1 0.5 %shard_map.75 = (bf16[128,256]{1,0:T(8,128)(2,1)S(1)}, bf16[128,256]{1,0:T(8,128)(2,1)S(1)}, bf16[128,256]{1,0:T(8,128)(2,1)S(1)}, bf16[128,256]{1,0:T(8,128)(2,1)S(1)}, f32[256,128]{1,0:T(8,128)S(1)}) custom-call(bf16[280,128]{1,0:T(8,128)(2,1)S(1)} %collective-permute-done.refs_0_, bf16[280,128]{1,0:T(8,128)(2,1)S(1)} %collective-permute-done.1.refs_1_, ...), custom_call_target="tpu_custom_call" | custom-call | tf_op jit(solution)/shard_map/pallas_call | solution.py:65
  14.5 0.8 %collective-permute-done.5.got_ref = bf16[256,128]{1,0:T(8,128)(2,1)S(1)} collective-permute-done((bf16[256,128]{1,0:T(8,128)(2,1)S(1)}, bf16[256,128]{1,0:T(8,128)(2,1)S(1)}, u32[]{:S(2)}, u32[]{:S(2)}) %collective-permute-start.5) | collective-permute-done | bytes 65568 | tf_op jit(solution)/shard_map/ppermute | solution.py:271
  15.3 1.6 %collective-permute-start.6 = (bf16[256,128]{1,0:T(8,128)(2,1)S(1)}, bf16[256,128]{1,0:T(8,128)(2,1)S(1)}, u32[]{:S(2)}, u32[]{:S(2)}) collective-permute-start(bf16[256,128]{1,0:T(8,128)(2,1)S(1)} %get-tuple-element.50), channel_id=1, source_target_pairs={{0,2},{1,3},{2,0},{3,1},{4,6},{5,7},{6,4},{7,5},{8,10},{9,11},{10,... | collective-permute-start | bytes 196616 | tf_op jit(solution)/shard_map/ppermute | solution.py:271
  16.9 0.5 %collective-permute-start.7 = (f32[64,128]{1,0:T(8,128)S(1)}, f32[64,128]{1,0:T(8,128)S(1)}, u32[]{:S(2)}, u32[]{:S(2)}) collective-permute-start(f32[64,128]{1,0:T(8,128)S(1)} %get-tuple-element.51.refs_2_), channel_id=1, source_target_pairs={{0,2},{1,3},{2,0},{3,1},{4,6},{5,7},{6,4},{7,5},{8,10},{9,11},{10,... | collective-permute-start | bytes 98312 | tf_op jit(solution)/shard_map/ppermute | solution.py:271
  17.4 3.4 %collective-permute-done.7.refs_3_ = f32[64,128]{1,0:T(8,128)S(1)} collective-permute-done((f32[64,128]{1,0:T(8,128)S(1)}, f32[64,128]{1,0:T(8,128)S(1)}, u32[]{:S(2)}, u32[]{:S(2)}) %collective-permute-start.7) | collective-permute-done | bytes 32800 | tf_op jit(solution)/shard_map/ppermute | solution.py:271
  20.8 0.1 shard_map.78
  21.0 0.2 shard_map.79
  21.2 1.0 %collective-permute-done.8.refs_2_.refs_0_ = bf16[128,256]{1,0:T(8,128)(2,1)S(1)} collective-permute-done((bf16[128,256]{1,0:T(8,128)(2,1)S(1)}, bf16[128,256]{1,0:T(8,128)(2,1)S(1)}, u32[]{:S(2)}, u32[]{:S(2)}) %collective-permute-start.8) | collective-permute-done | bytes 65568 | tf_op jit(solution)/shard_map/ppermute | solution.py:271
  22.2 0.2 shard_map.83
  22.4 1.6 %collective-permute-start.11 = (bf16[128,256]{1,0:T(8,128)(2,1)S(1)}, bf16[128,256]{1,0:T(8,128)(2,1)S(1)}, u32[]{:S(2)}, u32[]{:S(2)}) collective-permute-start(bf16[128,256]{1,0:T(8,128)(2,1)S(1)} %shard_map.83), channel_id=1, source_target_pairs={{0,4},{4,0},{8,12},{12,8},{1,5},{5,1},{9,13},{13,9},{2,6},{6,2},{1... | collective-permute-start | bytes 196616 | tf_op jit(solution)/shard_map/ppermute | solution.py:274
  24.0 0.2 shard_map.82
  24.2 2.1 %collective-permute-start.10 = (bf16[128,256]{1,0:T(8,128)(2,1)S(1)}, bf16[128,256]{1,0:T(8,128)(2,1)S(1)}, u32[]{:S(2)}, u32[]{:S(2)}) collective-permute-start(bf16[128,256]{1,0:T(8,128)(2,1)S(1)} %shard_map.82), channel_id=1, source_target_pairs={{0,12},{4,8},{8,0},{12,4},{1,13},{5,9},{9,1},{13,5},{2,14},{6,10},... | collective-permute-start | bytes 196616 | tf_op jit(solution)/shard_map/ppermute | solution.py:274
  26.2 0.2 shard_map.81
  26.4 1.0 %collective-permute-start.9 = (bf16[128,256]{1,0:T(8,128)(2,1)S(1)}, bf16[128,256]{1,0:T(8,128)(2,1)S(1)}, u32[]{:S(2)}, u32[]{:S(2)}) collective-permute-start(bf16[128,256]{1,0:T(8,128)(2,1)S(1)} %shard_map.81), channel_id=1, source_target_pairs={{0,8},{4,12},{8,4},{12,0},{1,9},{5,13},{9,5},{13,1},{2,10},{6,14},... | collective-permute-start | bytes 196616 | tf_op jit(solution)/shard_map/ppermute | solution.py:274
  27.4 0.2 shard_map.80
  27.5 0.6 %copy.7 = f32[64,128]{1,0:T(8,128)} copy(f32[64,128]{1,0:T(8,128)S(1)} %get-tuple-element.77) | data formatting | bytes 65536
  28.1 3.5 %collective-permute-done.10.refs_2_ = bf16[128,256]{1,0:T(8,128)(2,1)S(1)} collective-permute-done((bf16[128,256]{1,0:T(8,128)(2,1)S(1)}, bf16[128,256]{1,0:T(8,128)(2,1)S(1)}, u32[]{:S(2)}, u32[]{:S(2)}) %collective-permute-start.10) | collective-permute-done | bytes 65568 | tf_op jit(solution)/shard_map/ppermute | solution.py:274
  31.6 1.0 %collective-permute-done.9.refs_1_ = bf16[128,256]{1,0:T(8,128)(2,1)S(1)} collective-permute-done((bf16[128,256]{1,0:T(8,128)(2,1)S(1)}, bf16[128,256]{1,0:T(8,128)(2,1)S(1)}, u32[]{:S(2)}, u32[]{:S(2)}) %collective-permute-start.9) | collective-permute-done | bytes 65568 | tf_op jit(solution)/shard_map/ppermute | solution.py:274
  32.6 0.7 %shard_map.84 = bf16[256,128]{1,0:T(8,128)(2,1)} custom-call(f32[128,256]{1,0:T(8,128)S(1)} %get-tuple-element.65.refs_0_, bf16[128,256]{1,0:T(8,128)(2,1)S(1)} %collective-permute-done.9.refs_1_, bf16[128,256]{1,0:T(8,128)(2,1)S(1)} %collective-permute-done.10.refs_2_, bf16[128,256]{1,0:T(8,128)(2,1)S(1)} %collective-permute-done.11.refs_3_), custom_call_target="tpu_custom_call" | custom-call | tf_op jit(solution)/shard_map/pallas_call | solution.py:65
  (12 shorter events, 0.3 us)
Async XLA Ops:
  1.5 11.1 %collective-permute-start.4 = (bf16[280,128]{1,0:T(8,128)(2,1)S(1)}, bf16[280,128]{1,0:T(8,128)(2,1)S(1)}, u32[]{:S(2)}, u32[]{:S(2)}) collective-permute-start(bf16[280,128]{1,0:T(8,128)(2,1)S(1)} %get-tuple-element.39.refs_0_), channel_id=1, source_target_pairs={{0,4},{4,8},{8,12},{12,0},{1,5},{5,9},{9,13},{13,1},{2,6},{6,10},{... | collective-permute-start | bytes 215048 | tf_op jit(solution)/shard_map/ppermute | solution.py:274
  4.6 8.8 %collective-permute-start = (bf16[280,128]{1,0:T(8,128)(2,1)S(1)}, bf16[280,128]{1,0:T(8,128)(2,1)S(1)}, u32[]{:S(2)}, u32[]{:S(2)}) collective-permute-start(bf16[280,128]{1,0:T(8,128)(2,1)S(1)} %get-tuple-element.39.refs_0_), channel_id=1, source_target_pairs={{0,12},{4,0},{8,4},{12,8},{1,13},{5,1},{9,5},{13,9},{2,14},{6,2},{... | collective-permute-start | bytes 215048 | tf_op jit(solution)/shard_map/ppermute | solution.py:274
  6.7 6.8 %collective-permute-start.1 = (bf16[280,128]{1,0:T(8,128)(2,1)S(1)}, bf16[280,128]{1,0:T(8,128)(2,1)S(1)}, u32[]{:S(2)}, u32[]{:S(2)}) collective-permute-start(bf16[280,128]{1,0:T(8,128)(2,1)S(1)} %get-tuple-element.39.refs_0_), channel_id=1, source_target_pairs={{0,8},{4,12},{8,0},{12,4},{1,9},{5,13},{9,1},{13,5},{2,10},{6,14},... | collective-permute-start | bytes 215048 | tf_op jit(solution)/shard_map/ppermute | solution.py:274
  7.7 1.2 %collective-permute-start.2 = (f32[8,128]{1,0:T(8,128)S(1)}, f32[8,128]{1,0:T(8,128)S(1)}, u32[]{:S(2)}, u32[]{:S(2)}) collective-permute-start(f32[8,128]{1,0:T(8,128)S(1)} %get-tuple-element.40.own_ref), channel_id=1, source_target_pairs={{0,1},{1,0},{2,3},{3,2},{4,5},{5,4},{6,7},{7,6},{8,9},{9,8},{10,11... | collective-permute-start | bytes 12296 | tf_op jit(solution)/shard_map/ppermute | solution.py:271
  8.9 3.7 %collective-permute-start.3 = (f32[16,128]{1,0:T(8,128)S(1)}, f32[16,128]{1,0:T(8,128)S(1)}, u32[]{:S(2)}, u32[]{:S(2)}) collective-permute-start(f32[16,128]{1,0:T(8,128)S(1)} %shard_map.69.refs_0_), channel_id=1, source_target_pairs={{0,2},{1,3},{2,0},{3,1},{4,6},{5,7},{6,4},{7,5},{8,10},{9,11},{10,... | collective-permute-start | bytes 24584 | tf_op jit(solution)/shard_map/ppermute | solution.py:271
  14.0 1.3 %collective-permute-start.5 = (bf16[256,128]{1,0:T(8,128)(2,1)S(1)}, bf16[256,128]{1,0:T(8,128)(2,1)S(1)}, u32[]{:S(2)}, u32[]{:S(2)}) collective-permute-start(bf16[256,128]{1,0:T(8,128)(2,1)S(1)} %get-tuple-element.48), channel_id=1, source_target_pairs={{0,1},{1,0},{2,3},{3,2},{4,5},{5,4},{6,7},{7,6},{8,9},{9,8},{10,11... | collective-permute-start | bytes 196616 | tf_op jit(solution)/shard_map/ppermute | solution.py:271
  15.3 5.5 %collective-permute-start.6 = (bf16[256,128]{1,0:T(8,128)(2,1)S(1)}, bf16[256,128]{1,0:T(8,128)(2,1)S(1)}, u32[]{:S(2)}, u32[]{:S(2)}) collective-permute-start(bf16[256,128]{1,0:T(8,128)(2,1)S(1)} %get-tuple-element.50), channel_id=1, source_target_pairs={{0,2},{1,3},{2,0},{3,1},{4,6},{5,7},{6,4},{7,5},{8,10},{9,11},{10,... | collective-permute-start | bytes 196616 | tf_op jit(solution)/shard_map/ppermute | solution.py:271
  16.9 3.9 %collective-permute-start.7 = (f32[64,128]{1,0:T(8,128)S(1)}, f32[64,128]{1,0:T(8,128)S(1)}, u32[]{:S(2)}, u32[]{:S(2)}) collective-permute-start(f32[64,128]{1,0:T(8,128)S(1)} %get-tuple-element.51.refs_2_), channel_id=1, source_target_pairs={{0,2},{1,3},{2,0},{3,1},{4,6},{5,7},{6,4},{7,5},{8,10},{9,11},{10,... | collective-permute-start | bytes 98312 | tf_op jit(solution)/shard_map/ppermute | solution.py:271
  20.9 1.3 %collective-permute-start.8 = (bf16[128,256]{1,0:T(8,128)(2,1)S(1)}, bf16[128,256]{1,0:T(8,128)(2,1)S(1)}, u32[]{:S(2)}, u32[]{:S(2)}) collective-permute-start(bf16[128,256]{1,0:T(8,128)(2,1)S(1)} %get-tuple-element.53.refs_0_), channel_id=1, source_target_pairs={{0,1},{1,0},{2,3},{3,2},{4,5},{5,4},{6,7},{7,6},{8,9},{9,8},{10,11... | collective-permute-start | bytes 196616 | tf_op jit(solution)/shard_map/ppermute | solution.py:271
  22.4 5.8 %collective-permute-start.11 = (bf16[128,256]{1,0:T(8,128)(2,1)S(1)}, bf16[128,256]{1,0:T(8,128)(2,1)S(1)}, u32[]{:S(2)}, u32[]{:S(2)}) collective-permute-start(bf16[128,256]{1,0:T(8,128)(2,1)S(1)} %shard_map.83), channel_id=1, source_target_pairs={{0,4},{4,0},{8,12},{12,8},{1,5},{5,1},{9,13},{13,9},{2,6},{6,2},{1... | collective-permute-start | bytes 196616 | tf_op jit(solution)/shard_map/ppermute | solution.py:274
  24.1 3.2 %copy-start = (f32[2,64,128]{2,1,0:T(8,128)S(1)}, f32[2,64,128]{2,1,0:T(8,128)}, u32[]{:S(2)}) copy-start(f32[2,64,128]{2,1,0:T(8,128)} %refs_1_.1) | copy-start | bytes 196612
  24.2 7.5 %collective-permute-start.10 = (bf16[128,256]{1,0:T(8,128)(2,1)S(1)}, bf16[128,256]{1,0:T(8,128)(2,1)S(1)}, u32[]{:S(2)}, u32[]{:S(2)}) collective-permute-start(bf16[128,256]{1,0:T(8,128)(2,1)S(1)} %shard_map.82), channel_id=1, source_target_pairs={{0,12},{4,8},{8,0},{12,4},{1,13},{5,9},{9,1},{13,5},{2,14},{6,10},... | collective-permute-start | bytes 196616 | tf_op jit(solution)/shard_map/ppermute | solution.py:274
  26.4 6.2 %collective-permute-start.9 = (bf16[128,256]{1,0:T(8,128)(2,1)S(1)}, bf16[128,256]{1,0:T(8,128)(2,1)S(1)}, u32[]{:S(2)}, u32[]{:S(2)}) collective-permute-start(bf16[128,256]{1,0:T(8,128)(2,1)S(1)} %shard_map.81), channel_id=1, source_target_pairs={{0,8},{4,12},{8,4},{12,0},{1,9},{5,13},{9,5},{13,1},{2,10},{6,14},... | collective-permute-start | bytes 196616 | tf_op jit(solution)/shard_map/ppermute | solution.py:274

commit v9 on v6

--- a/solution.py
+++ b/solution.py
@@ -281,7 +281,7 @@
     flips = list(range(2, nq, 2))
     zb = {0: zbuf}
     for d in ring:
-        zb[d] = send(zbuf, [(i - d) % nz for i in range(nz)])
+        zb[d] = send(zbuf, ring_shift(nz, -d))
     (cores,) = run(join_body, [shape((16, width), f32)], wide, swap(wide, 1))
     lats = [cores] + [swap(cores, s) for s in flips]
     fils = [filters] + [swap(filters, s) for s in flips]
@@ -344,10 +344,9 @@
     )
     parts = dict(zip(order, parts))
     landed = []
-    for targets in reduce_rounds(nz):
-        planes = {}
-        for i, target in enumerate(targets):
-            planes.setdefault((target - i) % nz, []).append(i)
+    for k in range(nz - 1):
+        targets = ring_shift(nz, k + 1)
+        planes = {k + 1: None}
         (node,) = run(
             lambda *refs: node_body(half, list(planes.values()), *refs),
             [shape((width, natom), bf16)],
@@ -375,15 +374,15 @@
 
 
 def gather_order(nz):
-    return list(range(nz - 1, 0, -1))
-
-
-def reduce_rounds(nz):
+    return sorted(range(1, nz), key=lambda d: (-min(d, nz - d), d))
+
+
+def ring_shift(nz, by):
     ring = list(range(nz))
     if nz <= 4:
         ring = ring[:1] + ring[1::2] + ring[2::2][::-1]
     place = {z: i for i, z in enumerate(ring)}
-    return [[ring[(place[z] + by) % nz] for z in range(nz)] for by in range(1, nz)]
+    return [ring[(place[z] + by) % nz] for z in range(nz)]
 
 
 def solution(mesh):

time: 33.3 us -> 33.6 us (level)
  local copies, waits for them, and re-layouts: 0.63 us -> 1.23 us
    unnamed x3, local copies, waits for them, and re-layouts: 0.63 us -> 1.23 us
  transfers between devices with their start and end apart: 12 -> 12, of which waited for: 8 -> 7; matrix products, arithmetic and copies ran while one was open for 2% -> 2% of each run, Pallas kernels for 8% -> 7%
where the time goes in v9:
time: 33.6 us; the launch traced here: 33.3 us
  starting transfers between devices  13.9 us (41%)
  waiting for transfers between devices  12.5 us (37%)
  Pallas kernels  4.86 us (14%)
  local copies, waits for them, and re-layouts  1.23 us (4%)
  between operations  0.78 us (2%)
    ppermute x6, starting transfers between devices, send(): return lax.ppermute(value, 'atoms', list(enumerate(targets)))  10.2 us
    ppermute x6, waiting for transfers between devices, swap(): return lax.ppermute(value, 'kvec', [(i, i ^ flip) for i in range(nq)])  8.05 us
    ppermute x6, waiting for transfers between devices, send(): return lax.ppermute(value, 'atoms', list(enumerate(targets)))  4.5 us
    pallas_call x16, Pallas kernels, call(): pl.pallas_call(body, out_shape=outs, in_specs=full_spec(len(args)), out_s...  3.95 us
    ppermute x6, starting transfers between devices, swap(): return lax.ppermute(value, 'kvec', [(i, i ^ flip) for i in range(nq)])  3.73 us
    unnamed x3, local copies, waits for them, and re-layouts  1.23 us
    pallas_call x1, Pallas kernels, pack(): pl.pallas_call(pack_body, out_shape=outs, in_specs=[pl.BlockSpec(memory_s...  0.9 us
  transfers between devices with their start and end apart: 12, of which 7 were waited for; matrix products, arithmetic and copies ran while one was open for 2% of the time, Pallas kernels for 7%

profile of v9, /device:TPU:0, one launch (start us, length us, event | category | flops | bytes accessed | tf_op | source)
XLA Modules:
  0.0 33.3 jit_solution(18303048919744237986)
XLA Ops:
  0.6 0.9 %shard_map.68 = (bf16[280,128]{1,0:T(8,128)(2,1)S(1)}, f32[8,128]{1,0:T(8,128)S(1)}, f32[64,128]{1,0:T(8,128)S(1)}) custom-call(s32[3,64]{1,0:T(4,128)} %lat_hbm.1, f32[3,256]{1,0:T(4,128)} %pos_hbm.1, bf16[256,128]{1,0:T(8,128)(2,1)} %cot_hbm.1, f32[64,128]{1,0:T(8,128)} %fil_hbm.1), custom_call_target="tpu_custom_call" | custom-call | tf_op jit(solution)/shard_map/pallas_call | solution.py:116
  1.5 5.1 %collective-permute-start.4 = (bf16[280,128]{1,0:T(8,128)(2,1)S(1)}, bf16[280,128]{1,0:T(8,128)(2,1)S(1)}, u32[]{:S(2)}, u32[]{:S(2)}) collective-permute-start(bf16[280,128]{1,0:T(8,128)(2,1)S(1)} %get-tuple-element.39.refs_0_), channel_id=1, source_target_pairs={{0,12},{4,8},{8,4},{12,0},{1,13},{5,9},{9,5},{13,1},{2,14},{6,10},... | collective-permute-start | bytes 215048 | tf_op jit(solution)/shard_map/ppermute | solution.py:274
  6.7 2.0 %collective-permute-start.1 = (bf16[280,128]{1,0:T(8,128)(2,1)S(1)}, bf16[280,128]{1,0:T(8,128)(2,1)S(1)}, u32[]{:S(2)}, u32[]{:S(2)}) collective-permute-start(bf16[280,128]{1,0:T(8,128)(2,1)S(1)} %get-tuple-element.39.refs_0_), channel_id=1, source_target_pairs={{0,4},{4,12},{8,0},{12,8},{1,5},{5,13},{9,1},{13,9},{2,6},{6,14},{... | collective-permute-start | bytes 215048 | tf_op jit(solution)/shard_map/ppermute | solution.py:274
  8.7 1.2 %collective-permute-done.2.got_ref = f32[8,128]{1,0:T(8,128)S(1)} collective-permute-done((f32[8,128]{1,0:T(8,128)S(1)}, f32[8,128]{1,0:T(8,128)S(1)}, u32[]{:S(2)}, u32[]{:S(2)}) %collective-permute-start.2) | collective-permute-done | bytes 4128 | tf_op jit(solution)/shard_map/ppermute | solution.py:271
  9.9 1.5 %collective-permute-start.3 = (f32[16,128]{1,0:T(8,128)S(1)}, f32[16,128]{1,0:T(8,128)S(1)}, u32[]{:S(2)}, u32[]{:S(2)}) collective-permute-start(f32[16,128]{1,0:T(8,128)S(1)} %shard_map.69.refs_0_), channel_id=1, source_target_pairs={{0,2},{1,3},{2,0},{3,1},{4,6},{5,7},{6,4},{7,5},{8,10},{9,11},{10,... | collective-permute-start | bytes 24584 | tf_op jit(solution)/shard_map/ppermute | solution.py:271
  11.4 0.1 shard_map.70.refs_1_.refs_2_
  11.5 0.3 shard_map.72
  11.8 1.7 %collective-permute-done.3.refs_0_ = f32[16,128]{1,0:T(8,128)S(1)} collective-permute-done((f32[16,128]{1,0:T(8,128)S(1)}, f32[16,128]{1,0:T(8,128)S(1)}, u32[]{:S(2)}, u32[]{:S(2)}) %collective-permute-start.3) | collective-permute-done | bytes 8224 | tf_op jit(solution)/shard_map/ppermute | solution.py:271
  13.5 0.1 shard_map.71.refs_2_.refs_3_
  13.6 0.5 %shard_map.74 = (bf16[128,256]{1,0:T(8,128)(2,1)S(1)}, bf16[128,256]{1,0:T(8,128)(2,1)S(1)}, bf16[128,256]{1,0:T(8,128)(2,1)S(1)}, bf16[128,256]{1,0:T(8,128)(2,...) custom-call(bf16[280,128]{1,0:T(8,128)(2,1)S(1)} %get-tuple-element.39.refs_0_, ...), custom_call_target="tpu_custom_call" | custom-call | tf_op jit(solution)/shard_map/pallas_call | solution.py:65
  14.1 0.3 shard_map.73
  14.5 0.5 %shard_map.76 = (bf16[128,256]{1,0:T(8,128)(2,1)S(1)}, bf16[128,256]{1,0:T(8,128)(2,1)S(1)}, bf16[128,256]{1,0:T(8,128)(2,1)S(1)}, bf16[128,256]{1,0:T(8,128)(2,1)S(1)}, bf16[256,128]{1,0:T(8,128)(2,1)S(1)}) custom-call(bf16[280,128]{1,0:T(8,128)(2,1)S(1)} %collective-permute-done.refs_0_, bf16[280,128]{1,0:T(8,128)(2,1)S(1)} %collective-permute-done.1.refs_1_, ...), custom_call_target="tpu_custom_call" | custom-call | tf_op jit(solution)/shard_map/pallas_call | solution.py:65
  14.9 0.1 collective-permute-start.5
  15.0 0.5 %shard_map.75 = (bf16[128,256]{1,0:T(8,128)(2,1)S(1)}, bf16[128,256]{1,0:T(8,128)(2,1)S(1)}, bf16[128,256]{1,0:T(8,128)(2,1)S(1)}, bf16[128,256]{1,0:T(8,128)(2,1)S(1)}, f32[256,128]{1,0:T(8,128)S(1)}) custom-call(bf16[280,128]{1,0:T(8,128)(2,1)S(1)} %collective-permute-done.refs_0_, bf16[280,128]{1,0:T(8,128)(2,1)S(1)} %collective-permute-done.1.refs_1_, ...), custom_call_target="tpu_custom_call" | custom-call | tf_op jit(solution)/shard_map/pallas_call | solution.py:65
  15.5 0.8 %collective-permute-done.5.got_ref = bf16[256,128]{1,0:T(8,128)(2,1)S(1)} collective-permute-done((bf16[256,128]{1,0:T(8,128)(2,1)S(1)}, bf16[256,128]{1,0:T(8,128)(2,1)S(1)}, u32[]{:S(2)}, u32[]{:S(2)}) %collective-permute-start.5) | collective-permute-done | bytes 65568 | tf_op jit(solution)/shard_map/ppermute | solution.py:271
  16.3 1.6 %collective-permute-start.6 = (bf16[256,128]{1,0:T(8,128)(2,1)S(1)}, bf16[256,128]{1,0:T(8,128)(2,1)S(1)}, u32[]{:S(2)}, u32[]{:S(2)}) collective-permute-start(bf16[256,128]{1,0:T(8,128)(2,1)S(1)} %get-tuple-element.50), channel_id=1, source_target_pairs={{0,2},{1,3},{2,0},{3,1},{4,6},{5,7},{6,4},{7,5},{8,10},{9,11},{10,... | collective-permute-start | bytes 196616 | tf_op jit(solution)/shard_map/ppermute | solution.py:271
  17.8 0.5 %collective-permute-start.7 = (f32[64,128]{1,0:T(8,128)S(1)}, f32[64,128]{1,0:T(8,128)S(1)}, u32[]{:S(2)}, u32[]{:S(2)}) collective-permute-start(f32[64,128]{1,0:T(8,128)S(1)} %get-tuple-element.51.refs_2_), channel_id=1, source_target_pairs={{0,2},{1,3},{2,0},{3,1},{4,6},{5,7},{6,4},{7,5},{8,10},{9,11},{10,... | collective-permute-start | bytes 98312 | tf_op jit(solution)/shard_map/ppermute | solution.py:271
  18.4 3.4 %collective-permute-done.7.refs_3_ = f32[64,128]{1,0:T(8,128)S(1)} collective-permute-done((f32[64,128]{1,0:T(8,128)S(1)}, f32[64,128]{1,0:T(8,128)S(1)}, u32[]{:S(2)}, u32[]{:S(2)}) %collective-permute-start.7) | collective-permute-done | bytes 32800 | tf_op jit(solution)/shard_map/ppermute | solution.py:271
  21.8 0.1 shard_map.78
  21.9 0.2 shard_map.79
  22.2 1.0 %collective-permute-done.8.refs_2_.refs_0_ = bf16[128,256]{1,0:T(8,128)(2,1)S(1)} collective-permute-done((bf16[128,256]{1,0:T(8,128)(2,1)S(1)}, bf16[128,256]{1,0:T(8,128)(2,1)S(1)}, u32[]{:S(2)}, u32[]{:S(2)}) %collective-permute-start.8) | collective-permute-done | bytes 65568 | tf_op jit(solution)/shard_map/ppermute | solution.py:271
  23.2 0.2 shard_map.83
  23.3 1.0 %collective-permute-start.11 = (bf16[128,256]{1,0:T(8,128)(2,1)S(1)}, bf16[128,256]{1,0:T(8,128)(2,1)S(1)}, u32[]{:S(2)}, u32[]{:S(2)}) collective-permute-start(bf16[128,256]{1,0:T(8,128)(2,1)S(1)} %shard_map.83), channel_id=1, source_target_pairs={{0,8},{4,0},{8,12},{12,4},{1,9},{5,1},{9,13},{13,5},{2,10},{6,2},{... | collective-permute-start | bytes 196616 | tf_op jit(solution)/shard_map/ppermute | solution.py:274
  24.3 0.2 shard_map.82
  24.5 2.0 %collective-permute-start.10 = (bf16[128,256]{1,0:T(8,128)(2,1)S(1)}, bf16[128,256]{1,0:T(8,128)(2,1)S(1)}, u32[]{:S(2)}, u32[]{:S(2)}) collective-permute-start(bf16[128,256]{1,0:T(8,128)(2,1)S(1)} %shard_map.82), channel_id=1, source_target_pairs={{0,12},{4,8},{8,4},{12,0},{1,13},{5,9},{9,5},{13,1},{2,14},{6,10},... | collective-permute-start | bytes 196616 | tf_op jit(solution)/shard_map/ppermute | solution.py:274
  26.4 0.2 shard_map.81
  26.7 0.6 %copy-done = f32[2,64,128]{2,1,0:T(8,128)S(1)} copy-done((f32[2,64,128]{2,1,0:T(8,128)S(1)}, f32[2,64,128]{2,1,0:T(8,128)}, u32[]{:S(2)}) %copy-start) | copy-done | bytes 65560
  27.3 0.2 shard_map.80
  27.4 0.6 %copy.7 = f32[64,128]{1,0:T(8,128)} copy(f32[64,128]{1,0:T(8,128)S(1)} %get-tuple-element.77) | data formatting | bytes 65536
  28.1 2.8 %collective-permute-done.10.refs_2_ = bf16[128,256]{1,0:T(8,128)(2,1)S(1)} collective-permute-done((bf16[128,256]{1,0:T(8,128)(2,1)S(1)}, bf16[128,256]{1,0:T(8,128)(2,1)S(1)}, u32[]{:S(2)}, u32[]{:S(2)}) %collective-permute-start.10) | collective-permute-done | bytes 65568 | tf_op jit(solution)/shard_map/ppermute | solution.py:274
  30.9 1.6 %collective-permute-done.9.refs_1_ = bf16[128,256]{1,0:T(8,128)(2,1)S(1)} collective-permute-done((bf16[128,256]{1,0:T(8,128)(2,1)S(1)}, bf16[128,256]{1,0:T(8,128)(2,1)S(1)}, u32[]{:S(2)}, u32[]{:S(2)}) %collective-permute-start.9) | collective-permute-done | bytes 65568 | tf_op jit(solution)/shard_map/ppermute | solution.py:274
  32.6 0.7 %shard_map.84 = bf16[256,128]{1,0:T(8,128)(2,1)} custom-call(f32[128,256]{1,0:T(8,128)S(1)} %get-tuple-element.65.refs_0_, bf16[128,256]{1,0:T(8,128)(2,1)S(1)} %collective-permute-done.9.refs_1_, bf16[128,256]{1,0:T(8,128)(2,1)S(1)} %collective-permute-done.10.refs_2_, bf16[128,256]{1,0:T(8,128)(2,1)S(1)} %collective-permute-done.11.refs_3_), custom_call_target="tpu_custom_call" | custom-call | tf_op jit(solution)/shard_map/pallas_call | solution.py:65
  (12 shorter events, 0.2 us)
Async XLA Ops:
  1.5 12.1 %collective-permute-start.4 = (bf16[280,128]{1,0:T(8,128)(2,1)S(1)}, bf16[280,128]{1,0:T(8,128)(2,1)S(1)}, u32[]{:S(2)}, u32[]{:S(2)}) collective-permute-start(bf16[280,128]{1,0:T(8,128)(2,1)S(1)} %get-tuple-element.39.refs_0_), channel_id=1, source_target_pairs={{0,12},{4,8},{8,4},{12,0},{1,13},{5,9},{9,5},{13,1},{2,14},{6,10},... | collective-permute-start | bytes 215048 | tf_op jit(solution)/shard_map/ppermute | solution.py:274
  6.7 7.8 %collective-permute-start = (bf16[280,128]{1,0:T(8,128)(2,1)S(1)}, bf16[280,128]{1,0:T(8,128)(2,1)S(1)}, u32[]{:S(2)}, u32[]{:S(2)}) collective-permute-start(bf16[280,128]{1,0:T(8,128)(2,1)S(1)} %get-tuple-element.39.refs_0_), channel_id=1, source_target_pairs={{0,8},{4,0},{8,12},{12,4},{1,9},{5,1},{9,13},{13,5},{2,10},{6,2},{... | collective-permute-start | bytes 215048 | tf_op jit(solution)/shard_map/ppermute | solution.py:274
  6.7 7.8 %collective-permute-start.1 = (bf16[280,128]{1,0:T(8,128)(2,1)S(1)}, bf16[280,128]{1,0:T(8,128)(2,1)S(1)}, u32[]{:S(2)}, u32[]{:S(2)}) collective-permute-start(bf16[280,128]{1,0:T(8,128)(2,1)S(1)} %get-tuple-element.39.refs_0_), channel_id=1, source_target_pairs={{0,4},{4,12},{8,0},{12,8},{1,5},{5,13},{9,1},{13,9},{2,6},{6,14},{... | collective-permute-start | bytes 215048 | tf_op jit(solution)/shard_map/ppermute | solution.py:274
  8.7 1.2 %collective-permute-start.2 = (f32[8,128]{1,0:T(8,128)S(1)}, f32[8,128]{1,0:T(8,128)S(1)}, u32[]{:S(2)}, u32[]{:S(2)}) collective-permute-start(f32[8,128]{1,0:T(8,128)S(1)} %get-tuple-element.40.own_ref), channel_id=1, source_target_pairs={{0,1},{1,0},{2,3},{3,2},{4,5},{5,4},{6,7},{7,6},{8,9},{9,8},{10,11... | collective-permute-start | bytes 12296 | tf_op jit(solution)/shard_map/ppermute | solution.py:271
  9.9 3.7 %collective-permute-start.3 = (f32[16,128]{1,0:T(8,128)S(1)}, f32[16,128]{1,0:T(8,128)S(1)}, u32[]{:S(2)}, u32[]{:S(2)}) collective-permute-start(f32[16,128]{1,0:T(8,128)S(1)} %shard_map.69.refs_0_), channel_id=1, source_target_pairs={{0,2},{1,3},{2,0},{3,1},{4,6},{5,7},{6,4},{7,5},{8,10},{9,11},{10,... | collective-permute-start | bytes 24584 | tf_op jit(solution)/shard_map/ppermute | solution.py:271
  14.9 1.3 %collective-permute-start.5 = (bf16[256,128]{1,0:T(8,128)(2,1)S(1)}, bf16[256,128]{1,0:T(8,128)(2,1)S(1)}, u32[]{:S(2)}, u32[]{:S(2)}) collective-permute-start(bf16[256,128]{1,0:T(8,128)(2,1)S(1)} %get-tuple-element.48), channel_id=1, source_target_pairs={{0,1},{1,0},{2,3},{3,2},{4,5},{5,4},{6,7},{7,6},{8,9},{9,8},{10,11... | collective-permute-start | bytes 196616 | tf_op jit(solution)/shard_map/ppermute | solution.py:271
  16.3 5.5 %collective-permute-start.6 = (bf16[256,128]{1,0:T(8,128)(2,1)S(1)}, bf16[256,128]{1,0:T(8,128)(2,1)S(1)}, u32[]{:S(2)}, u32[]{:S(2)}) collective-permute-start(bf16[256,128]{1,0:T(8,128)(2,1)S(1)} %get-tuple-element.50), channel_id=1, source_target_pairs={{0,2},{1,3},{2,0},{3,1},{4,6},{5,7},{6,4},{7,5},{8,10},{9,11},{10,... | collective-permute-start | bytes 196616 | tf_op jit(solution)/shard_map/ppermute | solution.py:271
  17.8 3.9 %collective-permute-start.7 = (f32[64,128]{1,0:T(8,128)S(1)}, f32[64,128]{1,0:T(8,128)S(1)}, u32[]{:S(2)}, u32[]{:S(2)}) collective-permute-start(f32[64,128]{1,0:T(8,128)S(1)} %get-tuple-element.51.refs_2_), channel_id=1, source_target_pairs={{0,2},{1,3},{2,0},{3,1},{4,6},{5,7},{6,4},{7,5},{8,10},{9,11},{10,... | collective-permute-start | bytes 98312 | tf_op jit(solution)/shard_map/ppermute | solution.py:271
  21.9 1.3 %collective-permute-start.8 = (bf16[128,256]{1,0:T(8,128)(2,1)S(1)}, bf16[128,256]{1,0:T(8,128)(2,1)S(1)}, u32[]{:S(2)}, u32[]{:S(2)}) collective-permute-start(bf16[128,256]{1,0:T(8,128)(2,1)S(1)} %get-tuple-element.53.refs_0_), channel_id=1, source_target_pairs={{0,1},{1,0},{2,3},{3,2},{4,5},{5,4},{6,7},{7,6},{8,9},{9,8},{10,11... | collective-permute-start | bytes 196616 | tf_op jit(solution)/shard_map/ppermute | solution.py:271
  23.3 4.7 %collective-permute-start.11 = (bf16[128,256]{1,0:T(8,128)(2,1)S(1)}, bf16[128,256]{1,0:T(8,128)(2,1)S(1)}, u32[]{:S(2)}, u32[]{:S(2)}) collective-permute-start(bf16[128,256]{1,0:T(8,128)(2,1)S(1)} %shard_map.83), channel_id=1, source_target_pairs={{0,8},{4,0},{8,12},{12,4},{1,9},{5,1},{9,13},{13,5},{2,10},{6,2},{... | collective-permute-start | bytes 196616 | tf_op jit(solution)/shard_map/ppermute | solution.py:274
  24.5 6.4 %collective-permute-start.10 = (bf16[128,256]{1,0:T(8,128)(2,1)S(1)}, bf16[128,256]{1,0:T(8,128)(2,1)S(1)}, u32[]{:S(2)}, u32[]{:S(2)}) collective-permute-start(bf16[128,256]{1,0:T(8,128)(2,1)S(1)} %shard_map.82), channel_id=1, source_target_pairs={{0,12},{4,8},{8,4},{12,0},{1,13},{5,9},{9,5},{13,1},{2,14},{6,10},... | collective-permute-start | bytes 196616 | tf_op jit(solution)/shard_map/ppermute | solution.py:274
  26.4 0.8 %copy-start = (f32[2,64,128]{2,1,0:T(8,128)S(1)}, f32[2,64,128]{2,1,0:T(8,128)}, u32[]{:S(2)}) copy-start(f32[2,64,128]{2,1,0:T(8,128)} %refs_1_.1) | copy-start | bytes 196612
  26.6 5.9 %collective-permute-start.9 = (bf16[128,256]{1,0:T(8,128)(2,1)S(1)}, bf16[128,256]{1,0:T(8,128)(2,1)S(1)}, u32[]{:S(2)}, u32[]{:S(2)}) collective-permute-start(bf16[128,256]{1,0:T(8,128)(2,1)S(1)} %shard_map.81), channel_id=1, source_target_pairs={{0,4},{4,12},{8,0},{12,8},{1,5},{5,13},{9,1},{13,9},{2,6},{6,14},{... | collective-permute-start | bytes 196616 | tf_op jit(solution)/shard_map/ppermute | solution.py:274

commit v10 on v6

--- a/solution.py
+++ b/solution.py
@@ -316,16 +316,19 @@
     for z in early:
         factor([z], [0, 1])
     for t in flips:
-        factor(early, [t, t + 1])
-    for z in order[len(early) : cut]:
+        factor(early, [t + 1])
+    between = order[len(early) : cut]
+    if between:
+        for t in flips:
+            factor(early, [t])
+    for z in between:
         factor([z], list(range(nq)))
     sent = factor(order[cut:], theirs, bf16)
+    for t in flips if not between else []:
+        factor(early, [t])
     kept = factor(order[cut:], mine, f32)
     pair, pair16 = run(
-        pair_body,
-        [shape((2 * count, width), f32), shape((2 * count, width), bf16)],
-        kept,
-        swap(sent, 1),
+        pair_body, [shape((2 * count, width), f32), shape((2 * count, width), bf16)], kept, swap(sent, 1)
     )
     got = [swap(pair16, s) for s in flips]
     weight, head = run(
@@ -365,11 +368,7 @@
         *[tiles[0, t] for t in theirs],
     )
     (node_grad,) = run(
-        lambda *refs: final_body(scale_k, *refs),
-        [shape((natom, width), bf16)],
-        own,
-        *landed,
-        keep_outs=False,
+        lambda *refs: final_body(scale_k, *refs), [shape((natom, width), bf16)], own, *landed, keep_outs=False
     )
     return (node_grad, filter_grad)
 

time: 33.3 us -> 33.3 us (level)
    ppermute x6, waiting for transfers between devices: 8.05 us -> 7.72 us  [swap(): return lax.ppermute(value, 'kvec', [(i, i ^ flip) for i in range(nq)])]
    pallas_call x16 -> x17, Pallas kernels: 3.97 us -> 4.16 us  [call(): pl.pallas_call(body, out_shape=outs, in_specs=full_spec(len(args)), out_s...]
where the time goes in v10:
time: 33.3 us; the launch traced here: 33 us
  starting transfers between devices  13.8 us (41%)
  waiting for transfers between devices  12.7 us (38%)
  Pallas kernels  5.06 us (15%)
  between operations  0.81 us (2%)
  local copies, waits for them, and re-layouts  0.62 us (2%)
    ppermute x6, starting transfers between devices, send(): return lax.ppermute(value, 'atoms', list(enumerate(targets)))  10 us
    ppermute x6, waiting for transfers between devices, swap(): return lax.ppermute(value, 'kvec', [(i, i ^ flip) for i in range(nq)])  7.72 us
    ppermute x6, waiting for transfers between devices, send(): return lax.ppermute(value, 'atoms', list(enumerate(targets)))  5 us
    pallas_call x17, Pallas kernels, call(): pl.pallas_call(body, out_shape=outs, in_specs=full_spec(len(args)), out_s...  4.16 us
    ppermute x6, starting transfers between devices, swap(): return lax.ppermute(value, 'kvec', [(i, i ^ flip) for i in range(nq)])  3.73 us
    pallas_call x1, Pallas kernels, pack(): pl.pallas_call(pack_body, out_shape=outs, in_specs=[pl.BlockSpec(memory_s...  0.9 us
  transfers between devices with their start and end apart: 12, of which 8 were waited for; matrix products, arithmetic and copies ran while one was open for 2% of the time, Pallas kernels for 8%

profile of v10, /device:TPU:0, one launch (start us, length us, event | category | flops | bytes accessed | tf_op | source)
XLA Modules:
  0.0 33.0 jit_solution(5560002625400683652)
XLA Ops:
  0.6 0.9 %shard_map.68 = (bf16[280,128]{1,0:T(8,128)(2,1)S(1)}, f32[8,128]{1,0:T(8,128)S(1)}, f32[64,128]{1,0:T(8,128)S(1)}) custom-call(s32[3,64]{1,0:T(4,128)} %lat_hbm.1, f32[3,256]{1,0:T(4,128)} %pos_hbm.1, bf16[256,128]{1,0:T(8,128)(2,1)} %cot_hbm.1, f32[64,128]{1,0:T(8,128)} %fil_hbm.1), custom_call_target="tpu_custom_call" | custom-call | tf_op jit(solution)/shard_map/pallas_call | solution.py:116
  1.5 3.1 %collective-permute-start.4 = (bf16[280,128]{1,0:T(8,128)(2,1)S(1)}, bf16[280,128]{1,0:T(8,128)(2,1)S(1)}, u32[]{:S(2)}, u32[]{:S(2)}) collective-permute-start(bf16[280,128]{1,0:T(8,128)(2,1)S(1)} %get-tuple-element.39.refs_0_), channel_id=1, source_target_pairs={{0,4},{4,8},{8,12},{12,0},{1,5},{5,9},{9,13},{13,1},{2,6},{6,10},{... | collective-permute-start | bytes 215048 | tf_op jit(solution)/shard_map/ppermute | solution.py:274
  4.6 2.1 %collective-permute-start = (bf16[280,128]{1,0:T(8,128)(2,1)S(1)}, bf16[280,128]{1,0:T(8,128)(2,1)S(1)}, u32[]{:S(2)}, u32[]{:S(2)}) collective-permute-start(bf16[280,128]{1,0:T(8,128)(2,1)S(1)} %get-tuple-element.39.refs_0_), channel_id=1, source_target_pairs={{0,12},{4,0},{8,4},{12,8},{1,13},{5,1},{9,5},{13,9},{2,14},{6,2},{... | collective-permute-start | bytes 215048 | tf_op jit(solution)/shard_map/ppermute | solution.py:274
  6.7 0.9 %collective-permute-start.1 = (bf16[280,128]{1,0:T(8,128)(2,1)S(1)}, bf16[280,128]{1,0:T(8,128)(2,1)S(1)}, u32[]{:S(2)}, u32[]{:S(2)}) collective-permute-start(bf16[280,128]{1,0:T(8,128)(2,1)S(1)} %get-tuple-element.39.refs_0_), channel_id=1, source_target_pairs={{0,8},{4,12},{8,0},{12,4},{1,9},{5,13},{9,1},{13,5},{2,10},{6,14},... | collective-permute-start | bytes 215048 | tf_op jit(solution)/shard_map/ppermute | solution.py:274
  7.7 1.2 %collective-permute-done.2.got_ref = f32[8,128]{1,0:T(8,128)S(1)} collective-permute-done((f32[8,128]{1,0:T(8,128)S(1)}, f32[8,128]{1,0:T(8,128)S(1)}, u32[]{:S(2)}, u32[]{:S(2)}) %collective-permute-start.2) | collective-permute-done | bytes 4128 | tf_op jit(solution)/shard_map/ppermute | solution.py:271
  8.9 1.5 %collective-permute-start.3 = (f32[16,128]{1,0:T(8,128)S(1)}, f32[16,128]{1,0:T(8,128)S(1)}, u32[]{:S(2)}, u32[]{:S(2)}) collective-permute-start(f32[16,128]{1,0:T(8,128)S(1)} %shard_map.69.refs_0_), channel_id=1, source_target_pairs={{0,2},{1,3},{2,0},{3,1},{4,6},{5,7},{6,4},{7,5},{8,10},{9,11},{10,... | collective-permute-start | bytes 24584 | tf_op jit(solution)/shard_map/ppermute | solution.py:271
  10.4 0.3 shard_map.72
  10.8 1.7 %collective-permute-done.3.refs_0_ = f32[16,128]{1,0:T(8,128)S(1)} collective-permute-done((f32[16,128]{1,0:T(8,128)S(1)}, f32[16,128]{1,0:T(8,128)S(1)}, u32[]{:S(2)}, u32[]{:S(2)}) %collective-permute-start.3) | collective-permute-done | bytes 8224 | tf_op jit(solution)/shard_map/ppermute | solution.py:271
  12.5 0.1 shard_map.71.refs_2_.refs_3_
  12.6 0.3 shard_map.76
  12.9 0.3 shard_map.73
  13.3 0.2 collective-permute-done.1.refs_1_
  13.5 0.5 %shard_map.77 = (bf16[128,256]{1,0:T(8,128)(2,1)S(1)}, bf16[128,256]{1,0:T(8,128)(2,1)S(1)}, bf16[128,256]{1,0:T(8,128)(2,1)S(1)}, bf16[128,256]{1,0:T(8,128)(2,1)S(1)}, bf16[256,128]{1,0:T(8,128)(2,1)S(1)}) custom-call(bf16[280,128]{1,0:T(8,128)(2,1)S(1)} %collective-permute-done.refs_0_, bf16[280,128]{1,0:T(8,128)(2,1)S(1)} %collective-permute-done.1.refs_1_, ...), custom_call_target="tpu_custom_call" | custom-call | tf_op jit(solution)/shard_map/pallas_call | solution.py:65
  14.1 0.3 shard_map.74
  14.4 0.5 %shard_map.75 = (bf16[128,256]{1,0:T(8,128)(2,1)S(1)}, bf16[128,256]{1,0:T(8,128)(2,1)S(1)}, bf16[128,256]{1,0:T(8,128)(2,1)S(1)}, bf16[128,256]{1,0:T(8,128)(2,1)S(1)}, f32[256,128]{1,0:T(8,128)S(1)}) custom-call(bf16[280,128]{1,0:T(8,128)(2,1)S(1)} %collective-permute-done.refs_0_, bf16[280,128]{1,0:T(8,128)(2,1)S(1)} %collective-permute-done.1.refs_1_, ...), custom_call_target="tpu_custom_call" | custom-call | tf_op jit(solution)/shard_map/pallas_call | solution.py:65
  14.9 0.4 %collective-permute-done.5.got_ref = bf16[256,128]{1,0:T(8,128)(2,1)S(1)} collective-permute-done((bf16[256,128]{1,0:T(8,128)(2,1)S(1)}, bf16[256,128]{1,0:T(8,128)(2,1)S(1)}, u32[]{:S(2)}, u32[]{:S(2)}) %collective-permute-start.5) | collective-permute-done | bytes 65568 | tf_op jit(solution)/shard_map/ppermute | solution.py:271
  15.3 1.6 %collective-permute-start.6 = (bf16[256,128]{1,0:T(8,128)(2,1)S(1)}, bf16[256,128]{1,0:T(8,128)(2,1)S(1)}, u32[]{:S(2)}, u32[]{:S(2)}) collective-permute-start(bf16[256,128]{1,0:T(8,128)(2,1)S(1)} %get-tuple-element.50), channel_id=1, source_target_pairs={{0,2},{1,3},{2,0},{3,1},{4,6},{5,7},{6,4},{7,5},{8,10},{9,11},{10,... | collective-permute-start | bytes 196616 | tf_op jit(solution)/shard_map/ppermute | solution.py:271
  16.9 0.5 %collective-permute-start.7 = (f32[64,128]{1,0:T(8,128)S(1)}, f32[64,128]{1,0:T(8,128)S(1)}, u32[]{:S(2)}, u32[]{:S(2)}) collective-permute-start(f32[64,128]{1,0:T(8,128)S(1)} %get-tuple-element.51.refs_2_), channel_id=1, source_target_pairs={{0,2},{1,3},{2,0},{3,1},{4,6},{5,7},{6,4},{7,5},{8,10},{9,11},{10,... | collective-permute-start | bytes 98312 | tf_op jit(solution)/shard_map/ppermute | solution.py:271
  17.4 3.4 %collective-permute-done.7.refs_3_ = f32[64,128]{1,0:T(8,128)S(1)} collective-permute-done((f32[64,128]{1,0:T(8,128)S(1)}, f32[64,128]{1,0:T(8,128)S(1)}, u32[]{:S(2)}, u32[]{:S(2)}) %collective-permute-start.7) | collective-permute-done | bytes 32800 | tf_op jit(solution)/shard_map/ppermute | solution.py:271
  20.8 0.1 shard_map.79
  21.0 0.2 shard_map.80
  21.2 1.0 %collective-permute-done.8.refs_2_.refs_0_ = bf16[128,256]{1,0:T(8,128)(2,1)S(1)} collective-permute-done((bf16[128,256]{1,0:T(8,128)(2,1)S(1)}, bf16[128,256]{1,0:T(8,128)(2,1)S(1)}, u32[]{:S(2)}, u32[]{:S(2)}) %collective-permute-start.8) | collective-permute-done | bytes 65568 | tf_op jit(solution)/shard_map/ppermute | solution.py:271
  22.2 0.2 shard_map.84
  22.4 2.0 %collective-permute-start.11 = (bf16[128,256]{1,0:T(8,128)(2,1)S(1)}, bf16[128,256]{1,0:T(8,128)(2,1)S(1)}, u32[]{:S(2)}, u32[]{:S(2)}) collective-permute-start(bf16[128,256]{1,0:T(8,128)(2,1)S(1)} %shard_map.84), channel_id=1, source_target_pairs={{0,8},{4,0},{8,12},{12,4},{1,9},{5,1},{9,13},{13,5},{2,10},{6,2},{... | collective-permute-start | bytes 196616 | tf_op jit(solution)/shard_map/ppermute | solution.py:274
  24.4 0.2 shard_map.83
  24.6 1.9 %collective-permute-start.10 = (bf16[128,256]{1,0:T(8,128)(2,1)S(1)}, bf16[128,256]{1,0:T(8,128)(2,1)S(1)}, u32[]{:S(2)}, u32[]{:S(2)}) collective-permute-start(bf16[128,256]{1,0:T(8,128)(2,1)S(1)} %shard_map.83), channel_id=1, source_target_pairs={{0,12},{4,8},{8,4},{12,0},{1,13},{5,9},{9,5},{13,1},{2,14},{6,10},... | collective-permute-start | bytes 196616 | tf_op jit(solution)/shard_map/ppermute | solution.py:274
  26.4 0.2 shard_map.82
  26.7 0.2 shard_map.81
  26.8 0.6 %copy.7 = f32[64,128]{1,0:T(8,128)} copy(f32[64,128]{1,0:T(8,128)S(1)} %get-tuple-element.77) | data formatting | bytes 65536
  27.5 3.5 %collective-permute-done.10.refs_2_ = bf16[128,256]{1,0:T(8,128)(2,1)S(1)} collective-permute-done((bf16[128,256]{1,0:T(8,128)(2,1)S(1)}, bf16[128,256]{1,0:T(8,128)(2,1)S(1)}, u32[]{:S(2)}, u32[]{:S(2)}) %collective-permute-start.10) | collective-permute-done | bytes 65568 | tf_op jit(solution)/shard_map/ppermute | solution.py:274
  31.0 1.2 %collective-permute-done.9.refs_1_ = bf16[128,256]{1,0:T(8,128)(2,1)S(1)} collective-permute-done((bf16[128,256]{1,0:T(8,128)(2,1)S(1)}, bf16[128,256]{1,0:T(8,128)(2,1)S(1)}, u32[]{:S(2)}, u32[]{:S(2)}) %collective-permute-start.9) | collective-permute-done | bytes 65568 | tf_op jit(solution)/shard_map/ppermute | solution.py:274
  32.2 0.7 %shard_map.85 = bf16[256,128]{1,0:T(8,128)(2,1)} custom-call(f32[128,256]{1,0:T(8,128)S(1)} %get-tuple-element.65.refs_0_, bf16[128,256]{1,0:T(8,128)(2,1)S(1)} %collective-permute-done.9.refs_1_, bf16[128,256]{1,0:T(8,128)(2,1)S(1)} %collective-permute-done.10.refs_2_, bf16[128,256]{1,0:T(8,128)(2,1)S(1)} %collective-permute-done.11.refs_3_), custom_call_target="tpu_custom_call" | custom-call | tf_op jit(solution)/shard_map/pallas_call | solution.py:65
  (13 shorter events, 0.3 us)
Async XLA Ops:
  1.5 11.1 %collective-permute-start.4 = (bf16[280,128]{1,0:T(8,128)(2,1)S(1)}, bf16[280,128]{1,0:T(8,128)(2,1)S(1)}, u32[]{:S(2)}, u32[]{:S(2)}) collective-permute-start(bf16[280,128]{1,0:T(8,128)(2,1)S(1)} %get-tuple-element.39.refs_0_), channel_id=1, source_target_pairs={{0,4},{4,8},{8,12},{12,0},{1,5},{5,9},{9,13},{13,1},{2,6},{6,10},{... | collective-permute-start | bytes 215048 | tf_op jit(solution)/shard_map/ppermute | solution.py:274
  4.6 8.6 %collective-permute-start = (bf16[280,128]{1,0:T(8,128)(2,1)S(1)}, bf16[280,128]{1,0:T(8,128)(2,1)S(1)}, u32[]{:S(2)}, u32[]{:S(2)}) collective-permute-start(bf16[280,128]{1,0:T(8,128)(2,1)S(1)} %get-tuple-element.39.refs_0_), channel_id=1, source_target_pairs={{0,12},{4,0},{8,4},{12,8},{1,13},{5,1},{9,5},{13,9},{2,14},{6,2},{... | collective-permute-start | bytes 215048 | tf_op jit(solution)/shard_map/ppermute | solution.py:274
  6.7 6.8 %collective-permute-start.1 = (bf16[280,128]{1,0:T(8,128)(2,1)S(1)}, bf16[280,128]{1,0:T(8,128)(2,1)S(1)}, u32[]{:S(2)}, u32[]{:S(2)}) collective-permute-start(bf16[280,128]{1,0:T(8,128)(2,1)S(1)} %get-tuple-element.39.refs_0_), channel_id=1, source_target_pairs={{0,8},{4,12},{8,0},{12,4},{1,9},{5,13},{9,1},{13,5},{2,10},{6,14},... | collective-permute-start | bytes 215048 | tf_op jit(solution)/shard_map/ppermute | solution.py:274
  7.7 1.2 %collective-permute-start.2 = (f32[8,128]{1,0:T(8,128)S(1)}, f32[8,128]{1,0:T(8,128)S(1)}, u32[]{:S(2)}, u32[]{:S(2)}) collective-permute-start(f32[8,128]{1,0:T(8,128)S(1)} %get-tuple-element.40.own_ref), channel_id=1, source_target_pairs={{0,1},{1,0},{2,3},{3,2},{4,5},{5,4},{6,7},{7,6},{8,9},{9,8},{10,11... | collective-permute-start | bytes 12296 | tf_op jit(solution)/shard_map/ppermute | solution.py:271
  8.9 3.7 %collective-permute-start.3 = (f32[16,128]{1,0:T(8,128)S(1)}, f32[16,128]{1,0:T(8,128)S(1)}, u32[]{:S(2)}, u32[]{:S(2)}) collective-permute-start(f32[16,128]{1,0:T(8,128)S(1)} %shard_map.69.refs_0_), channel_id=1, source_target_pairs={{0,2},{1,3},{2,0},{3,1},{4,6},{5,7},{6,4},{7,5},{8,10},{9,11},{10,... | collective-permute-start | bytes 24584 | tf_op jit(solution)/shard_map/ppermute | solution.py:271
  14.0 1.3 %collective-permute-start.5 = (bf16[256,128]{1,0:T(8,128)(2,1)S(1)}, bf16[256,128]{1,0:T(8,128)(2,1)S(1)}, u32[]{:S(2)}, u32[]{:S(2)}) collective-permute-start(bf16[256,128]{1,0:T(8,128)(2,1)S(1)} %get-tuple-element.48), channel_id=1, source_target_pairs={{0,1},{1,0},{2,3},{3,2},{4,5},{5,4},{6,7},{7,6},{8,9},{9,8},{10,11... | collective-permute-start | bytes 196616 | tf_op jit(solution)/shard_map/ppermute | solution.py:271
  15.3 5.5 %collective-permute-start.6 = (bf16[256,128]{1,0:T(8,128)(2,1)S(1)}, bf16[256,128]{1,0:T(8,128)(2,1)S(1)}, u32[]{:S(2)}, u32[]{:S(2)}) collective-permute-start(bf16[256,128]{1,0:T(8,128)(2,1)S(1)} %get-tuple-element.50), channel_id=1, source_target_pairs={{0,2},{1,3},{2,0},{3,1},{4,6},{5,7},{6,4},{7,5},{8,10},{9,11},{10,... | collective-permute-start | bytes 196616 | tf_op jit(solution)/shard_map/ppermute | solution.py:271
  16.9 3.9 %collective-permute-start.7 = (f32[64,128]{1,0:T(8,128)S(1)}, f32[64,128]{1,0:T(8,128)S(1)}, u32[]{:S(2)}, u32[]{:S(2)}) collective-permute-start(f32[64,128]{1,0:T(8,128)S(1)} %get-tuple-element.51.refs_2_), channel_id=1, source_target_pairs={{0,2},{1,3},{2,0},{3,1},{4,6},{5,7},{6,4},{7,5},{8,10},{9,11},{10,... | collective-permute-start | bytes 98312 | tf_op jit(solution)/shard_map/ppermute | solution.py:271
  20.9 1.3 %collective-permute-start.8 = (bf16[128,256]{1,0:T(8,128)(2,1)S(1)}, bf16[128,256]{1,0:T(8,128)(2,1)S(1)}, u32[]{:S(2)}, u32[]{:S(2)}) collective-permute-start(bf16[128,256]{1,0:T(8,128)(2,1)S(1)} %get-tuple-element.53.refs_0_), channel_id=1, source_target_pairs={{0,1},{1,0},{2,3},{3,2},{4,5},{5,4},{6,7},{7,6},{8,9},{9,8},{10,11... | collective-permute-start | bytes 196616 | tf_op jit(solution)/shard_map/ppermute | solution.py:271
  22.4 5.1 %collective-permute-start.11 = (bf16[128,256]{1,0:T(8,128)(2,1)S(1)}, bf16[128,256]{1,0:T(8,128)(2,1)S(1)}, u32[]{:S(2)}, u32[]{:S(2)}) collective-permute-start(bf16[128,256]{1,0:T(8,128)(2,1)S(1)} %shard_map.84), channel_id=1, source_target_pairs={{0,8},{4,0},{8,12},{12,4},{1,9},{5,1},{9,13},{13,5},{2,10},{6,2},{... | collective-permute-start | bytes 196616 | tf_op jit(solution)/shard_map/ppermute | solution.py:274
  24.5 2.1 %copy-start = (f32[2,64,128]{2,1,0:T(8,128)S(1)}, f32[2,64,128]{2,1,0:T(8,128)}, u32[]{:S(2)}) copy-start(f32[2,64,128]{2,1,0:T(8,128)} %refs_1_.1) | copy-start | bytes 196612
  24.6 6.4 %collective-permute-start.10 = (bf16[128,256]{1,0:T(8,128)(2,1)S(1)}, bf16[128,256]{1,0:T(8,128)(2,1)S(1)}, u32[]{:S(2)}, u32[]{:S(2)}) collective-permute-start(bf16[128,256]{1,0:T(8,128)(2,1)S(1)} %shard_map.83), channel_id=1, source_target_pairs={{0,12},{4,8},{8,4},{12,0},{1,13},{5,9},{9,5},{13,1},{2,14},{6,10},... | collective-permute-start | bytes 196616 | tf_op jit(solution)/shard_map/ppermute | solution.py:274
  26.6 5.6 %collective-permute-start.9 = (bf16[128,256]{1,0:T(8,128)(2,1)S(1)}, bf16[128,256]{1,0:T(8,128)(2,1)S(1)}, u32[]{:S(2)}, u32[]{:S(2)}) collective-permute-start(bf16[128,256]{1,0:T(8,128)(2,1)S(1)} %shard_map.82), channel_id=1, source_target_pairs={{0,4},{4,12},{8,0},{12,8},{1,5},{5,13},{9,1},{13,9},{2,6},{6,14},{... | collective-permute-start | bytes 196616 | tf_op jit(solution)/shard_map/ppermute | solution.py:274
